TPU v7x, 256 devices: a whole 4x4x8 slice. The times are simulated.
256 devices in a mesh: dp: 16 (over y, x_hi, core), space: 16 (over x_lo, z).
Axes of the slice: x: 4 (x_hi: 2, x_lo: 2; x = x_hi * 2 + x_lo), y: 4, z: 8, core: 2. Of those that a mesh axis runs over, the one named last changes fastest.
Arguments:
- act_in: bfloat16 [16, 32, 64, 2048], P('dp', 'space'), may hold values from -6 to 6
- weight_one: bfloat16 [3, 3, 3, 32, 64], replicated, may hold values from -0.21875 to 0.21875
- bias_one: float32 [64], replicated, may hold values from -3 to 3
- weight_two: bfloat16 [3, 3, 3, 64, 128], replicated, may hold values from -0.15625 to 0.15625
- bias_two: float32 [128], replicated, may hold values from -3 to 3
- cotangent: bfloat16 [16, 16, 32, 4096], P('dp', 'space'), may hold values from -24 to 24
Outputs:
- grad_input: bfloat16 [16, 32, 64, 2048], P('dp', 'space')
- grad_w_one: float32 [3, 3, 3, 32, 64], replicated
- grad_b_one: float32 [64], replicated
- grad_w_two: float32 [3, 3, 3, 64, 128], replicated
- grad_b_two: float32 [128], replicated
All inputs are finite; a program needn't handle non-finite values.
Results may differ from a plain program's by a relative error of at most 0.01.
Values may be sent and summed in bfloat16 or wider, within the bound.
No kernel may reach another device: no remote copies, remote signals or barrier semaphores. Data moves between devices by JAX's collectives and lax.ppermute only.
A program may use at most 128 MiB of HBM per device.

v0:
```python
import functools
import math

import jax
import jax.numpy as jnp
from jax import lax
from jax.experimental import pallas as pl
from jax.experimental.pallas import tpu as pltpu
from jax.sharding import PartitionSpec as P


F32 = jnp.float32
BF16 = jnp.bfloat16
LANES = 128
MIB = 1024 * 1024


def _params(mib):
    return pltpu.CompilerParams(vmem_limit_bytes=mib * MIB)


def _cost(flops, moved):
    return pl.CostEstimate(flops=int(flops), bytes_accessed=int(moved), transcendentals=0)


def _dot(a, b):
    return lax.dot_general(a, b, (((1,), (0,)), ((), ())), preferred_element_type=F32)


def _dot_t(a, b):
    return lax.dot_general(a, b, (((1,), (1,)), ((), ())), preferred_element_type=F32)


def _sigmoid(v):
    return 1.0 / (1.0 + jnp.exp(-v))


def _zero_edges(buf, rows):
    tiles = buf.shape[0]
    buf[:, 0:8, :] = jnp.zeros((tiles, 8, LANES), F32)
    buf[:, 8 + rows : 16 + rows, :] = jnp.zeros((tiles, 8, LANES), F32)


def _spread(load, tiles, rows, shift, buf, out):
    lane = lax.broadcasted_iota(jnp.int32, (rows, LANES), 1)
    before = jnp.zeros((rows, LANES), F32)
    for t in range(tiles + 1):
        now = pltpu.roll(load(t).astype(F32), shift, 1) if t < tiles else jnp.zeros((rows, LANES), F32)
        tile = jnp.where(lane < shift, before, now)
        buf[t, 8 : 8 + rows, :] = tile
        out[1, t] = tile.astype(BF16)
        before = now
    for t in range(tiles + 1):
        out[0, t] = buf[t, 7 : 7 + rows, :].astype(BF16)
        out[2, t] = buf[t, 9 : 9 + rows, :].astype(BF16)


def _cols(ref, first, groups):
    rows = ref.shape[1]
    a = ref[pl.ds(first, groups)].reshape(groups * rows, LANES)
    b = ref[pl.ds(first + 1, groups)].reshape(groups * rows, LANES)
    return jnp.concatenate([a, b], axis=1)


def _prep_kernel(w_one_ref, w_two_ref, back_one, band_two, back_two):
    for ref in (back_one, band_two, back_two):
        ref[...] = jnp.zeros(ref.shape, BF16)
    for kk in range(9):
        kd, kh = kk // 3, kk % 3
        for kw in range(3):
            tap = w_one_ref[3 * kk + kw]
            for j in range(8):
                c = 768 * kh + 64 * (j - kw + 3)
                back_one[kd, 32 * j : 32 * j + 32, c : c + 64] = tap
            tap = w_two_ref[3 * kk + kw]
            for j in range(2):
                r = 256 * kk + 64 * (j + kw)
                band_two[r : r + 64, LANES * j : LANES * (j + 1)] = tap
            for j in range(4):
                c = 768 * kh + LANES * (j - kw + 2)
                back_two[kd, 64 * j : 64 * j + 64, c : c + LANES] = tap


def _first_kernel(x0_ref, x1_ref, w_ref, pre_ref, xs_ref, band_ref, buf):
    rows, groups = x0_ref.shape[0], pre_ref.shape[1]
    band_ref[...] = jnp.zeros(band_ref.shape, BF16)
    for kk in range(9):
        for kw in range(3):
            tap = w_ref[3 * kk + kw]
            for j in range(4):
                r = 256 * kk + 32 * (j + kw)
                band_ref[r : r + 32, 64 * j : 64 * j + 64] = tap
    _zero_edges(buf, rows)
    for p, ref in enumerate((x0_ref, x1_ref)):
        _spread(lambda t, ref=ref: ref[:, LANES * t : LANES * (t + 1)], groups, rows, 32, buf, xs_ref.at[p])
    step = 8

    def chunk(c, carry):
        g = c * step
        sides = [[_cols(xs_ref.at[p, kh], g, step) for kh in range(3)] for p in range(2)]
        lhs = jnp.concatenate(sides[0] + sides[1], axis=1)
        pre_ref[0, pl.ds(g, step)] = _dot(lhs, band_ref[768:2304, :]).reshape(step, rows, 256)
        pre_ref[1, pl.ds(g, step)] = _dot(lhs, band_ref[0:1536, :]).reshape(step, rows, 256)
        return carry

    lax.fori_loop(0, groups // step, chunk, 0)


def _second_kernel(left_ref, right_ref, pre_ref, band_ref, bias_ref, slope_ref, pool_ref, xs_ref, buf, low, high):
    rows, groups = left_ref.shape[0], pre_ref.shape[1]
    half = rows // 2
    bias = jnp.concatenate([bias_ref[...]] * 4, axis=1)
    _zero_edges(buf, rows)
    for s, ref in enumerate((left_ref, right_ref)):
        _spread(lambda t, ref=ref: ref[:, LANES * t : LANES * (t + 1)], groups, rows, 32, buf, xs_ref.at[s])
    step = 4
    lane = lax.broadcasted_iota(jnp.int32, (step * half, LANES), 1)

    def chunk(c, carry):
        g = c * step
        total = None
        for p in range(2):
            lhs = jnp.concatenate([_cols(xs_ref.at[p, kh], g, step) for kh in range(3)], axis=1)
            more = _dot(lhs, band_ref[1536 * p : 1536 * p + 768, :])
            pre = pre_ref[p, pl.ds(g, step)].reshape(step * rows, 256) + more + bias
            sig = _sigmoid(pre)
            slope_ref[p, pl.ds(g, step)] = (sig * (1.0 + pre * (1.0 - sig))).reshape(step, rows, 256)
            act = pre * sig
            total = act if total is None else total + act
        for part, lanes in ((low, 0), (high, LANES)):
            v = total[:, lanes : lanes + LANES]
            part[...] = v + pltpu.roll(v, 64, 1)
        a = low[pl.ds(0, step * half, stride=2), :] + low[pl.ds(1, step * half, stride=2), :]
        b = high[pl.ds(0, step * half, stride=2), :] + high[pl.ds(1, step * half, stride=2), :]
        mean = jnp.where(lane < 64, a, b) * 0.125
        pool_ref[pl.ds(g, step)] = mean.astype(BF16).reshape(step, half, LANES)
        return carry

    lax.fori_loop(0, groups // step, chunk, 0)


def _mid_kernel(own_ref, band_ref, bias_ref, ps_ref, pre_ref, buf):
    groups, rows = own_ref.shape[0], own_ref.shape[1]
    _zero_edges(buf, rows)
    _spread(lambda t: own_ref[t], groups, rows, 64, buf, ps_ref)
    lhs = jnp.concatenate([_cols(ps_ref.at[kh], 0, groups) for kh in range(3)], axis=1)
    bias = jnp.concatenate([bias_ref[...]] * 2, axis=1)
    pre_ref[...] = _dot(lhs, band_ref[768:1536, :]) + bias


def _third_kernel(
    left_ref, right_ref, pre_ref, band_ref, back_ref, cot_ref, delta_ref, ps_ref, ds_ref, gl_ref, gr_ref, buf
):
    groups, rows = left_ref.shape[0], left_ref.shape[1]
    _zero_edges(buf, rows)
    for s, ref in enumerate((left_ref, right_ref)):
        _spread(lambda t, ref=ref: ref[t], groups, rows, 64, buf, ps_ref.at[s])
    near = jnp.concatenate([_cols(ps_ref.at[0, kh], 0, groups) for kh in range(3)], axis=1)
    far = jnp.concatenate([_cols(ps_ref.at[1, kh], 0, groups) for kh in range(3)], axis=1)
    pre = pre_ref[...] + _dot(near, band_ref[0:768, :]) + _dot(far, band_ref[1536:2304, :])
    sig = _sigmoid(pre)
    cot = jnp.concatenate([cot_ref[:, 256 * g : 256 * (g + 1)] for g in range(groups)], axis=0)
    delta = (cot.astype(F32) * (sig * (1.0 + pre * (1.0 - sig)))).astype(BF16)
    delta_ref[...] = delta
    again = delta.astype(F32)
    cells = 2 * groups
    zero = jnp.zeros((rows, LANES), BF16)
    for kh in range(3):
        ds_ref[kh, 0] = zero
        ds_ref[kh, cells + 1] = zero
    for t in range(cells):
        g, j = t // 2, t % 2
        tile = again[g * rows : (g + 1) * rows, LANES * j : LANES * (j + 1)]
        spot = buf.at[t % buf.shape[0]]
        spot[8 : 8 + rows, :] = tile
        ds_ref[0, t + 1] = spot[9 : 9 + rows, :].astype(BF16)
        ds_ref[1, t + 1] = tile.astype(BF16)
        ds_ref[2, t + 1] = spot[7 : 7 + rows, :].astype(BF16)
    wide = cells // 4
    lhs = _window(ds_ref, 0, wide)
    for kd, ref in ((0, gl_ref), (2, gr_ref)):
        _put_cells(ref, _dot_t(lhs, back_ref[kd]), wide, rows)


def _put_cells(ref, out, wide, rows):
    for g in range(wide):
        for j in range(2):
            ref[2 * g + j] = out[g * rows : (g + 1) * rows, LANES * j : LANES * (j + 1)].astype(ref.dtype)


def _own_two_kernel(delta_ref, own_ref, halo_ref, ds_ref, back_ref, gm_ref, out_ref):
    groups, rows = own_ref.shape[1] - 1, own_ref.shape[2]
    out_ref[1728:, :] = jnp.zeros((out_ref.shape[0] - 1728, LANES), BF16)
    _put_cells(gm_ref, _dot_t(_window(ds_ref, 0, groups // 2), back_ref[1]), groups // 2, rows)
    delta = delta_ref[...]
    flip = delta.astype(F32).T.astype(BF16)
    planes = (halo_ref.at[0], own_ref, halo_ref.at[1])
    for kk in range(9):
        full = _dot(flip, _cols(planes[kk // 3].at[kk % 3], 0, groups))
        band = full[0:LANES, :] + pltpu.roll(full[LANES:256, :], 192, 1)
        out_ref[192 * kk : 192 * (kk + 1), :] = band.T[0:192, :].astype(BF16)
    total = jnp.sum(delta.astype(F32), axis=0, keepdims=True)
    line = total[:, 0:LANES] + total[:, LANES:256]
    out_ref[1728:1744, :] = jnp.broadcast_to(line, (16, LANES)).astype(BF16)


def _grad_one_kernel(
    gm_ref, fl_ref, fr_ref, slope_ref, own_ref, halo_ref, two_ref, delta_ref, out_ref, sums, up0, up1, flip, one
):
    groups, rows = slope_ref.shape[1], slope_ref.shape[2]
    half = rows // 2
    lane = lax.broadcasted_iota(jnp.int32, (half, LANES), 1)
    sums[...] = jnp.zeros(sums.shape, F32)
    for g in range(groups):
        v = (gm_ref[g] + fl_ref[g].astype(F32) + fr_ref[g].astype(F32)) * 0.125
        turned = pltpu.roll(v, 64, 1)
        a = jnp.where(lane < 64, v, turned)
        b = jnp.where(lane < 64, turned, v)
        for j, (ref, val) in enumerate(((up0, a), (up1, b))):
            spot = ref.at[g % 2]
            spot[pl.ds(0, half, stride=2), :] = val
            spot[pl.ds(1, half, stride=2), :] = val
            lanes = slice(LANES * j, LANES * (j + 1))
            both = []
            for p in range(2):
                low = (spot[...] * slope_ref[p, g, :, lanes]).astype(BF16)
                delta_ref[p, g, :, lanes] = low
                both.append(low.astype(F32))
            sums[:, lanes] += jnp.sum(both[0].reshape(rows // 8, 8, LANES) + both[1].reshape(rows // 8, 8, LANES), axis=0)
            turn = jnp.concatenate(both, axis=0).T.astype(BF16)
            flip[lanes, 2 * rows * g : 2 * rows * (g + 1)] = turn
    one[...] = jnp.zeros(one.shape, BF16)
    planes = (halo_ref.at[0], own_ref.at[0], own_ref.at[1], halo_ref.at[1])
    for kd in range(3):
        for kh in range(3):
            kk = 3 * kd + kh
            a = planes[kd].at[kh]
            b = planes[kd + 1].at[kh]
            left = jnp.concatenate([r[g] for g in range(groups) for r in (a, b)], axis=0)
            right = jnp.concatenate([r[g + 1] for g in range(groups) for r in (a, b)], axis=0)
            full = _dot(flip[...], jnp.concatenate([left, right], axis=1))
            band = full[0:64, 0:LANES]
            for j in range(1, 4):
                band = band + pltpu.roll(full[64 * j : 64 * j + 64, :], 256 - 32 * j, 1)[:, 0:LANES]
            tall = band.T[0:96, :].astype(BF16)
            for r in range(0, 96, 48):
                at = 96 * kk + r
                side = at // 432
                one[at - 432 * side : at - 432 * side + 48, 64 * side : 64 * side + 64] = tall[r : r + 48, :]
    total = jnp.sum(sums[...], axis=0, keepdims=True)
    line = total[:, 0:LANES] + total[:, LANES:256]
    line = line + pltpu.roll(line, 64, 1)
    one[432:448, :] = jnp.broadcast_to(line, (16, LANES)).astype(BF16)
    count = out_ref.shape[0]
    rows_two, rows_one = two_ref.shape[0] // count, one.shape[0] // count
    for i in range(count):
        out_ref[i, 0:rows_two, :] = two_ref[i * rows_two : (i + 1) * rows_two, :]
        out_ref[i, rows_two:, :] = one[i * rows_one : (i + 1) * rows_one, :]


def _sides_kernel(delta_ref, back_ref, ds_ref, gl_ref, gr_ref, buf):
    groups, rows = delta_ref.shape[1], delta_ref.shape[2]
    cells = 2 * groups
    _zero_edges(buf, rows)
    zero = jnp.zeros((rows, LANES), BF16)
    for p in range(2):
        for kh in range(3):
            ds_ref[p, kh, 0] = zero
            ds_ref[p, kh, cells + 1] = zero

    def group(g, carry):
        for p in range(2):
            for j in range(2):
                low = delta_ref[p, g, :, LANES * j : LANES * (j + 1)]
                spot = buf.at[2 * p + j]
                spot[8 : 8 + rows, :] = low.astype(F32)
                t = 2 * g + j + 1
                ds_ref[p, 0, t] = spot[9 : 9 + rows, :].astype(BF16)
                ds_ref[p, 1, t] = low
                ds_ref[p, 2, t] = spot[7 : 7 + rows, :].astype(BF16)
        return carry

    lax.fori_loop(0, groups, group, 0)
    step = cells // 8

    def chunk(c, carry):
        for p, kd, ref in ((0, 0, gl_ref), (1, 2, gr_ref)):
            out = _dot_t(_window(ds_ref.at[p], c * step, step), back_ref[kd])
            ref[pl.ds(c * step, step)] = out.astype(BF16).reshape(step, rows, 256)
        return carry

    lax.fori_loop(0, 2, chunk, 0)


def _window(ref, first, count):
    parts = []
    for kh in range(3):
        for i in range(6):
            parts.append(jnp.concatenate([ref[kh, 4 * (first + g) + i] for g in range(count)], axis=0))
    return jnp.concatenate(parts, axis=1)


def _grad_input_kernel(ds_ref, back_ref, fl_ref, fr_ref, out_ref):
    wide, rows = fl_ref.shape[0], fl_ref.shape[1]
    for g in range(0, wide, 2):
        near = _window(ds_ref.at[0], g, 2)
        far = _window(ds_ref.at[1], g, 2)
        first = _dot_t(near, back_ref[1]) + _dot_t(far, back_ref[0])
        second = _dot_t(near, back_ref[2]) + _dot_t(far, back_ref[1])
        for s in range(2):
            for p, val, ref in ((0, first, fl_ref), (1, second, fr_ref)):
                whole = val[s * rows : (s + 1) * rows] + ref[g + s].astype(F32)
                out_ref[p, :, 256 * (g + s) : 256 * (g + s + 1)] = whole.astype(BF16)


def _split_kernel(scale_two, scale_one, rows_two, in_ref, out_ref, buf):
    count, rows = out_ref.shape[0], in_ref.shape[1]
    whole = jnp.sum(in_ref[...].astype(F32), axis=0)
    buf[0:rows_two, :] = whole[0:rows_two] * scale_two
    buf[rows_two:rows, :] = whole[rows_two:] * scale_one
    buf[rows:, :] = jnp.zeros((buf.shape[0] - rows, LANES), F32)
    part, tall = rows // count, out_ref.shape[1]
    for i in range(count):
        out_ref[i] = buf[i * part : i * part + tall, :].astype(BF16)


def _sum_kernel(in_ref, out_ref):
    whole = jnp.sum(in_ref[...].astype(F32), axis=0).astype(BF16)
    for i in range(out_ref.shape[0]):
        out_ref[i] = whole


def _join_kernel(in_ref, out_ref, buf):
    count, tall = in_ref.shape[0], in_ref.shape[1]
    rows = out_ref.shape[1]
    part = rows // count
    for i in range(count):
        buf[i * part : i * part + tall, :] = in_ref[i].astype(F32)
    whole = buf[0:rows, :].astype(BF16)
    for i in range(out_ref.shape[0]):
        out_ref[i] = whole


def _unpack_kernel(rows_two, rows_one, in_ref, w_two_ref, b_two_ref, w_one_ref, b_one_ref):
    two, one = w_two_ref.shape[0], w_one_ref.shape[0] // 2
    for i in range(in_ref.shape[0]):
        at = i * rows_two
        take = min(rows_two, max(two - at, 0))
        if take:
            w_two_ref[at : at + take, :] = in_ref[i, 0:take, :].astype(F32)
        if at <= two < at + rows_two:
            b_two_ref[...] = in_ref[i, two - at : two - at + 16, :].astype(F32)[0:1]
        at = i * rows_one
        take = min(rows_one, max(one - at, 0))
        if take:
            block = in_ref[i, rows_two : rows_two + take, :].astype(F32)
            w_one_ref[at : at + take, :] = block[:, 0:64]
            w_one_ref[one + at : one + at + take, :] = block[:, 64:128]
        if at <= one < at + rows_one:
            spot = rows_two + one - at
            b_one_ref[...] = in_ref[i, spot : spot + 16, :].astype(F32)[0:1, 0:64]


def _shape(shape, dtype):
    return jax.ShapeDtypeStruct(shape, dtype)


def _call(kernel, out, scratch, flops, moved, mib, args):
    return pl.pallas_call(
        kernel, out_shape=out, scratch_shapes=scratch, compiler_params=_params(mib), cost_estimate=_cost(flops, moved)
    )(*args)


def _round_up(value, unit):
    return -(-value // unit) * unit


def local(act_in, weight_one, bias_one, weight_two, bias_two, cotangent):
    _, slab, side, merged = act_in.shape
    half = side // 2
    c0, c1 = weight_one.shape[3:]
    c2 = weight_two.shape[4]
    dp, space = lax.axis_size("dp"), lax.axis_size("space")
    depth_all = slab * space
    scale_one = 16.0 / math.sqrt(dp * depth_all * side * side)
    scale_two = 1.0 / math.sqrt(dp * (depth_all // 2) * half * half)
    up = [(i, i + 1) for i in range(space - 1)]
    down = [(i + 1, i) for i in range(space - 1)]

    x = act_in.reshape(slab, side, merged)
    x0, x1 = x[0], x[slab - 1]
    from_left = lax.ppermute(x1, "space", up)
    from_right = lax.ppermute(x0, "space", down)
    w_one = weight_one.reshape(27, c0, c1)
    w_two = weight_two.reshape(27, c1, c2)
    groups = merged // LANES
    xs_shape = (2, 3, groups + 1, side, LANES)
    work = 2 * side * groups * 256
    rows_mid = groups * half
    work_two = rows_mid * 256 * 768
    tile = _shape((groups, half, LANES), BF16)
    tall = pltpu.VMEM((groups + 1, side + 16, LANES), F32)
    short = pltpu.VMEM((groups + 1, half + 16, LANES), F32)
    pre, xs_own, band_one = _call(
        _first_kernel,
        (_shape((2, groups, side, 256), F32), _shape(xs_shape, BF16), _shape((2304, 256), BF16)),
        [tall],
        2 * work * 1536,
        8 * MIB,
        16,
        (x0, x1, w_one),
    )
    back_one, band_two, back_two = _call(
        _prep_kernel,
        (_shape((3, 256, 2304), BF16), _shape((2304, 256), BF16), _shape((3, 256, 2304), BF16)),
        [],
        work * 768,
        8 * MIB,
        16,
        (w_one, w_two),
    )
    slope, pooled, xs_halo = _call(
        _second_kernel,
        (_shape((2, groups, side, 256), F32), tile, _shape(xs_shape, BF16)),
        [tall] + [pltpu.VMEM((4 * side, LANES), F32)] * 2,
        2 * work * 768,
        8 * MIB,
        16,
        (from_left, from_right, pre, band_one, bias_one.reshape(1, c1)),
    )
    pool_left = lax.ppermute(pooled, "space", up)
    pool_right = lax.ppermute(pooled, "space", down)
    ps_own, pre_two = _call(
        _mid_kernel,
        (_shape((3, groups + 1, half, LANES), BF16), _shape((rows_mid, 256), F32)),
        [short],
        2 * work_two,
        2 * MIB,
        12,
        (pooled, band_two, bias_two.reshape(1, c2)),
    )
    delta_two, ps_halo, ds_two, gp_left, gp_right = _call(
        _third_kernel,
        (
            _shape((rows_mid, 256), BF16),
            _shape((2, 3, groups + 1, half, LANES), BF16),
            _shape((3, 2 * groups + 2, half, LANES), BF16),
            tile,
            tile,
        ),
        [short],
        8 * work_two,
        4 * MIB,
        16,
        (pool_left, pool_right, pre_two, band_two, back_two, cotangent.reshape(half, -1)),
    )
    gp_from_right = lax.ppermute(gp_left, "space", down)
    gp_from_left = lax.ppermute(gp_right, "space", up)
    rows_two = _round_up(1744, 16 * dp)
    rows_one = _round_up(448, 16 * dp)
    gp_own, part_two = _call(
        _own_two_kernel,
        (_shape((groups, half, LANES), F32), _shape((rows_two, LANES), BF16)),
        [],
        8 * work_two,
        2 * MIB,
        16,
        (delta_two, ps_own, ps_halo, ds_two, back_two),
    )
    rows_all = (rows_two + rows_one) // dp
    delta_one, parts = _call(
        _grad_one_kernel,
        (_shape((2, groups, side, 256), BF16), _shape((dp, rows_all, LANES), BF16)),
        [pltpu.VMEM((8, 256), F32)]
        + [pltpu.VMEM((2, side, LANES), F32)] * 2
        + [pltpu.VMEM((256, 2 * groups * side), BF16), pltpu.VMEM((rows_one, LANES), BF16)],
        2 * work * 2304,
        4 * MIB,
        16,
        (gp_own, gp_from_left, gp_from_right, slope, xs_own, xs_halo, part_two),
    )
    rows_two //= dp
    rows_one //= dp
    met = lax.all_to_all(parts, "dp", 0, 0)
    ds, gx_left, gx_right = _call(
        _sides_kernel,
        (
            _shape((2, 3, 2 * groups + 2, side, LANES), BF16),
            _shape((groups // 2, side, 256), BF16),
            _shape((groups // 2, side, 256), BF16),
        ),
        [pltpu.VMEM((4, side + 16, LANES), F32)],
        2 * work * 2304 // 2,
        8 * MIB,
        16,
        (delta_one, back_one),
    )
    gx_from_right = lax.ppermute(gx_left, "space", down)
    gx_from_left = lax.ppermute(gx_right, "space", up)
    grad_x = _call(
        _grad_input_kernel,
        _shape((2, side, merged), BF16),
        [],
        2 * work * 2304,
        8 * MIB,
        16,
        (ds, back_one, gx_from_left, gx_from_right),
    )
    small = _shape((space, _round_up(rows_all // space, 16), LANES), BF16)
    pieces = _call(
        functools.partial(_split_kernel, scale_two, scale_one, rows_two),
        small,
        [pltpu.VMEM((rows_all + 16, LANES), F32)],
        0,
        MIB,
        8,
        (met,),
    )
    met = lax.all_to_all(pieces, "space", 0, 0)
    total = _call(_sum_kernel, small, [], 0, MIB, 8, (met,))
    met = lax.all_to_all(total, "space", 0, 0)
    joined = _call(
        _join_kernel, _shape((dp, rows_all, LANES), BF16), [pltpu.VMEM((rows_all + 16, LANES), F32)], 0, MIB, 8, (met,)
    )
    done = lax.all_to_all(joined, "dp", 0, 0)
    gw_two, gb_two, gw_one, gb_one = _call(
        functools.partial(_unpack_kernel, rows_two, rows_one),
        (
            _shape((27 * c1, c2), F32),
            _shape((1, c2), F32),
            _shape((27 * c0, c1), F32),
            _shape((1, c1), F32),
        ),
        [],
        0,
        MIB,
        8,
        (done,),
    )
    return (
        grad_x.reshape(act_in.shape),
        gw_one.reshape(weight_one.shape),
        gb_one.reshape(bias_one.shape),
        gw_two.reshape(weight_two.shape),
        gb_two.reshape(bias_two.shape),
    )


def solution(mesh):
    placed = (P("dp", "space", None, None), P(), P(), P(), P(), P("dp", "space", None, None))
    return jax.shard_map(
        local,
        mesh=mesh,
        in_specs=placed,
        out_specs=(P("dp", "space", None, None), P(), P(), P(), P()),
        check_vma=False,
    )
```

profile of v0, /device:TPU:1, one launch (start us, length us, event | category | flops | bytes accessed | tf_op | source)
XLA Modules:
  0.0 127.5 jit_solution(13692410580358588022)
XLA Ops:
  0.6 1.1 slice_bitcast_fusion
  1.7 1.3 %collective-permute-start.1 = (bf16[64,2048]{1,0:T(8,128)(2,1)S(1)}, bf16[64,2048]{1,0:T(8,128)(2,1)S(1)}, u32[]{:S(2)}, u32[]{:S(2)}) collective-permute-start(bf16[64,2048]{1,0:T(8,128)(2,1)S(1)} %get-tuple-element.59.x0_ref), channel_id=1, source_target_pairs={{1,0},{2,1},{3,2},{4,3},{5,4},{6,5},{7,6},{8,7},{9,8},{10,9},{11,1... | collective-permute-start | bytes 786440 | tf_op jit(solution)/shard_map/ppermute | solution.py:393
  3.0 5.0 %collective-permute-start = (bf16[64,2048]{1,0:T(8,128)(2,1)S(1)}, bf16[64,2048]{1,0:T(8,128)(2,1)S(1)}, u32[]{:S(2)}, u32[]{:S(2)}) collective-permute-start(bf16[64,2048]{1,0:T(8,128)(2,1)S(1)} %get-tuple-element.60.x1_ref), channel_id=1, source_target_pairs={{0,1},{1,2},{2,3},{3,4},{4,5},{5,6},{6,7},{7,8},{8,9},{9,10},{10,1... | collective-permute-start | bytes 786440 | tf_op jit(solution)/shard_map/ppermute | solution.py:392
  8.0 0.0 copy-start.7
  8.0 0.9 copy-done.7
  9.0 2.4 %shard_map.101 = (f32[2,16,64,256]{3,2,1,0:T(8,128)S(1)}, bf16[2,3,17,64,128]{4,3,2,1,0:T(8,128)(2,1)S(1)}, bf16[2304,256]{1,0:T(8,128)(2,1)S(1)}) custom-call(bf16[64,2048]{1,0:T(8,128)(2,1)S(1)} %get-tuple-element.59.x0_ref, bf16[64,2048]{1,0:T(8,128)(2,1)S(1)} %get-tuple-element.60.x1_ref, bf16[27,32,64]{2,1,0:T(8,128)(2,1)S(1)} %bitcast.18), custom_call_target="tpu_custom_call" | custom-call | flops 1610612736 | bytes 8388608 | tf_op jit(solution)/shard_map/pallas_call | solution.py:369
  11.4 0.0 copy-start.6
  11.4 0.0 copy-start.8
  11.4 0.0 collective-permute-done.1.right_ref
  11.4 0.0 collective-permute-done.left_ref
  11.4 0.0 copy-done.4
  11.4 0.0 copy-start.5
  11.5 2.8 %shard_map.102 = (f32[2,16,64,256]{3,2,1,0:T(8,128)S(1)}, bf16[16,32,128]{2,1,0:T(8,128)(2,1)S(1)}, bf16[2,3,17,64,128]{4,3,2,1,0:T(8,128)(2,1)S(1)}) custom-call(bf16[64,2048]{1,0:T(8,128)(2,1)S(1)} %collective-permute-done.left_ref, bf16[64,2048]{1,0:T(8,128)(2,1)S(1)} %collective-permute-done.1.right_ref, ...), custom_call_target="tpu_custom_call" | custom-call | flops 805306368 | bytes 8388608 | tf_op jit(solution)/shard_map/pallas_call | solution.py:369
  14.3 0.0 copy-start.3
  14.3 1.4 %collective-permute-start.3 = (bf16[16,32,128]{2,1,0:T(8,128)(2,1)S(1)}, bf16[16,32,128]{2,1,0:T(8,128)(2,1)S(1)}, u32[]{:S(2)}, u32[]{:S(2)}) collective-permute-start(bf16[16,32,128]{2,1,0:T(8,128)(2,1)S(1)} %get-tuple-element.34.own_ref), channel_id=1, source_target_pairs={{1,0},{2,1},{3,2},{4,3},{5,4},{6,5},{7,6},{8,7},{9,8},{10,9},{11,1... | collective-permute-start | bytes 393224 | tf_op jit(solution)/shard_map/ppermute | solution.py:432
  15.7 5.6 %collective-permute-start.2 = (bf16[16,32,128]{2,1,0:T(8,128)(2,1)S(1)}, bf16[16,32,128]{2,1,0:T(8,128)(2,1)S(1)}, u32[]{:S(2)}, u32[]{:S(2)}) collective-permute-start(bf16[16,32,128]{2,1,0:T(8,128)(2,1)S(1)} %get-tuple-element.34.own_ref), channel_id=1, source_target_pairs={{0,1},{1,2},{2,3},{3,4},{4,5},{5,6},{6,7},{7,8},{8,9},{9,10},{10,1... | collective-permute-start | bytes 393224 | tf_op jit(solution)/shard_map/ppermute | solution.py:431
  21.3 0.0 copy-done.6
  21.3 0.0 copy-done.8
  21.3 1.1 shard_map.103
  22.5 0.4 shard_map.104
  22.9 0.0 collective-permute-done.3.right_ref
  22.9 0.3 collective-permute-done.2.left_ref
  23.2 0.0 copy-done.3
  23.2 2.3 %shard_map.105 = (bf16[512,256]{1,0:T(8,128)(2,1)S(1)}, bf16[2,3,17,32,128]{4,3,2,1,0:T(8,128)(2,1)S(1)}, bf16[3,34,32,128]{3,2,1,0:T(8,128)(2,1)S(1)}, bf16[16,...) custom-call(bf16[16,32,128]{2,1,0:T(8,128)(2,1)S(1)} %collective-permute-done.2.left_ref, ...), custom_call_target="tpu_custom_call" | custom-call | flops 805306368 | bytes 4194304 | tf_op jit(solution)/shard_map/pallas_call | solution.py:369
  25.5 4.1 %collective-permute-start.4 = (bf16[16,32,128]{2,1,0:T(8,128)(2,1)S(1)}, bf16[16,32,128]{2,1,0:T(8,128)(2,1)S(1)}, u32[]{:S(2)}, u32[]{:S(2)}) collective-permute-start(bf16[16,32,128]{2,1,0:T(8,128)(2,1)S(1)} %get-tuple-element.43), channel_id=1, source_target_pairs={{0,1},{1,2},{2,3},{3,4},{4,5},{5,6},{6,7},{7,8},{8,9},{9,10},{10,1... | collective-permute-start | bytes 393224 | tf_op jit(solution)/shard_map/ppermute | solution.py:458
  29.6 1.3 %collective-permute-start.5 = (bf16[16,32,128]{2,1,0:T(8,128)(2,1)S(1)}, bf16[16,32,128]{2,1,0:T(8,128)(2,1)S(1)}, u32[]{:S(2)}, u32[]{:S(2)}) collective-permute-start(bf16[16,32,128]{2,1,0:T(8,128)(2,1)S(1)} %get-tuple-element.44), channel_id=1, source_target_pairs={{1,0},{2,1},{3,2},{4,3},{5,4},{6,5},{7,6},{8,7},{9,8},{10,9},{11,1... | collective-permute-start | bytes 393224 | tf_op jit(solution)/shard_map/ppermute | solution.py:457
  30.9 1.4 %shard_map.106 = (f32[16,32,128]{2,1,0:T(8,128)S(1)}, bf16[1792,128]{1,0:T(8,128)(2,1)S(1)}) custom-call(bf16[512,256]{1,0:T(8,128)(2,1)S(1)} %get-tuple-element.38.delta_ref, bf16[3,17,32,128]{3,2,1,0:T(8,128)(2,1)S(1)} %get-tuple-element.39.own_ref, bf16[2,3,17,32,128]{4,3,2,1,0:T(8,128)(2,1)S(1)} %get-tuple-element.40.halo_ref, ...), custom_call_target="tpu_custom_call" | custom-call | flops 805306368 | bytes 2097152 | tf_op jit(solution)/shard_map/pallas_call | solution.py:369
  32.4 0.0 collective-permute-done.4.fl_ref
  32.4 3.8 %collective-permute-done.5.fr_ref = bf16[16,32,128]{2,1,0:T(8,128)(2,1)S(1)} collective-permute-done((bf16[16,32,128]{2,1,0:T(8,128)(2,1)S(1)}, bf16[16,32,128]{2,1,0:T(8,128)(2,1)S(1)}, u32[]{:S(2)}, u32[]{:S(2)}) %collective-permute-start.5) | collective-permute-done | bytes 131104 | tf_op jit(solution)/shard_map/ppermute | solution.py:457
  36.2 3.5 %shard_map.107 = (bf16[2,16,64,256]{3,2,1,0:T(8,128)(2,1)S(1)}, bf16[16,144,128]{2,1,0:T(8,128)(2,1)S(1)}) custom-call(f32[16,32,128]{2,1,0:T(8,128)S(1)} %get-tuple-element.42.gm_ref, bf16[16,32,128]{2,1,0:T(8,128)(2,1)S(1)} %collective-permute-done.4.fl_ref, bf16[16,32,128]{2,1,0:T(8,128)(2,1)S(1)} %collective-permute-done.5.fr_ref, ...), custom_call_target="tpu_custom_call" | custom-call | flops 2415919104 | bytes 4194304 | tf_op jit(solution)/shard_map/pallas_call | solution.py:369
  39.7 23.1 %all_to_all.20.in_ref = bf16[16,144,128]{2,1,0:T(8,128)(2,1)S(1)} all-to-all(bf16[16,144,128]{2,1,0:T(8,128)(2,1)S(1)} %get-tuple-element.54), channel_id=1, replica_groups=mesh['dp'=16,'space'=16] {'dp'}, dimensions={0} | all-to-all | bytes 1179648 | tf_op jit(solution)/shard_map/all_to_all | solution.py:484
  62.8 0.1 shard_map.110
  62.9 22.4 %all_to_all.21.in_ref = bf16[16,16,128]{2,1,0:T(8,128)(2,1)S(1)} all-to-all(bf16[16,16,128]{2,1,0:T(8,128)(2,1)S(1)} %shard_map.110), channel_id=1, replica_groups=mesh['dp'=16,'space'=16] {'space'}, dimensions={0} | all-to-all | bytes 131072 | tf_op jit(solution)/shard_map/all_to_all | solution.py:519
  85.3 0.0 copy-done.1
  85.3 10.0 %all_to_all.22.in_ref = bf16[16,16,128]{2,1,0:T(8,128)(2,1)S(1)} all-to-all(bf16[16,16,128]{2,1,0:T(8,128)(2,1)S(1)} %shard_map.111), channel_id=1, replica_groups=mesh['dp'=16,'space'=16] {'space'}, dimensions={0} | all-to-all | bytes 131072 | tf_op jit(solution)/shard_map/all_to_all | solution.py:521
  95.3 0.1 shard_map.112
  95.3 0.0 copy-start
  95.3 0.8 copy-done
  96.1 7.0 %all-to-all-start.3 = ((bf16[16,144,128]{2,1,0:T(8,128)(2,1)}), bf16[16,144,128]{2,1,0:T(8,128)(2,1)}, u32[]{:S(2)}, u32[]{:S(2)}) async-start(bf16[16,144,128]{2,1,0:T(8,128)(2,1)} %copy-done), calls=%async_computation.3 | async-start | bytes 1179648 | tf_op jit(solution)/shard_map/all_to_all | solution.py:525
  103.1 1.2 copy-done.2
  104.4 2.2 %shard_map.108 = (bf16[2,3,34,64,128]{4,3,2,1,0:T(8,128)(2,1)S(1)}, bf16[8,64,256]{2,1,0:T(8,128)(2,1)S(1)}, bf16[8,64,256]{2,1,0:T(8,128)(2,1)S(1)}) custom-call(bf16[2,16,64,256]{3,2,1,0:T(8,128)(2,1)S(1)} %copy-done.2, bf16[3,256,2304]{2,1,0:T(8,128)(2,1)S(1)} %get-tuple-element.50.back_ref), custom_call_target="tpu_custom_call" | custom-call | flops 1207959552 | bytes 8388608 | tf_op jit(solution)/shard_map/pallas_call | solution.py:369
  106.5 2.6 %collective-permute-start.6 = (bf16[8,64,256]{2,1,0:T(8,128)(2,1)S(1)}, bf16[8,64,256]{2,1,0:T(8,128)(2,1)S(1)}, u32[]{:S(2)}, u32[]{:S(2)}) collective-permute-start(bf16[8,64,256]{2,1,0:T(8,128)(2,1)S(1)} %get-tuple-element.52), channel_id=1, source_target_pairs={{0,1},{1,2},{2,3},{3,4},{4,5},{5,6},{6,7},{7,8},{8,9},{9,10},{10,1... | collective-permute-start | bytes 786440 | tf_op jit(solution)/shard_map/ppermute | solution.py:499
  109.2 1.5 %collective-permute-start.7 = (bf16[8,64,256]{2,1,0:T(8,128)(2,1)S(1)}, bf16[8,64,256]{2,1,0:T(8,128)(2,1)S(1)}, u32[]{:S(2)}, u32[]{:S(2)}) collective-permute-start(bf16[8,64,256]{2,1,0:T(8,128)(2,1)S(1)} %get-tuple-element.53), channel_id=1, source_target_pairs={{1,0},{2,1},{3,2},{4,3},{5,4},{6,5},{7,6},{8,7},{9,8},{10,9},{11,1... | collective-permute-start | bytes 786440 | tf_op jit(solution)/shard_map/ppermute | solution.py:498
  110.7 3.9 %collective-permute-done.6.fl_ref = bf16[8,64,256]{2,1,0:T(8,128)(2,1)S(1)} collective-permute-done((bf16[8,64,256]{2,1,0:T(8,128)(2,1)S(1)}, bf16[8,64,256]{2,1,0:T(8,128)(2,1)S(1)}, u32[]{:S(2)}, u32[]{:S(2)}) %collective-permute-start.6) | collective-permute-done | bytes 262176 | tf_op jit(solution)/shard_map/ppermute | solution.py:499
  114.5 3.8 %collective-permute-done.7.fr_ref = bf16[8,64,256]{2,1,0:T(8,128)(2,1)S(1)} collective-permute-done((bf16[8,64,256]{2,1,0:T(8,128)(2,1)S(1)}, bf16[8,64,256]{2,1,0:T(8,128)(2,1)S(1)}, u32[]{:S(2)}, u32[]{:S(2)}) %collective-permute-start.7) | collective-permute-done | bytes 262176 | tf_op jit(solution)/shard_map/ppermute | solution.py:498
  118.4 6.9 %shard_map.109 = bf16[2,64,2048]{2,1,0:T(8,128)(2,1)} custom-call(bf16[2,3,34,64,128]{4,3,2,1,0:T(8,128)(2,1)S(1)} %get-tuple-element.51.ds_ref, bf16[3,256,2304]{2,1,0:T(8,128)(2,1)S(1)} %get-tuple-element.50.back_ref, bf16[8,64,256]{2,1,0:T(8,128)(2,1)S(1)} %collective-permute-done.6.fl_ref, bf16[8,64,256]{2,1,0:T(8,128)(2,1)S(1)} %collective-permute-done.7.fr_ref), custom_call_target="tpu_custom_call" | custom-call | flops 2415919104 | bytes 8388608 | tf_op jit(solution)/shard_map/pallas_call | solution.py:369
  125.3 0.0 all-to-all-done.3.in_ref
  125.3 2.2 %shard_map.113 = (f32[1728,128]{1,0:T(8,128)}, f32[1,128]{1,0:T(1,128)}, f32[864,64]{1,0:T(8,128)}, f32[1,64]{1,0:T(1,128)}) custom-call(bf16[16,144,128]{2,1,0:T(8,128)(2,1)} %all-to-all-done.3.in_ref), custom_call_target="tpu_custom_call" | custom-call | bytes 1048576 | tf_op jit(solution)/shard_map/pallas_call | solution.py:369
  (5 shorter events, 0.0 us)
Async XLA Ops:
  1.7 9.7 %collective-permute-start.1 = (bf16[64,2048]{1,0:T(8,128)(2,1)S(1)}, bf16[64,2048]{1,0:T(8,128)(2,1)S(1)}, u32[]{:S(2)}, u32[]{:S(2)}) collective-permute-start(bf16[64,2048]{1,0:T(8,128)(2,1)S(1)} %get-tuple-element.59.x0_ref), channel_id=1, source_target_pairs={{1,0},{2,1},{3,2},{4,3},{5,4},{6,5},{7,6},{8,7},{9,8},{10,9},{11,1... | collective-permute-start | bytes 786440 | tf_op jit(solution)/shard_map/ppermute | solution.py:393
  3.0 8.4 %collective-permute-start = (bf16[64,2048]{1,0:T(8,128)(2,1)S(1)}, bf16[64,2048]{1,0:T(8,128)(2,1)S(1)}, u32[]{:S(2)}, u32[]{:S(2)}) collective-permute-start(bf16[64,2048]{1,0:T(8,128)(2,1)S(1)} %get-tuple-element.60.x1_ref), channel_id=1, source_target_pairs={{0,1},{1,2},{2,3},{3,4},{4,5},{5,6},{6,7},{7,8},{8,9},{9,10},{10,1... | collective-permute-start | bytes 786440 | tf_op jit(solution)/shard_map/ppermute | solution.py:392
  8.0 0.9 copy-start.7
  8.9 2.5 %copy-start.4 = (f32[64]{0:T(128)S(1)}, f32[64]{0:T(128)}, u32[]{:S(2)}) copy-start(f32[64]{0:T(128)} %param.8) | copy-start | bytes 772
  11.4 9.9 %copy-start.6 = (bf16[3,3,3,64,128]{4,3,2,1,0:T(8,128)(2,1)S(1)}, bf16[3,3,3,64,128]{4,3,2,1,0:T(8,128)(2,1)}, u32[]{:S(2)}) copy-start(bf16[3,3,3,64,128]{4,3,2,1,0:T(8,128)(2,1)} %param.9) | copy-start | bytes 1327108
  11.4 9.9 %copy-start.8 = (bf16[3,3,3,32,64]{4,3,2,1,0:T(8,128)(2,1)S(1)}, bf16[3,3,3,32,64]{4,3,2,1,0:T(8,128)(2,1)}, u32[]{:S(2)}) copy-start(bf16[3,3,3,32,64]{4,3,2,1,0:T(8,128)(2,1)} %param.7) | copy-start | bytes 331780
  11.4 11.0 %copy-start.5 = (f32[128]{0:T(128)S(1)}, f32[128]{0:T(128)}, u32[]{:S(2)}) copy-start(f32[128]{0:T(128)} %param.10) | copy-start | bytes 1540
  14.3 9.0 %copy-start.3 = (bf16[1,1,32,4096]{3,2,1,0:T(8,128)(2,1)S(1)}, bf16[1,1,32,4096]{3,2,1,0:T(8,128)(2,1)}, u32[]{:S(2)}) copy-start(bf16[1,1,32,4096]{3,2,1,0:T(8,128)(2,1)} %param.11) | copy-start | bytes 786436
  14.3 8.6 %collective-permute-start.3 = (bf16[16,32,128]{2,1,0:T(8,128)(2,1)S(1)}, bf16[16,32,128]{2,1,0:T(8,128)(2,1)S(1)}, u32[]{:S(2)}, u32[]{:S(2)}) collective-permute-start(bf16[16,32,128]{2,1,0:T(8,128)(2,1)S(1)} %get-tuple-element.34.own_ref), channel_id=1, source_target_pairs={{1,0},{2,1},{3,2},{4,3},{5,4},{6,5},{7,6},{8,7},{9,8},{10,9},{11,1... | collective-permute-start | bytes 393224 | tf_op jit(solution)/shard_map/ppermute | solution.py:432
  15.7 7.5 %collective-permute-start.2 = (bf16[16,32,128]{2,1,0:T(8,128)(2,1)S(1)}, bf16[16,32,128]{2,1,0:T(8,128)(2,1)S(1)}, u32[]{:S(2)}, u32[]{:S(2)}) collective-permute-start(bf16[16,32,128]{2,1,0:T(8,128)(2,1)S(1)} %get-tuple-element.34.own_ref), channel_id=1, source_target_pairs={{0,1},{1,2},{2,3},{3,4},{4,5},{5,6},{6,7},{7,8},{8,9},{9,10},{10,1... | collective-permute-start | bytes 393224 | tf_op jit(solution)/shard_map/ppermute | solution.py:431
  25.5 6.8 %collective-permute-start.4 = (bf16[16,32,128]{2,1,0:T(8,128)(2,1)S(1)}, bf16[16,32,128]{2,1,0:T(8,128)(2,1)S(1)}, u32[]{:S(2)}, u32[]{:S(2)}) collective-permute-start(bf16[16,32,128]{2,1,0:T(8,128)(2,1)S(1)} %get-tuple-element.43), channel_id=1, source_target_pairs={{0,1},{1,2},{2,3},{3,4},{4,5},{5,6},{6,7},{7,8},{8,9},{9,10},{10,1... | collective-permute-start | bytes 393224 | tf_op jit(solution)/shard_map/ppermute | solution.py:458
  29.6 6.5 %collective-permute-start.5 = (bf16[16,32,128]{2,1,0:T(8,128)(2,1)S(1)}, bf16[16,32,128]{2,1,0:T(8,128)(2,1)S(1)}, u32[]{:S(2)}, u32[]{:S(2)}) collective-permute-start(bf16[16,32,128]{2,1,0:T(8,128)(2,1)S(1)} %get-tuple-element.44), channel_id=1, source_target_pairs={{1,0},{2,1},{3,2},{4,3},{5,4},{6,5},{7,6},{8,7},{9,8},{10,9},{11,1... | collective-permute-start | bytes 393224 | tf_op jit(solution)/shard_map/ppermute | solution.py:457
  39.7 45.6 %copy-start.1 = (bf16[2,16,64,256]{3,2,1,0:T(8,128)(2,1)}, bf16[2,16,64,256]{3,2,1,0:T(8,128)(2,1)S(1)}, u32[]{:S(2)}) copy-start(bf16[2,16,64,256]{3,2,1,0:T(8,128)(2,1)S(1)} %get-tuple-element.49.delta_ref) | copy-start | bytes 3145732
  95.3 0.8 copy-start
  96.1 29.1 %all-to-all-start.3 = ((bf16[16,144,128]{2,1,0:T(8,128)(2,1)}), bf16[16,144,128]{2,1,0:T(8,128)(2,1)}, u32[]{:S(2)}, u32[]{:S(2)}) async-start(bf16[16,144,128]{2,1,0:T(8,128)(2,1)} %copy-done), calls=%async_computation.3 | async-start | bytes 1179648 | tf_op jit(solution)/shard_map/all_to_all | solution.py:525
  103.1 1.2 copy-start.2
  106.5 8.0 %collective-permute-start.6 = (bf16[8,64,256]{2,1,0:T(8,128)(2,1)S(1)}, bf16[8,64,256]{2,1,0:T(8,128)(2,1)S(1)}, u32[]{:S(2)}, u32[]{:S(2)}) collective-permute-start(bf16[8,64,256]{2,1,0:T(8,128)(2,1)S(1)} %get-tuple-element.52), channel_id=1, source_target_pairs={{0,1},{1,2},{2,3},{3,4},{4,5},{5,6},{6,7},{7,8},{8,9},{9,10},{10,1... | collective-permute-start | bytes 786440 | tf_op jit(solution)/shard_map/ppermute | solution.py:499
  109.2 9.2 %collective-permute-start.7 = (bf16[8,64,256]{2,1,0:T(8,128)(2,1)S(1)}, bf16[8,64,256]{2,1,0:T(8,128)(2,1)S(1)}, u32[]{:S(2)}, u32[]{:S(2)}) collective-permute-start(bf16[8,64,256]{2,1,0:T(8,128)(2,1)S(1)} %get-tuple-element.53), channel_id=1, source_target_pairs={{1,0},{2,1},{3,2},{4,3},{5,4},{6,5},{7,6},{8,7},{9,8},{10,9},{11,1... | collective-permute-start | bytes 786440 | tf_op jit(solution)/shard_map/ppermute | solution.py:498
where the time goes:
time: 129 us; the launch traced here: 127 us
  blocking collectives  55.4 us (43%)
  starting transfers between devices  29.8 us (23%)
  Pallas kernels  25.5 us (20%)
  waiting for transfers between devices  11.9 us (9%)
  local copies, waits for them, and re-layouts  4.06 us (3%)
    pallas_call x13, Pallas kernels, _call(): pl.pallas_call(kernel, out_shape=out, scratch_shapes=scratch, compiler_pa...  25.5 us
    all_to_all x1, blocking collectives, local(): met = lax.all_to_all(parts, 'dp', 0, 0)  23.1 us
    all_to_all x1, blocking collectives, local(): met = lax.all_to_all(pieces, 'space', 0, 0)  22.4 us
    all_to_all x1, blocking collectives, local(): met = lax.all_to_all(total, 'space', 0, 0)  9.95 us
    all_to_all x1, starting transfers between devices, local(): done = lax.all_to_all(joined, 'dp', 0, 0)  7 us
    ppermute x1, starting transfers between devices, local(): pool_left = lax.ppermute(pooled, 'space', up)  5.59 us
    ppermute x1, starting transfers between devices, local(): from_left = lax.ppermute(x1, 'space', up)  5 us
    ppermute x1, starting transfers between devices, local(): gp_from_left = lax.ppermute(gp_right, 'space', up)  4.11 us
  transfers between devices with their start and end apart: 9, of which 4 were waited for; matrix products, arithmetic and copies ran while one was open for 0% of the time, Pallas kernels for 11%

commit v1 on v0

--- a/solution.py
+++ b/solution.py
@@ -25,10 +25,6 @@
 
 def _dot(a, b):
     return lax.dot_general(a, b, (((1,), (0,)), ((), ())), preferred_element_type=F32)
-
-
-def _dot_t(a, b):
-    return lax.dot_general(a, b, (((1,), (1,)), ((), ())), preferred_element_type=F32)
 
 
 def _sigmoid(v):
@@ -62,34 +58,34 @@
     return jnp.concatenate([a, b], axis=1)
 
 
-def _prep_kernel(w_one_ref, w_two_ref, back_one, band_two, back_two):
-    for ref in (back_one, band_two, back_two):
-        ref[...] = jnp.zeros(ref.shape, BF16)
+def _back_bands(w_ref, kk, out, size, first):
+    chan_in, chan_out = w_ref.shape[1] // 3, w_ref.shape[2]
+    flip = w_ref[kk].astype(F32).T.astype(BF16)
+    for i in range(size // chan_out):
+        start = chan_in * (i - first)
+        low, high = max(start, 0), min(start + 3 * chan_in, 256)
+        if low < high:
+            r = size * (kk % 3) + chan_out * i
+            out[r : r + chan_out, low:high] = flip[:, low - start : high - start]
+
+
+def _prep_kernel(w_ref, band_two, back_two):
+    band_two[...] = jnp.zeros(band_two.shape, BF16)
+    back_two[...] = jnp.zeros(back_two.shape, BF16)
     for kk in range(9):
-        kd, kh = kk // 3, kk % 3
-        for kw in range(3):
-            tap = w_one_ref[3 * kk + kw]
-            for j in range(8):
-                c = 768 * kh + 64 * (j - kw + 3)
-                back_one[kd, 32 * j : 32 * j + 32, c : c + 64] = tap
-            tap = w_two_ref[3 * kk + kw]
-            for j in range(2):
-                r = 256 * kk + 64 * (j + kw)
-                band_two[r : r + 64, LANES * j : LANES * (j + 1)] = tap
-            for j in range(4):
-                c = 768 * kh + LANES * (j - kw + 2)
-                back_two[kd, 64 * j : 64 * j + 64, c : c + LANES] = tap
+        for j in range(2):
+            r = 256 * kk + 64 * j
+            band_two[r : r + 192, LANES * j : LANES * (j + 1)] = w_ref[kk]
+        _back_bands(w_ref, kk, back_two.at[kk // 3], 768, 2)
 
 
 def _first_kernel(x0_ref, x1_ref, w_ref, pre_ref, xs_ref, band_ref, buf):
     rows, groups = x0_ref.shape[0], pre_ref.shape[1]
     band_ref[...] = jnp.zeros(band_ref.shape, BF16)
     for kk in range(9):
-        for kw in range(3):
-            tap = w_ref[3 * kk + kw]
-            for j in range(4):
-                r = 256 * kk + 32 * (j + kw)
-                band_ref[r : r + 32, 64 * j : 64 * j + 64] = tap
+        for j in range(4):
+            r = 256 * kk + 32 * j
+            band_ref[r : r + 96, 64 * j : 64 * j + 64] = w_ref[kk]
     _zero_edges(buf, rows)
     for p, ref in enumerate((x0_ref, x1_ref)):
         _spread(lambda t, ref=ref: ref[:, LANES * t : LANES * (t + 1)], groups, rows, 32, buf, xs_ref.at[p])
@@ -179,7 +175,7 @@
     wide = cells // 4
     lhs = _window(ds_ref, 0, wide)
     for kd, ref in ((0, gl_ref), (2, gr_ref)):
-        _put_cells(ref, _dot_t(lhs, back_ref[kd]), wide, rows)
+        _put_cells(ref, _dot(lhs, back_ref[kd]), wide, rows)
 
 
 def _put_cells(ref, out, wide, rows):
@@ -191,7 +187,7 @@
 def _own_two_kernel(delta_ref, own_ref, halo_ref, ds_ref, back_ref, gm_ref, out_ref):
     groups, rows = own_ref.shape[1] - 1, own_ref.shape[2]
     out_ref[1728:, :] = jnp.zeros((out_ref.shape[0] - 1728, LANES), BF16)
-    _put_cells(gm_ref, _dot_t(_window(ds_ref, 0, groups // 2), back_ref[1]), groups // 2, rows)
+    _put_cells(gm_ref, _dot(_window(ds_ref, 0, groups // 2), back_ref[1]), groups // 2, rows)
     delta = delta_ref[...]
     flip = delta.astype(F32).T.astype(BF16)
     planes = (halo_ref.at[0], own_ref, halo_ref.at[1])
@@ -258,15 +254,18 @@
         out_ref[i, rows_two:, :] = one[i * rows_one : (i + 1) * rows_one, :]
 
 
-def _sides_kernel(delta_ref, back_ref, ds_ref, gl_ref, gr_ref, buf):
+def _input_kernel(delta_ref, w_ref, gl_ref, own_ref, gr_ref, ds, back, buf):
     groups, rows = delta_ref.shape[1], delta_ref.shape[2]
     cells = 2 * groups
+    back[...] = jnp.zeros(back.shape, BF16)
+    for kk in range(9):
+        _back_bands(w_ref, kk, back.at[kk // 3], 768, 3)
     _zero_edges(buf, rows)
     zero = jnp.zeros((rows, LANES), BF16)
     for p in range(2):
         for kh in range(3):
-            ds_ref[p, kh, 0] = zero
-            ds_ref[p, kh, cells + 1] = zero
+            ds[p, kh, 0] = zero
+            ds[p, kh, cells + 1] = zero
 
     def group(g, carry):
         for p in range(2):
@@ -275,21 +274,26 @@
                 spot = buf.at[2 * p + j]
                 spot[8 : 8 + rows, :] = low.astype(F32)
                 t = 2 * g + j + 1
-                ds_ref[p, 0, t] = spot[9 : 9 + rows, :].astype(BF16)
-                ds_ref[p, 1, t] = low
-                ds_ref[p, 2, t] = spot[7 : 7 + rows, :].astype(BF16)
+                ds[p, 0, t] = spot[9 : 9 + rows, :].astype(BF16)
+                ds[p, 1, t] = low
+                ds[p, 2, t] = spot[7 : 7 + rows, :].astype(BF16)
         return carry
 
     lax.fori_loop(0, groups, group, 0)
-    step = cells // 8
+    step = 4
 
     def chunk(c, carry):
-        for p, kd, ref in ((0, 0, gl_ref), (1, 2, gr_ref)):
-            out = _dot_t(_window(ds_ref.at[p], c * step, step), back_ref[kd])
-            ref[pl.ds(c * step, step)] = out.astype(BF16).reshape(step, rows, 256)
+        g = c * step
+        spot = pl.ds(g, step)
+        near = _window(ds.at[0], g, step)
+        far = _window(ds.at[1], g, step)
+        gl_ref[spot] = _dot(near, back[0]).astype(BF16).reshape(step, rows, 256)
+        gr_ref[spot] = _dot(far, back[2]).astype(BF16).reshape(step, rows, 256)
+        own_ref[0, spot] = (_dot(near, back[1]) + _dot(far, back[0])).reshape(step, rows, 256)
+        own_ref[1, spot] = (_dot(near, back[2]) + _dot(far, back[1])).reshape(step, rows, 256)
         return carry
 
-    lax.fori_loop(0, 2, chunk, 0)
+    lax.fori_loop(0, groups // 2 // step, chunk, 0)
 
 
 def _window(ref, first, count):
@@ -300,17 +304,11 @@
     return jnp.concatenate(parts, axis=1)
 
 
-def _grad_input_kernel(ds_ref, back_ref, fl_ref, fr_ref, out_ref):
-    wide, rows = fl_ref.shape[0], fl_ref.shape[1]
-    for g in range(0, wide, 2):
-        near = _window(ds_ref.at[0], g, 2)
-        far = _window(ds_ref.at[1], g, 2)
-        first = _dot_t(near, back_ref[1]) + _dot_t(far, back_ref[0])
-        second = _dot_t(near, back_ref[2]) + _dot_t(far, back_ref[1])
-        for s in range(2):
-            for p, val, ref in ((0, first, fl_ref), (1, second, fr_ref)):
-                whole = val[s * rows : (s + 1) * rows] + ref[g + s].astype(F32)
-                out_ref[p, :, 256 * (g + s) : 256 * (g + s + 1)] = whole.astype(BF16)
+def _edges_kernel(own_ref, fl_ref, fr_ref, out_ref):
+    for g in range(fl_ref.shape[0]):
+        for p, ref in ((0, fl_ref), (1, fr_ref)):
+            whole = own_ref[p, g] + ref[g].astype(F32)
+            out_ref[p, :, 256 * g : 256 * (g + 1)] = whole.astype(BF16)
 
 
 def _split_kernel(scale_two, scale_one, rows_two, in_ref, out_ref, buf):
@@ -391,8 +389,8 @@
     x0, x1 = x[0], x[slab - 1]
     from_left = lax.ppermute(x1, "space", up)
     from_right = lax.ppermute(x0, "space", down)
-    w_one = weight_one.reshape(27, c0, c1)
-    w_two = weight_two.reshape(27, c1, c2)
+    w_one = weight_one.reshape(9, 3 * c0, c1)
+    w_two = weight_two.reshape(9, 3 * c1, c2)
     groups = merged // LANES
     xs_shape = (2, 3, groups + 1, side, LANES)
     work = 2 * side * groups * 256
@@ -410,14 +408,8 @@
         16,
         (x0, x1, w_one),
     )
-    back_one, band_two, back_two = _call(
-        _prep_kernel,
-        (_shape((3, 256, 2304), BF16), _shape((2304, 256), BF16), _shape((3, 256, 2304), BF16)),
-        [],
-        work * 768,
-        8 * MIB,
-        16,
-        (w_one, w_two),
+    band_two, back_two = _call(
+        _prep_kernel, (_shape((2304, 256), BF16), _shape((3, 2304, 256), BF16)), [], work * 768, 8 * MIB, 12, (w_two,)
     )
     slope, pooled, xs_halo = _call(
         _second_kernel,
@@ -482,29 +474,30 @@
     rows_two //= dp
     rows_one //= dp
     met = lax.all_to_all(parts, "dp", 0, 0)
-    ds, gx_left, gx_right = _call(
-        _sides_kernel,
-        (
-            _shape((2, 3, 2 * groups + 2, side, LANES), BF16),
-            _shape((groups // 2, side, 256), BF16),
-            _shape((groups // 2, side, 256), BF16),
-        ),
-        [pltpu.VMEM((4, side + 16, LANES), F32)],
+    block = _shape((groups // 2, side, 256), BF16)
+    gx_left, gx_own, gx_right = _call(
+        _input_kernel,
+        (block, _shape((2, groups // 2, side, 256), F32), block),
+        [
+            pltpu.VMEM((2, 3, 2 * groups + 2, side, LANES), BF16),
+            pltpu.VMEM((3, 2304, 256), BF16),
+            pltpu.VMEM((4, side + 16, LANES), F32),
+        ],
         2 * work * 2304 // 2,
         8 * MIB,
-        16,
-        (delta_one, back_one),
+        20,
+        (delta_one, w_one),
     )
     gx_from_right = lax.ppermute(gx_left, "space", down)
     gx_from_left = lax.ppermute(gx_right, "space", up)
     grad_x = _call(
-        _grad_input_kernel,
+        _edges_kernel,
         _shape((2, side, merged), BF16),
         [],
-        2 * work * 2304,
-        8 * MIB,
-        16,
-        (ds, back_one, gx_from_left, gx_from_right),
+        2 * work * 128,
+        4 * MIB,
+        12,
+        (gx_own, gx_from_left, gx_from_right),
     )
     small = _shape((space, _round_up(rows_all // space, 16), LANES), BF16)
     pieces = _call(

time: 129 us -> 119 us (0.922)
  blocking collectives: 55.4 us -> 46.5 us
  waiting for transfers between devices: 11.9 us -> 19.7 us
  Pallas kernels: 25.5 us -> 22.2 us
  starting transfers between devices: 29.8 us -> 26.5 us
  local copies, waits for them, and re-layouts: 4.06 us -> 2.02 us
    all_to_all x1, blocking collectives: 22.4 us -> 12.7 us  [local(): met = lax.all_to_all(pieces, 'space', 0, 0)]
    ppermute x1, waiting for transfers between devices: 0.01 us -> 4.55 us  [local(): pool_right = lax.ppermute(pooled, 'space', down)]
    ppermute x1, waiting for transfers between devices: 0.01 us -> 4.19 us  [local(): from_right = lax.ppermute(x0, 'space', down)]
    pallas_call x13, Pallas kernels: 25.5 us -> 22.2 us  [_call(): pl.pallas_call(kernel, out_shape=out, scratch_shapes=scratch, compiler_pa...]
    unnamed x18 -> x12, local copies, waits for them, and re-layouts: 2.99 us -> 0.95 us
    ppermute x1, starting transfers between devices: 5.59 us -> 3.7 us  [local(): pool_left = lax.ppermute(pooled, 'space', up)]
  transfers between devices with their start and end apart: 9 -> 9, of which waited for: 4 -> 6; matrix products, arithmetic and copies ran while one was open for 0% -> 0% of each run, Pallas kernels for 11% -> 10%
where the time goes in v1:
time: 119 us; the launch traced here: 118 us
  blocking collectives  46.5 us (39%)
  starting transfers between devices  26.5 us (22%)
  Pallas kernels  22.2 us (19%)
  waiting for transfers between devices  19.7 us (17%)
  local copies, waits for them, and re-layouts  2.02 us (2%)
    all_to_all x1, blocking collectives, local(): met = lax.all_to_all(parts, 'dp', 0, 0)  23.8 us
    pallas_call x13, Pallas kernels, _call(): pl.pallas_call(kernel, out_shape=out, scratch_shapes=scratch, compiler_pa...  22.2 us
    all_to_all x1, blocking collectives, local(): met = lax.all_to_all(pieces, 'space', 0, 0)  12.7 us
    all_to_all x1, blocking collectives, local(): met = lax.all_to_all(total, 'space', 0, 0)  9.95 us
    all_to_all x1, starting transfers between devices, local(): done = lax.all_to_all(joined, 'dp', 0, 0)  6.39 us
    ppermute x1, waiting for transfers between devices, local(): pool_right = lax.ppermute(pooled, 'space', down)  4.55 us
    ppermute x1, starting transfers between devices, local(): from_left = lax.ppermute(x1, 'space', up)  4.38 us
    ppermute x1, starting transfers between devices, local(): gp_from_left = lax.ppermute(gp_right, 'space', up)  4.3 us
  transfers between devices with their start and end apart: 9, of which 6 were waited for; matrix products, arithmetic and copies ran while one was open for 0% of the time, Pallas kernels for 10%

profile of v1, /device:TPU:1, one launch (start us, length us, event | category | flops | bytes accessed | tf_op | source)
XLA Modules:
  0.0 117.7 jit_solution(5410870747353417013)
XLA Ops:
  0.6 1.1 slice_bitcast_fusion
  1.7 4.4 %collective-permute-start = (bf16[64,2048]{1,0:T(8,128)(2,1)S(1)}, bf16[64,2048]{1,0:T(8,128)(2,1)S(1)}, u32[]{:S(2)}, u32[]{:S(2)}) collective-permute-start(bf16[64,2048]{1,0:T(8,128)(2,1)S(1)} %get-tuple-element.58.x1_ref), channel_id=1, source_target_pairs={{0,1},{1,2},{2,3},{3,4},{4,5},{5,6},{6,7},{7,8},{8,9},{9,10},{10,1... | collective-permute-start | bytes 786440 | tf_op jit(solution)/shard_map/ppermute | solution.py:390
  6.1 1.3 %collective-permute-start.1 = (bf16[64,2048]{1,0:T(8,128)(2,1)S(1)}, bf16[64,2048]{1,0:T(8,128)(2,1)S(1)}, u32[]{:S(2)}, u32[]{:S(2)}) collective-permute-start(bf16[64,2048]{1,0:T(8,128)(2,1)S(1)} %get-tuple-element.57.x0_ref), channel_id=1, source_target_pairs={{1,0},{2,1},{3,2},{4,3},{5,4},{6,5},{7,6},{8,7},{9,8},{10,9},{11,1... | collective-permute-start | bytes 786440 | tf_op jit(solution)/shard_map/ppermute | solution.py:391
  7.4 0.0 copy-start.4
  7.4 0.9 copy-done.4
  8.3 0.0 copy-start.1
  8.3 2.6 %shard_map.101 = (f32[2,16,64,256]{3,2,1,0:T(8,128)S(1)}, bf16[2,3,17,64,128]{4,3,2,1,0:T(8,128)(2,1)S(1)}, bf16[2304,256]{1,0:T(8,128)(2,1)S(1)}) custom-call(bf16[64,2048]{1,0:T(8,128)(2,1)S(1)} %get-tuple-element.57.x0_ref, bf16[64,2048]{1,0:T(8,128)(2,1)S(1)} %get-tuple-element.58.x1_ref, bf16[9,96,64]{2,1,0:T(8,128)(2,1)S(1)} %bitcast.18), custom_call_target="tpu_custom_call" | custom-call | flops 1610612736 | bytes 8388608 | tf_op jit(solution)/shard_map/pallas_call | solution.py:367
  10.9 0.2 collective-permute-done.left_ref
  11.0 4.2 %collective-permute-done.1.right_ref = bf16[64,2048]{1,0:T(8,128)(2,1)S(1)} collective-permute-done((bf16[64,2048]{1,0:T(8,128)(2,1)S(1)}, bf16[64,2048]{1,0:T(8,128)(2,1)S(1)}, u32[]{:S(2)}, u32[]{:S(2)}) %collective-permute-start.1) | collective-permute-done | bytes 262176 | tf_op jit(solution)/shard_map/ppermute | solution.py:391
  15.2 0.0 copy-done.1
  15.2 0.0 copy-start.3
  15.2 0.0 copy-start.2
  15.2 2.9 %shard_map.102 = (f32[2,16,64,256]{3,2,1,0:T(8,128)S(1)}, bf16[16,32,128]{2,1,0:T(8,128)(2,1)S(1)}, bf16[2,3,17,64,128]{4,3,2,1,0:T(8,128)(2,1)S(1)}) custom-call(bf16[64,2048]{1,0:T(8,128)(2,1)S(1)} %collective-permute-done.left_ref, bf16[64,2048]{1,0:T(8,128)(2,1)S(1)} %collective-permute-done.1.right_ref, ...), custom_call_target="tpu_custom_call" | custom-call | flops 805306368 | bytes 8388608 | tf_op jit(solution)/shard_map/pallas_call | solution.py:367
  18.1 0.0 copy-start
  18.1 3.7 %collective-permute-start.2 = (bf16[16,32,128]{2,1,0:T(8,128)(2,1)S(1)}, bf16[16,32,128]{2,1,0:T(8,128)(2,1)S(1)}, u32[]{:S(2)}, u32[]{:S(2)}) collective-permute-start(bf16[16,32,128]{2,1,0:T(8,128)(2,1)S(1)} %get-tuple-element.33.own_ref), channel_id=1, source_target_pairs={{0,1},{1,2},{2,3},{3,4},{4,5},{5,6},{6,7},{7,8},{8,9},{9,10},{10,1... | collective-permute-start | bytes 393224 | tf_op jit(solution)/shard_map/ppermute | solution.py:423
  21.8 1.3 %collective-permute-start.3 = (bf16[16,32,128]{2,1,0:T(8,128)(2,1)S(1)}, bf16[16,32,128]{2,1,0:T(8,128)(2,1)S(1)}, u32[]{:S(2)}, u32[]{:S(2)}) collective-permute-start(bf16[16,32,128]{2,1,0:T(8,128)(2,1)S(1)} %get-tuple-element.33.own_ref), channel_id=1, source_target_pairs={{1,0},{2,1},{3,2},{4,3},{5,4},{6,5},{7,6},{8,7},{9,8},{10,9},{11,1... | collective-permute-start | bytes 393224 | tf_op jit(solution)/shard_map/ppermute | solution.py:424
  23.1 0.0 copy-done.3
  23.1 0.9 shard_map.103
  24.0 0.0 copy-done.2
  24.0 0.4 shard_map.104
  24.5 0.0 collective-permute-done.2.left_ref
  24.5 4.5 %collective-permute-done.3.right_ref = bf16[16,32,128]{2,1,0:T(8,128)(2,1)S(1)} collective-permute-done((bf16[16,32,128]{2,1,0:T(8,128)(2,1)S(1)}, bf16[16,32,128]{2,1,0:T(8,128)(2,1)S(1)}, u32[]{:S(2)}, u32[]{:S(2)}) %collective-permute-start.3) | collective-permute-done | bytes 131104 | tf_op jit(solution)/shard_map/ppermute | solution.py:424
  29.0 0.0 copy-done
  29.0 2.3 %shard_map.105 = (bf16[512,256]{1,0:T(8,128)(2,1)S(1)}, bf16[2,3,17,32,128]{4,3,2,1,0:T(8,128)(2,1)S(1)}, bf16[3,34,32,128]{3,2,1,0:T(8,128)(2,1)S(1)}, bf16[16,...) custom-call(bf16[16,32,128]{2,1,0:T(8,128)(2,1)S(1)} %collective-permute-done.2.left_ref, ...), custom_call_target="tpu_custom_call" | custom-call | flops 805306368 | bytes 4194304 | tf_op jit(solution)/shard_map/pallas_call | solution.py:367
  31.3 4.3 %collective-permute-start.4 = (bf16[16,32,128]{2,1,0:T(8,128)(2,1)S(1)}, bf16[16,32,128]{2,1,0:T(8,128)(2,1)S(1)}, u32[]{:S(2)}, u32[]{:S(2)}) collective-permute-start(bf16[16,32,128]{2,1,0:T(8,128)(2,1)S(1)} %get-tuple-element.42), channel_id=1, source_target_pairs={{0,1},{1,2},{2,3},{3,4},{4,5},{5,6},{6,7},{7,8},{8,9},{9,10},{10,1... | collective-permute-start | bytes 393224 | tf_op jit(solution)/shard_map/ppermute | solution.py:450
  35.6 1.3 %collective-permute-start.5 = (bf16[16,32,128]{2,1,0:T(8,128)(2,1)S(1)}, bf16[16,32,128]{2,1,0:T(8,128)(2,1)S(1)}, u32[]{:S(2)}, u32[]{:S(2)}) collective-permute-start(bf16[16,32,128]{2,1,0:T(8,128)(2,1)S(1)} %get-tuple-element.43), channel_id=1, source_target_pairs={{1,0},{2,1},{3,2},{4,3},{5,4},{6,5},{7,6},{8,7},{9,8},{10,9},{11,1... | collective-permute-start | bytes 393224 | tf_op jit(solution)/shard_map/ppermute | solution.py:449
  36.9 1.4 %shard_map.106 = (f32[16,32,128]{2,1,0:T(8,128)S(1)}, bf16[1792,128]{1,0:T(8,128)(2,1)S(1)}) custom-call(bf16[512,256]{1,0:T(8,128)(2,1)S(1)} %get-tuple-element.37.delta_ref, bf16[3,17,32,128]{3,2,1,0:T(8,128)(2,1)S(1)} %get-tuple-element.38.own_ref, bf16[2,3,17,32,128]{4,3,2,1,0:T(8,128)(2,1)S(1)} %get-tuple-element.39.halo_ref, ...), custom_call_target="tpu_custom_call" | custom-call | flops 805306368 | bytes 2097152 | tf_op jit(solution)/shard_map/pallas_call | solution.py:367
  38.4 0.0 collective-permute-done.4.fl_ref
  38.4 3.0 %collective-permute-done.5.fr_ref = bf16[16,32,128]{2,1,0:T(8,128)(2,1)S(1)} collective-permute-done((bf16[16,32,128]{2,1,0:T(8,128)(2,1)S(1)}, bf16[16,32,128]{2,1,0:T(8,128)(2,1)S(1)}, u32[]{:S(2)}, u32[]{:S(2)}) %collective-permute-start.5) | collective-permute-done | bytes 131104 | tf_op jit(solution)/shard_map/ppermute | solution.py:449
  41.4 3.5 %shard_map.107 = (bf16[2,16,64,256]{3,2,1,0:T(8,128)(2,1)S(1)}, bf16[16,144,128]{2,1,0:T(8,128)(2,1)S(1)}) custom-call(f32[16,32,128]{2,1,0:T(8,128)S(1)} %get-tuple-element.41.gm_ref, bf16[16,32,128]{2,1,0:T(8,128)(2,1)S(1)} %collective-permute-done.4.fl_ref, bf16[16,32,128]{2,1,0:T(8,128)(2,1)S(1)} %collective-permute-done.5.fr_ref, ...), custom_call_target="tpu_custom_call" | custom-call | flops 2415919104 | bytes 4194304 | tf_op jit(solution)/shard_map/pallas_call | solution.py:367
  44.9 23.8 %all_to_all.20.in_ref = bf16[16,144,128]{2,1,0:T(8,128)(2,1)S(1)} all-to-all(bf16[16,144,128]{2,1,0:T(8,128)(2,1)S(1)} %get-tuple-element.52), channel_id=1, replica_groups=mesh['dp'=16,'space'=16] {'dp'}, dimensions={0} | all-to-all | bytes 1179648 | tf_op jit(solution)/shard_map/all_to_all | solution.py:476
  68.7 0.0 copy-start.5
  68.7 0.1 shard_map.110
  68.8 12.7 %all_to_all.21.in_ref = bf16[16,16,128]{2,1,0:T(8,128)(2,1)S(1)} all-to-all(bf16[16,16,128]{2,1,0:T(8,128)(2,1)S(1)} %shard_map.110), channel_id=1, replica_groups=mesh['dp'=16,'space'=16] {'space'}, dimensions={0} | all-to-all | bytes 131072 | tf_op jit(solution)/shard_map/all_to_all | solution.py:512
  81.6 9.9 %all_to_all.22.in_ref = bf16[16,16,128]{2,1,0:T(8,128)(2,1)S(1)} all-to-all(bf16[16,16,128]{2,1,0:T(8,128)(2,1)S(1)} %shard_map.111), channel_id=1, replica_groups=mesh['dp'=16,'space'=16] {'space'}, dimensions={0} | all-to-all | bytes 131072 | tf_op jit(solution)/shard_map/all_to_all | solution.py:514
  91.5 0.9 shard_map.112
  92.4 6.4 %all-to-all-start.3 = ((bf16[16,144,128]{2,1,0:T(8,128)(2,1)}), bf16[16,144,128]{2,1,0:T(8,128)(2,1)S(1)}, u32[]{:S(2)}, u32[]{:S(2)}) async-start(bf16[16,144,128]{2,1,0:T(8,128)(2,1)} %shard_map.112), calls=%async_computation.3 | async-start | bytes 1179648 | tf_op jit(solution)/shard_map/all_to_all | solution.py:518
  98.8 0.0 copy-done.5
  98.8 5.2 %shard_map.108 = (bf16[8,64,256]{2,1,0:T(8,128)(2,1)S(1)}, f32[2,8,64,256]{3,2,1,0:T(8,128)S(1)}, bf16[8,64,256]{2,1,0:T(8,128)(2,1)S(1)}) custom-call(bf16[2,16,64,256]{3,2,1,0:T(8,128)(2,1)S(1)} %get-tuple-element.48.delta_ref, bf16[9,96,64]{2,1,0:T(8,128)(2,1)S(1)} %bitcast.19), custom_call_target="tpu_custom_call" | custom-call | flops 1207959552 | bytes 8388608 | tf_op jit(solution)/shard_map/pallas_call | solution.py:367
  104.0 2.6 %collective-permute-start.6 = (bf16[8,64,256]{2,1,0:T(8,128)(2,1)S(1)}, bf16[8,64,256]{2,1,0:T(8,128)(2,1)S(1)}, u32[]{:S(2)}, u32[]{:S(2)}) collective-permute-start(bf16[8,64,256]{2,1,0:T(8,128)(2,1)S(1)} %get-tuple-element.50), channel_id=1, source_target_pairs={{0,1},{1,2},{2,3},{3,4},{4,5},{5,6},{6,7},{7,8},{8,9},{9,10},{10,1... | collective-permute-start | bytes 786440 | tf_op jit(solution)/shard_map/ppermute | solution.py:492
  106.6 1.3 %collective-permute-start.7 = (bf16[8,64,256]{2,1,0:T(8,128)(2,1)S(1)}, bf16[8,64,256]{2,1,0:T(8,128)(2,1)S(1)}, u32[]{:S(2)}, u32[]{:S(2)}) collective-permute-start(bf16[8,64,256]{2,1,0:T(8,128)(2,1)S(1)} %get-tuple-element.51), channel_id=1, source_target_pairs={{1,0},{2,1},{3,2},{4,3},{5,4},{6,5},{7,6},{8,7},{9,8},{10,9},{11,1... | collective-permute-start | bytes 786440 | tf_op jit(solution)/shard_map/ppermute | solution.py:491
  107.9 3.9 %collective-permute-done.6.fl_ref = bf16[8,64,256]{2,1,0:T(8,128)(2,1)S(1)} collective-permute-done((bf16[8,64,256]{2,1,0:T(8,128)(2,1)S(1)}, bf16[8,64,256]{2,1,0:T(8,128)(2,1)S(1)}, u32[]{:S(2)}, u32[]{:S(2)}) %collective-permute-start.6) | collective-permute-done | bytes 262176 | tf_op jit(solution)/shard_map/ppermute | solution.py:492
  111.8 3.8 %collective-permute-done.7.fr_ref = bf16[8,64,256]{2,1,0:T(8,128)(2,1)S(1)} collective-permute-done((bf16[8,64,256]{2,1,0:T(8,128)(2,1)S(1)}, bf16[8,64,256]{2,1,0:T(8,128)(2,1)S(1)}, u32[]{:S(2)}, u32[]{:S(2)}) %collective-permute-start.7) | collective-permute-done | bytes 262176 | tf_op jit(solution)/shard_map/ppermute | solution.py:491
  115.7 0.9 shard_map.109
  116.6 0.0 all-to-all-done.3.in_ref
  116.6 1.1 shard_map.113
  (1 shorter events, 0.0 us)
Async XLA Ops:
  1.7 9.3 %collective-permute-start = (bf16[64,2048]{1,0:T(8,128)(2,1)S(1)}, bf16[64,2048]{1,0:T(8,128)(2,1)S(1)}, u32[]{:S(2)}, u32[]{:S(2)}) collective-permute-start(bf16[64,2048]{1,0:T(8,128)(2,1)S(1)} %get-tuple-element.58.x1_ref), channel_id=1, source_target_pairs={{0,1},{1,2},{2,3},{3,4},{4,5},{5,6},{6,7},{7,8},{8,9},{9,10},{10,1... | collective-permute-start | bytes 786440 | tf_op jit(solution)/shard_map/ppermute | solution.py:390
  6.1 9.1 %collective-permute-start.1 = (bf16[64,2048]{1,0:T(8,128)(2,1)S(1)}, bf16[64,2048]{1,0:T(8,128)(2,1)S(1)}, u32[]{:S(2)}, u32[]{:S(2)}) collective-permute-start(bf16[64,2048]{1,0:T(8,128)(2,1)S(1)} %get-tuple-element.57.x0_ref), channel_id=1, source_target_pairs={{1,0},{2,1},{3,2},{4,3},{5,4},{6,5},{7,6},{8,7},{9,8},{10,9},{11,1... | collective-permute-start | bytes 786440 | tf_op jit(solution)/shard_map/ppermute | solution.py:391
  7.4 0.9 copy-start.4
  8.3 6.9 %copy-start.1 = (f32[64]{0:T(128)S(1)}, f32[64]{0:T(128)}, u32[]{:S(2)}) copy-start(f32[64]{0:T(128)} %param.8) | copy-start | bytes 772
  15.2 7.9 %copy-start.3 = (bf16[3,3,3,64,128]{4,3,2,1,0:T(8,128)(2,1)S(1)}, bf16[3,3,3,64,128]{4,3,2,1,0:T(8,128)(2,1)}, u32[]{:S(2)}) copy-start(bf16[3,3,3,64,128]{4,3,2,1,0:T(8,128)(2,1)} %param.9) | copy-start | bytes 1327108
  15.2 8.8 %copy-start.2 = (f32[128]{0:T(128)S(1)}, f32[128]{0:T(128)}, u32[]{:S(2)}) copy-start(f32[128]{0:T(128)} %param.10) | copy-start | bytes 1540
  18.1 10.9 %copy-start = (bf16[1,1,32,4096]{3,2,1,0:T(8,128)(2,1)S(1)}, bf16[1,1,32,4096]{3,2,1,0:T(8,128)(2,1)}, u32[]{:S(2)}) copy-start(bf16[1,1,32,4096]{3,2,1,0:T(8,128)(2,1)} %param.11) | copy-start | bytes 786436
  18.1 6.3 %collective-permute-start.2 = (bf16[16,32,128]{2,1,0:T(8,128)(2,1)S(1)}, bf16[16,32,128]{2,1,0:T(8,128)(2,1)S(1)}, u32[]{:S(2)}, u32[]{:S(2)}) collective-permute-start(bf16[16,32,128]{2,1,0:T(8,128)(2,1)S(1)} %get-tuple-element.33.own_ref), channel_id=1, source_target_pairs={{0,1},{1,2},{2,3},{3,4},{4,5},{5,6},{6,7},{7,8},{8,9},{9,10},{10,1... | collective-permute-start | bytes 393224 | tf_op jit(solution)/shard_map/ppermute | solution.py:423
  21.8 7.2 %collective-permute-start.3 = (bf16[16,32,128]{2,1,0:T(8,128)(2,1)S(1)}, bf16[16,32,128]{2,1,0:T(8,128)(2,1)S(1)}, u32[]{:S(2)}, u32[]{:S(2)}) collective-permute-start(bf16[16,32,128]{2,1,0:T(8,128)(2,1)S(1)} %get-tuple-element.33.own_ref), channel_id=1, source_target_pairs={{1,0},{2,1},{3,2},{4,3},{5,4},{6,5},{7,6},{8,7},{9,8},{10,9},{11,1... | collective-permute-start | bytes 393224 | tf_op jit(solution)/shard_map/ppermute | solution.py:424
  31.3 7.0 %collective-permute-start.4 = (bf16[16,32,128]{2,1,0:T(8,128)(2,1)S(1)}, bf16[16,32,128]{2,1,0:T(8,128)(2,1)S(1)}, u32[]{:S(2)}, u32[]{:S(2)}) collective-permute-start(bf16[16,32,128]{2,1,0:T(8,128)(2,1)S(1)} %get-tuple-element.42), channel_id=1, source_target_pairs={{0,1},{1,2},{2,3},{3,4},{4,5},{5,6},{6,7},{7,8},{8,9},{9,10},{10,1... | collective-permute-start | bytes 393224 | tf_op jit(solution)/shard_map/ppermute | solution.py:450
  35.6 5.7 %collective-permute-start.5 = (bf16[16,32,128]{2,1,0:T(8,128)(2,1)S(1)}, bf16[16,32,128]{2,1,0:T(8,128)(2,1)S(1)}, u32[]{:S(2)}, u32[]{:S(2)}) collective-permute-start(bf16[16,32,128]{2,1,0:T(8,128)(2,1)S(1)} %get-tuple-element.43), channel_id=1, source_target_pairs={{1,0},{2,1},{3,2},{4,3},{5,4},{6,5},{7,6},{8,7},{9,8},{10,9},{11,1... | collective-permute-start | bytes 393224 | tf_op jit(solution)/shard_map/ppermute | solution.py:449
  68.7 30.0 %copy-start.5 = (bf16[3,3,3,32,64]{4,3,2,1,0:T(8,128)(2,1)S(1)}, bf16[3,3,3,32,64]{4,3,2,1,0:T(8,128)(2,1)}, u32[]{:S(2)}) copy-start(bf16[3,3,3,32,64]{4,3,2,1,0:T(8,128)(2,1)} %param.7) | copy-start | bytes 331780
  92.4 24.2 %all-to-all-start.3 = ((bf16[16,144,128]{2,1,0:T(8,128)(2,1)}), bf16[16,144,128]{2,1,0:T(8,128)(2,1)S(1)}, u32[]{:S(2)}, u32[]{:S(2)}) async-start(bf16[16,144,128]{2,1,0:T(8,128)(2,1)} %shard_map.112), calls=%async_computation.3 | async-start | bytes 1179648 | tf_op jit(solution)/shard_map/all_to_all | solution.py:518
  104.0 7.8 %collective-permute-start.6 = (bf16[8,64,256]{2,1,0:T(8,128)(2,1)S(1)}, bf16[8,64,256]{2,1,0:T(8,128)(2,1)S(1)}, u32[]{:S(2)}, u32[]{:S(2)}) collective-permute-start(bf16[8,64,256]{2,1,0:T(8,128)(2,1)S(1)} %get-tuple-element.50), channel_id=1, source_target_pairs={{0,1},{1,2},{2,3},{3,4},{4,5},{5,6},{6,7},{7,8},{8,9},{9,10},{10,1... | collective-permute-start | bytes 786440 | tf_op jit(solution)/shard_map/ppermute | solution.py:492
  106.6 9.1 %collective-permute-start.7 = (bf16[8,64,256]{2,1,0:T(8,128)(2,1)S(1)}, bf16[8,64,256]{2,1,0:T(8,128)(2,1)S(1)}, u32[]{:S(2)}, u32[]{:S(2)}) collective-permute-start(bf16[8,64,256]{2,1,0:T(8,128)(2,1)S(1)} %get-tuple-element.51), channel_id=1, source_target_pairs={{1,0},{2,1},{3,2},{4,3},{5,4},{6,5},{7,6},{8,7},{9,8},{10,9},{11,1... | collective-permute-start | bytes 786440 | tf_op jit(solution)/shard_map/ppermute | solution.py:491

commit v2 on v1

--- a/solution.py
+++ b/solution.py
@@ -289,8 +289,9 @@
         far = _window(ds.at[1], g, step)
         gl_ref[spot] = _dot(near, back[0]).astype(BF16).reshape(step, rows, 256)
         gr_ref[spot] = _dot(far, back[2]).astype(BF16).reshape(step, rows, 256)
-        own_ref[0, spot] = (_dot(near, back[1]) + _dot(far, back[0])).reshape(step, rows, 256)
-        own_ref[1, spot] = (_dot(near, back[2]) + _dot(far, back[1])).reshape(step, rows, 256)
+        for p in range(2):
+            own = _dot(near, back[1 + p]) + _dot(far, back[p])
+            own_ref[p, spot] = own.astype(BF16).reshape(step, rows, 256)
         return carry
 
     lax.fori_loop(0, groups // 2 // step, chunk, 0)
@@ -307,34 +308,22 @@
 def _edges_kernel(own_ref, fl_ref, fr_ref, out_ref):
     for g in range(fl_ref.shape[0]):
         for p, ref in ((0, fl_ref), (1, fr_ref)):
-            whole = own_ref[p, g] + ref[g].astype(F32)
+            whole = own_ref[p, g].astype(F32) + ref[g].astype(F32)
             out_ref[p, :, 256 * g : 256 * (g + 1)] = whole.astype(BF16)
 
 
-def _split_kernel(scale_two, scale_one, rows_two, in_ref, out_ref, buf):
-    count, rows = out_ref.shape[0], in_ref.shape[1]
+def _split_kernel(scale_two, scale_one, rows_two, in_ref, out_ref):
     whole = jnp.sum(in_ref[...].astype(F32), axis=0)
-    buf[0:rows_two, :] = whole[0:rows_two] * scale_two
-    buf[rows_two:rows, :] = whole[rows_two:] * scale_one
-    buf[rows:, :] = jnp.zeros((buf.shape[0] - rows, LANES), F32)
-    part, tall = rows // count, out_ref.shape[1]
-    for i in range(count):
-        out_ref[i] = buf[i * part : i * part + tall, :].astype(BF16)
-
-
-def _sum_kernel(in_ref, out_ref):
-    whole = jnp.sum(in_ref[...].astype(F32), axis=0).astype(BF16)
-    for i in range(out_ref.shape[0]):
-        out_ref[i] = whole
-
-
-def _join_kernel(in_ref, out_ref, buf):
-    count, tall = in_ref.shape[0], in_ref.shape[1]
-    rows = out_ref.shape[1]
-    part = rows // count
-    for i in range(count):
-        buf[i * part : i * part + tall, :] = in_ref[i].astype(F32)
-    whole = buf[0:rows, :].astype(BF16)
+    out_ref[0:rows_two, :] = (whole[0:rows_two] * scale_two).astype(BF16)
+    out_ref[rows_two:, :] = (whole[rows_two:] * scale_one).astype(BF16)
+
+
+def _add_kernel(a_ref, b_ref, out_ref):
+    out_ref[...] = (a_ref[...].astype(F32) + b_ref[...].astype(F32)).astype(BF16)
+
+
+def _join_kernel(a_ref, b_ref, out_ref):
+    whole = (a_ref[...].astype(F32) + b_ref[...].astype(F32)).astype(BF16)
     for i in range(out_ref.shape[0]):
         out_ref[i] = whole
 
@@ -477,7 +466,7 @@
     block = _shape((groups // 2, side, 256), BF16)
     gx_left, gx_own, gx_right = _call(
         _input_kernel,
-        (block, _shape((2, groups // 2, side, 256), F32), block),
+        (block, _shape((2, groups // 2, side, 256), BF16), block),
         [
             pltpu.VMEM((2, 3, 2 * groups + 2, side, LANES), BF16),
             pltpu.VMEM((3, 2304, 256), BF16),
@@ -499,22 +488,14 @@
         12,
         (gx_own, gx_from_left, gx_from_right),
     )
-    small = _shape((space, _round_up(rows_all // space, 16), LANES), BF16)
-    pieces = _call(
-        functools.partial(_split_kernel, scale_two, scale_one, rows_two),
-        small,
-        [pltpu.VMEM((rows_all + 16, LANES), F32)],
-        0,
-        MIB,
-        8,
-        (met,),
-    )
-    met = lax.all_to_all(pieces, "space", 0, 0)
-    total = _call(_sum_kernel, small, [], 0, MIB, 8, (met,))
-    met = lax.all_to_all(total, "space", 0, 0)
-    joined = _call(
-        _join_kernel, _shape((dp, rows_all, LANES), BF16), [pltpu.VMEM((rows_all + 16, LANES), F32)], 0, MIB, 8, (met,)
-    )
+    flat = _shape((rows_all, LANES), BF16)
+    mine = _call(functools.partial(_split_kernel, scale_two, scale_one, rows_two), flat, [], 0, MIB, 8, (met,))
+    far = [space // 2] + [2**k for k in range(space.bit_length() - 2)]
+    for k, gap in enumerate(far):
+        other = lax.ppermute(mine, "space", [(i, i ^ gap) for i in range(space)])
+        if k < len(far) - 1:
+            mine = _call(_add_kernel, flat, [], 0, MIB, 8, (mine, other))
+    joined = _call(_join_kernel, _shape((dp, rows_all, LANES), BF16), [], 0, MIB, 8, (mine, other))
     done = lax.all_to_all(joined, "dp", 0, 0)
     gw_two, gb_two, gw_one, gb_one = _call(
         functools.partial(_unpack_kernel, rows_two, rows_one),

time: 119 us -> 116 us (0.975)
  blocking collectives: 46.5 us -> 23.8 us
  starting transfers between devices: 26.5 us -> 37.3 us
  waiting for transfers between devices: 19.7 us -> 28.7 us
    all_to_all x2 -> x0, blocking collectives: 22.6 us -> none  [the longest x1 12.7 us: local(): met = lax.all_to_all(pieces, 'space', 0, 0)]
    ppermute x0 -> x4, waiting for transfers between devices: none -> 8.84 us  [local(): other = lax.ppermute(mine, 'space', [(i, i ^ gap) for i in range(space)])]
    ppermute x0 -> x4, starting transfers between devices: none -> 8.14 us  [local(): other = lax.ppermute(mine, 'space', [(i, i ^ gap) for i in range(space)])]
    all_to_all x1, starting transfers between devices: 6.39 us -> 8 us  [local(): done = lax.all_to_all(joined, 'dp', 0, 0)]
    pallas_call x13 -> x15, Pallas kernels: 22.2 us -> 22.2 us  [_call(): pl.pallas_call(kernel, out_shape=out, scratch_shapes=scratch, compiler_pa...]
  transfers between devices with their start and end apart: 9 -> 13, of which waited for: 6 -> 10; matrix products, arithmetic and copies ran while one was open for 0% -> 0% of each run, Pallas kernels for 10% -> 10%
where the time goes in v2:
time: 116 us; the launch traced here: 115 us
  starting transfers between devices  37.3 us (32%)
  waiting for transfers between devices  28.7 us (25%)
  blocking collectives  23.8 us (21%)
  Pallas kernels  22.2 us (19%)
  local copies, waits for them, and re-layouts  2.02 us (2%)
    all_to_all x1, blocking collectives, local(): met = lax.all_to_all(parts, 'dp', 0, 0)  23.8 us
    pallas_call x15, Pallas kernels, _call(): pl.pallas_call(kernel, out_shape=out, scratch_shapes=scratch, compiler_pa...  22.2 us
    ppermute x4, waiting for transfers between devices, local(): other = lax.ppermute(mine, 'space', [(i, i ^ gap) for i in range(space)])  8.84 us
    ppermute x4, starting transfers between devices, local(): other = lax.ppermute(mine, 'space', [(i, i ^ gap) for i in range(space)])  8.14 us
    all_to_all x1, starting transfers between devices, local(): done = lax.all_to_all(joined, 'dp', 0, 0)  8 us
    ppermute x1, waiting for transfers between devices, local(): pool_right = lax.ppermute(pooled, 'space', down)  4.55 us
    ppermute x1, starting transfers between devices, local(): from_left = lax.ppermute(x1, 'space', up)  4.38 us
    ppermute x1, starting transfers between devices, local(): gp_from_left = lax.ppermute(gp_right, 'space', up)  4.3 us
  transfers between devices with their start and end apart: 13, of which 10 were waited for; matrix products, arithmetic and copies ran while one was open for 0% of the time, Pallas kernels for 10%

profile of v2, /device:TPU:1, one launch (start us, length us, event | category | flops | bytes accessed | tf_op | source)
XLA Modules:
  0.0 114.9 jit_solution(2583175867750612560)
XLA Ops:
  0.6 1.1 slice_bitcast_fusion
  1.7 4.4 %collective-permute-start = (bf16[64,2048]{1,0:T(8,128)(2,1)S(1)}, bf16[64,2048]{1,0:T(8,128)(2,1)S(1)}, u32[]{:S(2)}, u32[]{:S(2)}) collective-permute-start(bf16[64,2048]{1,0:T(8,128)(2,1)S(1)} %get-tuple-element.58.x1_ref), channel_id=1, source_target_pairs={{0,1},{1,2},{2,3},{3,4},{4,5},{5,6},{6,7},{7,8},{8,9},{9,10},{10,1... | collective-permute-start | bytes 786440 | tf_op jit(solution)/shard_map/ppermute | solution.py:379
  6.1 1.3 %collective-permute-start.1 = (bf16[64,2048]{1,0:T(8,128)(2,1)S(1)}, bf16[64,2048]{1,0:T(8,128)(2,1)S(1)}, u32[]{:S(2)}, u32[]{:S(2)}) collective-permute-start(bf16[64,2048]{1,0:T(8,128)(2,1)S(1)} %get-tuple-element.57.x0_ref), channel_id=1, source_target_pairs={{1,0},{2,1},{3,2},{4,3},{5,4},{6,5},{7,6},{8,7},{9,8},{10,9},{11,1... | collective-permute-start | bytes 786440 | tf_op jit(solution)/shard_map/ppermute | solution.py:380
  7.4 0.0 copy-start.4
  7.4 0.9 copy-done.4
  8.3 2.6 %shard_map.101 = (f32[2,16,64,256]{3,2,1,0:T(8,128)S(1)}, bf16[2,3,17,64,128]{4,3,2,1,0:T(8,128)(2,1)S(1)}, bf16[2304,256]{1,0:T(8,128)(2,1)S(1)}) custom-call(bf16[64,2048]{1,0:T(8,128)(2,1)S(1)} %get-tuple-element.57.x0_ref, bf16[64,2048]{1,0:T(8,128)(2,1)S(1)} %get-tuple-element.58.x1_ref, bf16[9,96,64]{2,1,0:T(8,128)(2,1)S(1)} %bitcast.18), custom_call_target="tpu_custom_call" | custom-call | flops 1610612736 | bytes 8388608 | tf_op jit(solution)/shard_map/pallas_call | solution.py:356
  10.9 0.2 collective-permute-done.left_ref
  11.0 4.2 %collective-permute-done.1.right_ref = bf16[64,2048]{1,0:T(8,128)(2,1)S(1)} collective-permute-done((bf16[64,2048]{1,0:T(8,128)(2,1)S(1)}, bf16[64,2048]{1,0:T(8,128)(2,1)S(1)}, u32[]{:S(2)}, u32[]{:S(2)}) %collective-permute-start.1) | collective-permute-done | bytes 262176 | tf_op jit(solution)/shard_map/ppermute | solution.py:380
  15.2 0.0 copy-done.1
  15.2 2.9 %shard_map.102 = (f32[2,16,64,256]{3,2,1,0:T(8,128)S(1)}, bf16[16,32,128]{2,1,0:T(8,128)(2,1)S(1)}, bf16[2,3,17,64,128]{4,3,2,1,0:T(8,128)(2,1)S(1)}) custom-call(bf16[64,2048]{1,0:T(8,128)(2,1)S(1)} %collective-permute-done.left_ref, bf16[64,2048]{1,0:T(8,128)(2,1)S(1)} %collective-permute-done.1.right_ref, ...), custom_call_target="tpu_custom_call" | custom-call | flops 805306368 | bytes 8388608 | tf_op jit(solution)/shard_map/pallas_call | solution.py:356
  18.1 0.0 copy-start
  18.1 3.7 %collective-permute-start.2 = (bf16[16,32,128]{2,1,0:T(8,128)(2,1)S(1)}, bf16[16,32,128]{2,1,0:T(8,128)(2,1)S(1)}, u32[]{:S(2)}, u32[]{:S(2)}) collective-permute-start(bf16[16,32,128]{2,1,0:T(8,128)(2,1)S(1)} %get-tuple-element.33.own_ref), channel_id=1, source_target_pairs={{0,1},{1,2},{2,3},{3,4},{4,5},{5,6},{6,7},{7,8},{8,9},{9,10},{10,1... | collective-permute-start | bytes 393224 | tf_op jit(solution)/shard_map/ppermute | solution.py:412
  21.8 1.3 %collective-permute-start.3 = (bf16[16,32,128]{2,1,0:T(8,128)(2,1)S(1)}, bf16[16,32,128]{2,1,0:T(8,128)(2,1)S(1)}, u32[]{:S(2)}, u32[]{:S(2)}) collective-permute-start(bf16[16,32,128]{2,1,0:T(8,128)(2,1)S(1)} %get-tuple-element.33.own_ref), channel_id=1, source_target_pairs={{1,0},{2,1},{3,2},{4,3},{5,4},{6,5},{7,6},{8,7},{9,8},{10,9},{11,1... | collective-permute-start | bytes 393224 | tf_op jit(solution)/shard_map/ppermute | solution.py:413
  23.1 0.0 copy-done.3
  23.1 0.9 shard_map.103
  24.0 0.0 copy-done.2
  24.0 0.4 shard_map.104
  24.5 0.0 collective-permute-done.2.left_ref
  24.5 4.5 %collective-permute-done.3.right_ref = bf16[16,32,128]{2,1,0:T(8,128)(2,1)S(1)} collective-permute-done((bf16[16,32,128]{2,1,0:T(8,128)(2,1)S(1)}, bf16[16,32,128]{2,1,0:T(8,128)(2,1)S(1)}, u32[]{:S(2)}, u32[]{:S(2)}) %collective-permute-start.3) | collective-permute-done | bytes 131104 | tf_op jit(solution)/shard_map/ppermute | solution.py:413
  29.0 0.0 copy-done
  29.0 2.3 %shard_map.105 = (bf16[512,256]{1,0:T(8,128)(2,1)S(1)}, bf16[2,3,17,32,128]{4,3,2,1,0:T(8,128)(2,1)S(1)}, bf16[3,34,32,128]{3,2,1,0:T(8,128)(2,1)S(1)}, bf16[16,...) custom-call(bf16[16,32,128]{2,1,0:T(8,128)(2,1)S(1)} %collective-permute-done.2.left_ref, ...), custom_call_target="tpu_custom_call" | custom-call | flops 805306368 | bytes 4194304 | tf_op jit(solution)/shard_map/pallas_call | solution.py:356
  31.3 4.3 %collective-permute-start.4 = (bf16[16,32,128]{2,1,0:T(8,128)(2,1)S(1)}, bf16[16,32,128]{2,1,0:T(8,128)(2,1)S(1)}, u32[]{:S(2)}, u32[]{:S(2)}) collective-permute-start(bf16[16,32,128]{2,1,0:T(8,128)(2,1)S(1)} %get-tuple-element.42), channel_id=1, source_target_pairs={{0,1},{1,2},{2,3},{3,4},{4,5},{5,6},{6,7},{7,8},{8,9},{9,10},{10,1... | collective-permute-start | bytes 393224 | tf_op jit(solution)/shard_map/ppermute | solution.py:439
  35.6 1.3 %collective-permute-start.5 = (bf16[16,32,128]{2,1,0:T(8,128)(2,1)S(1)}, bf16[16,32,128]{2,1,0:T(8,128)(2,1)S(1)}, u32[]{:S(2)}, u32[]{:S(2)}) collective-permute-start(bf16[16,32,128]{2,1,0:T(8,128)(2,1)S(1)} %get-tuple-element.43), channel_id=1, source_target_pairs={{1,0},{2,1},{3,2},{4,3},{5,4},{6,5},{7,6},{8,7},{9,8},{10,9},{11,1... | collective-permute-start | bytes 393224 | tf_op jit(solution)/shard_map/ppermute | solution.py:438
  36.9 1.4 %shard_map.106 = (f32[16,32,128]{2,1,0:T(8,128)S(1)}, bf16[1792,128]{1,0:T(8,128)(2,1)S(1)}) custom-call(bf16[512,256]{1,0:T(8,128)(2,1)S(1)} %get-tuple-element.37.delta_ref, bf16[3,17,32,128]{3,2,1,0:T(8,128)(2,1)S(1)} %get-tuple-element.38.own_ref, bf16[2,3,17,32,128]{4,3,2,1,0:T(8,128)(2,1)S(1)} %get-tuple-element.39.halo_ref, ...), custom_call_target="tpu_custom_call" | custom-call | flops 805306368 | bytes 2097152 | tf_op jit(solution)/shard_map/pallas_call | solution.py:356
  38.4 0.0 collective-permute-done.4.fl_ref
  38.4 3.0 %collective-permute-done.5.fr_ref = bf16[16,32,128]{2,1,0:T(8,128)(2,1)S(1)} collective-permute-done((bf16[16,32,128]{2,1,0:T(8,128)(2,1)S(1)}, bf16[16,32,128]{2,1,0:T(8,128)(2,1)S(1)}, u32[]{:S(2)}, u32[]{:S(2)}) %collective-permute-start.5) | collective-permute-done | bytes 131104 | tf_op jit(solution)/shard_map/ppermute | solution.py:438
  41.4 3.5 %shard_map.107 = (bf16[2,16,64,256]{3,2,1,0:T(8,128)(2,1)S(1)}, bf16[16,144,128]{2,1,0:T(8,128)(2,1)S(1)}) custom-call(f32[16,32,128]{2,1,0:T(8,128)S(1)} %get-tuple-element.41.gm_ref, bf16[16,32,128]{2,1,0:T(8,128)(2,1)S(1)} %collective-permute-done.4.fl_ref, bf16[16,32,128]{2,1,0:T(8,128)(2,1)S(1)} %collective-permute-done.5.fr_ref, ...), custom_call_target="tpu_custom_call" | custom-call | flops 2415919104 | bytes 4194304 | tf_op jit(solution)/shard_map/pallas_call | solution.py:356
  44.9 23.8 %all_to_all.10.in_ref = bf16[16,144,128]{2,1,0:T(8,128)(2,1)S(1)} all-to-all(bf16[16,144,128]{2,1,0:T(8,128)(2,1)S(1)} %get-tuple-element.52), channel_id=1, replica_groups=mesh['dp'=16,'space'=16] {'dp'}, dimensions={0} | all-to-all | bytes 1179648 | tf_op jit(solution)/shard_map/all_to_all | solution.py:465
  68.7 0.1 shard_map.110.a_ref
  68.8 0.5 collective-permute-start.8
  69.3 2.4 %collective-permute-done.8.b_ref = bf16[144,128]{1,0:T(8,128)(2,1)S(1)} collective-permute-done((bf16[144,128]{1,0:T(8,128)(2,1)S(1)}, bf16[144,128]{1,0:T(8,128)(2,1)S(1)}, u32[]{:S(2)}, u32[]{:S(2)}) %collective-permute-start.8) | collective-permute-done | bytes 36896 | tf_op jit(solution)/shard_map/ppermute | solution.py:495
  71.7 1.8 %collective-permute-start.9 = (bf16[144,128]{1,0:T(8,128)(2,1)S(1)}, bf16[144,128]{1,0:T(8,128)(2,1)S(1)}, u32[]{:S(2)}, u32[]{:S(2)}) collective-permute-start(bf16[144,128]{1,0:T(8,128)(2,1)S(1)} %shard_map.111.a_ref), channel_id=1, source_target_pairs={{0,1},{1,0},{2,3},{3,2},{4,5},{5,4},{6,7},{7,6},{8,9},{9,8},{10,11... | collective-permute-start | bytes 110600 | tf_op jit(solution)/shard_map/ppermute | solution.py:495
  73.5 1.3 %collective-permute-done.9.b_ref = bf16[144,128]{1,0:T(8,128)(2,1)S(1)} collective-permute-done((bf16[144,128]{1,0:T(8,128)(2,1)S(1)}, bf16[144,128]{1,0:T(8,128)(2,1)S(1)}, u32[]{:S(2)}, u32[]{:S(2)}) %collective-permute-start.9) | collective-permute-done | bytes 36896 | tf_op jit(solution)/shard_map/ppermute | solution.py:495
  74.9 2.2 %collective-permute-start.10 = (bf16[144,128]{1,0:T(8,128)(2,1)S(1)}, bf16[144,128]{1,0:T(8,128)(2,1)S(1)}, u32[]{:S(2)}, u32[]{:S(2)}) collective-permute-start(bf16[144,128]{1,0:T(8,128)(2,1)S(1)} %shard_map.112.a_ref), channel_id=1, source_target_pairs={{0,2},{1,3},{2,0},{3,1},{4,6},{5,7},{6,4},{7,5},{8,10},{9,11},{10,... | collective-permute-start | bytes 110600 | tf_op jit(solution)/shard_map/ppermute | solution.py:495
  77.1 1.6 %collective-permute-done.10.b_ref = bf16[144,128]{1,0:T(8,128)(2,1)S(1)} collective-permute-done((bf16[144,128]{1,0:T(8,128)(2,1)S(1)}, bf16[144,128]{1,0:T(8,128)(2,1)S(1)}, u32[]{:S(2)}, u32[]{:S(2)}) %collective-permute-start.10) | collective-permute-done | bytes 36896 | tf_op jit(solution)/shard_map/ppermute | solution.py:495
  78.7 3.6 %collective-permute-start.11 = (bf16[144,128]{1,0:T(8,128)(2,1)S(1)}, bf16[144,128]{1,0:T(8,128)(2,1)S(1)}, u32[]{:S(2)}, u32[]{:S(2)}) collective-permute-start(bf16[144,128]{1,0:T(8,128)(2,1)S(1)} %shard_map.113.a_ref), channel_id=1, source_target_pairs={{0,4},{1,5},{2,6},{3,7},{4,0},{5,1},{6,2},{7,3},{8,12},{9,13},{10,... | collective-permute-start | bytes 110600 | tf_op jit(solution)/shard_map/ppermute | solution.py:495
  82.3 3.5 %collective-permute-done.11.b_ref = bf16[144,128]{1,0:T(8,128)(2,1)S(1)} collective-permute-done((bf16[144,128]{1,0:T(8,128)(2,1)S(1)}, bf16[144,128]{1,0:T(8,128)(2,1)S(1)}, u32[]{:S(2)}, u32[]{:S(2)}) %collective-permute-start.11) | collective-permute-done | bytes 36896 | tf_op jit(solution)/shard_map/ppermute | solution.py:495
  85.8 0.9 shard_map.114
  86.7 8.0 %all-to-all-start.1 = ((bf16[16,144,128]{2,1,0:T(8,128)(2,1)}), bf16[16,144,128]{2,1,0:T(8,128)(2,1)S(1)}, u32[]{:S(2)}, u32[]{:S(2)}) async-start(bf16[16,144,128]{2,1,0:T(8,128)(2,1)} %shard_map.114), calls=%async_computation.1 | async-start | bytes 1179648 | tf_op jit(solution)/shard_map/all_to_all | solution.py:499
  94.7 0.0 copy-done.5
  94.7 5.2 %shard_map.108 = (bf16[8,64,256]{2,1,0:T(8,128)(2,1)S(1)}, bf16[2,8,64,256]{3,2,1,0:T(8,128)(2,1)S(1)}, bf16[8,64,256]{2,1,0:T(8,128)(2,1)S(1)}) custom-call(bf16[2,16,64,256]{3,2,1,0:T(8,128)(2,1)S(1)} %get-tuple-element.48.delta_ref, bf16[9,96,64]{2,1,0:T(8,128)(2,1)S(1)} %bitcast.19), custom_call_target="tpu_custom_call" | custom-call | flops 1207959552 | bytes 8388608 | tf_op jit(solution)/shard_map/pallas_call | solution.py:356
  99.9 3.6 %collective-permute-start.6 = (bf16[8,64,256]{2,1,0:T(8,128)(2,1)S(1)}, bf16[8,64,256]{2,1,0:T(8,128)(2,1)S(1)}, u32[]{:S(2)}, u32[]{:S(2)}) collective-permute-start(bf16[8,64,256]{2,1,0:T(8,128)(2,1)S(1)} %get-tuple-element.50), channel_id=1, source_target_pairs={{0,1},{1,2},{2,3},{3,4},{4,5},{5,6},{6,7},{7,8},{8,9},{9,10},{10,1... | collective-permute-start | bytes 786440 | tf_op jit(solution)/shard_map/ppermute | solution.py:481
  103.6 1.3 %collective-permute-start.7 = (bf16[8,64,256]{2,1,0:T(8,128)(2,1)S(1)}, bf16[8,64,256]{2,1,0:T(8,128)(2,1)S(1)}, u32[]{:S(2)}, u32[]{:S(2)}) collective-permute-start(bf16[8,64,256]{2,1,0:T(8,128)(2,1)S(1)} %get-tuple-element.51), channel_id=1, source_target_pairs={{1,0},{2,1},{3,2},{4,3},{5,4},{6,5},{7,6},{8,7},{9,8},{10,9},{11,1... | collective-permute-start | bytes 786440 | tf_op jit(solution)/shard_map/ppermute | solution.py:480
  104.9 4.1 %collective-permute-done.6.fl_ref = bf16[8,64,256]{2,1,0:T(8,128)(2,1)S(1)} collective-permute-done((bf16[8,64,256]{2,1,0:T(8,128)(2,1)S(1)}, bf16[8,64,256]{2,1,0:T(8,128)(2,1)S(1)}, u32[]{:S(2)}, u32[]{:S(2)}) %collective-permute-start.6) | collective-permute-done | bytes 262176 | tf_op jit(solution)/shard_map/ppermute | solution.py:481
  109.0 3.8 %collective-permute-done.7.fr_ref = bf16[8,64,256]{2,1,0:T(8,128)(2,1)S(1)} collective-permute-done((bf16[8,64,256]{2,1,0:T(8,128)(2,1)S(1)}, bf16[8,64,256]{2,1,0:T(8,128)(2,1)S(1)}, u32[]{:S(2)}, u32[]{:S(2)}) %collective-permute-start.7) | collective-permute-done | bytes 262176 | tf_op jit(solution)/shard_map/ppermute | solution.py:480
  112.8 0.9 shard_map.109
  113.8 0.0 all-to-all-done.1.in_ref
  113.8 1.1 shard_map.115
  (7 shorter events, 0.0 us)
Async XLA Ops:
  1.7 9.3 %collective-permute-start = (bf16[64,2048]{1,0:T(8,128)(2,1)S(1)}, bf16[64,2048]{1,0:T(8,128)(2,1)S(1)}, u32[]{:S(2)}, u32[]{:S(2)}) collective-permute-start(bf16[64,2048]{1,0:T(8,128)(2,1)S(1)} %get-tuple-element.58.x1_ref), channel_id=1, source_target_pairs={{0,1},{1,2},{2,3},{3,4},{4,5},{5,6},{6,7},{7,8},{8,9},{9,10},{10,1... | collective-permute-start | bytes 786440 | tf_op jit(solution)/shard_map/ppermute | solution.py:379
  6.1 9.1 %collective-permute-start.1 = (bf16[64,2048]{1,0:T(8,128)(2,1)S(1)}, bf16[64,2048]{1,0:T(8,128)(2,1)S(1)}, u32[]{:S(2)}, u32[]{:S(2)}) collective-permute-start(bf16[64,2048]{1,0:T(8,128)(2,1)S(1)} %get-tuple-element.57.x0_ref), channel_id=1, source_target_pairs={{1,0},{2,1},{3,2},{4,3},{5,4},{6,5},{7,6},{8,7},{9,8},{10,9},{11,1... | collective-permute-start | bytes 786440 | tf_op jit(solution)/shard_map/ppermute | solution.py:380
  7.4 0.9 copy-start.4
  8.3 6.9 %copy-start.1 = (f32[64]{0:T(128)S(1)}, f32[64]{0:T(128)}, u32[]{:S(2)}) copy-start(f32[64]{0:T(128)} %param.8) | copy-start | bytes 772
  15.2 7.9 %copy-start.3 = (bf16[3,3,3,64,128]{4,3,2,1,0:T(8,128)(2,1)S(1)}, bf16[3,3,3,64,128]{4,3,2,1,0:T(8,128)(2,1)}, u32[]{:S(2)}) copy-start(bf16[3,3,3,64,128]{4,3,2,1,0:T(8,128)(2,1)} %param.9) | copy-start | bytes 1327108
  15.2 8.8 %copy-start.2 = (f32[128]{0:T(128)S(1)}, f32[128]{0:T(128)}, u32[]{:S(2)}) copy-start(f32[128]{0:T(128)} %param.10) | copy-start | bytes 1540
  18.1 10.9 %copy-start = (bf16[1,1,32,4096]{3,2,1,0:T(8,128)(2,1)S(1)}, bf16[1,1,32,4096]{3,2,1,0:T(8,128)(2,1)}, u32[]{:S(2)}) copy-start(bf16[1,1,32,4096]{3,2,1,0:T(8,128)(2,1)} %param.11) | copy-start | bytes 786436
  18.1 6.3 %collective-permute-start.2 = (bf16[16,32,128]{2,1,0:T(8,128)(2,1)S(1)}, bf16[16,32,128]{2,1,0:T(8,128)(2,1)S(1)}, u32[]{:S(2)}, u32[]{:S(2)}) collective-permute-start(bf16[16,32,128]{2,1,0:T(8,128)(2,1)S(1)} %get-tuple-element.33.own_ref), channel_id=1, source_target_pairs={{0,1},{1,2},{2,3},{3,4},{4,5},{5,6},{6,7},{7,8},{8,9},{9,10},{10,1... | collective-permute-start | bytes 393224 | tf_op jit(solution)/shard_map/ppermute | solution.py:412
  21.8 7.2 %collective-permute-start.3 = (bf16[16,32,128]{2,1,0:T(8,128)(2,1)S(1)}, bf16[16,32,128]{2,1,0:T(8,128)(2,1)S(1)}, u32[]{:S(2)}, u32[]{:S(2)}) collective-permute-start(bf16[16,32,128]{2,1,0:T(8,128)(2,1)S(1)} %get-tuple-element.33.own_ref), channel_id=1, source_target_pairs={{1,0},{2,1},{3,2},{4,3},{5,4},{6,5},{7,6},{8,7},{9,8},{10,9},{11,1... | collective-permute-start | bytes 393224 | tf_op jit(solution)/shard_map/ppermute | solution.py:413
  31.3 7.0 %collective-permute-start.4 = (bf16[16,32,128]{2,1,0:T(8,128)(2,1)S(1)}, bf16[16,32,128]{2,1,0:T(8,128)(2,1)S(1)}, u32[]{:S(2)}, u32[]{:S(2)}) collective-permute-start(bf16[16,32,128]{2,1,0:T(8,128)(2,1)S(1)} %get-tuple-element.42), channel_id=1, source_target_pairs={{0,1},{1,2},{2,3},{3,4},{4,5},{5,6},{6,7},{7,8},{8,9},{9,10},{10,1... | collective-permute-start | bytes 393224 | tf_op jit(solution)/shard_map/ppermute | solution.py:439
  35.6 5.7 %collective-permute-start.5 = (bf16[16,32,128]{2,1,0:T(8,128)(2,1)S(1)}, bf16[16,32,128]{2,1,0:T(8,128)(2,1)S(1)}, u32[]{:S(2)}, u32[]{:S(2)}) collective-permute-start(bf16[16,32,128]{2,1,0:T(8,128)(2,1)S(1)} %get-tuple-element.43), channel_id=1, source_target_pairs={{1,0},{2,1},{3,2},{4,3},{5,4},{6,5},{7,6},{8,7},{9,8},{10,9},{11,1... | collective-permute-start | bytes 393224 | tf_op jit(solution)/shard_map/ppermute | solution.py:438
  68.7 26.0 %copy-start.5 = (bf16[3,3,3,32,64]{4,3,2,1,0:T(8,128)(2,1)S(1)}, bf16[3,3,3,32,64]{4,3,2,1,0:T(8,128)(2,1)}, u32[]{:S(2)}) copy-start(bf16[3,3,3,32,64]{4,3,2,1,0:T(8,128)(2,1)} %param.7) | copy-start | bytes 331780
  68.8 2.9 %collective-permute-start.8 = (bf16[144,128]{1,0:T(8,128)(2,1)S(1)}, bf16[144,128]{1,0:T(8,128)(2,1)S(1)}, u32[]{:S(2)}, u32[]{:S(2)}) collective-permute-start(bf16[144,128]{1,0:T(8,128)(2,1)S(1)} %shard_map.110.a_ref), channel_id=1, source_target_pairs={{0,8},{1,9},{2,10},{3,11},{4,12},{5,13},{6,14},{7,15},{8,0},{9,1},... | collective-permute-start | bytes 110600 | tf_op jit(solution)/shard_map/ppermute | solution.py:495
  71.7 3.2 %collective-permute-start.9 = (bf16[144,128]{1,0:T(8,128)(2,1)S(1)}, bf16[144,128]{1,0:T(8,128)(2,1)S(1)}, u32[]{:S(2)}, u32[]{:S(2)}) collective-permute-start(bf16[144,128]{1,0:T(8,128)(2,1)S(1)} %shard_map.111.a_ref), channel_id=1, source_target_pairs={{0,1},{1,0},{2,3},{3,2},{4,5},{5,4},{6,7},{7,6},{8,9},{9,8},{10,11... | collective-permute-start | bytes 110600 | tf_op jit(solution)/shard_map/ppermute | solution.py:495
  74.9 3.8 %collective-permute-start.10 = (bf16[144,128]{1,0:T(8,128)(2,1)S(1)}, bf16[144,128]{1,0:T(8,128)(2,1)S(1)}, u32[]{:S(2)}, u32[]{:S(2)}) collective-permute-start(bf16[144,128]{1,0:T(8,128)(2,1)S(1)} %shard_map.112.a_ref), channel_id=1, source_target_pairs={{0,2},{1,3},{2,0},{3,1},{4,6},{5,7},{6,4},{7,5},{8,10},{9,11},{10,... | collective-permute-start | bytes 110600 | tf_op jit(solution)/shard_map/ppermute | solution.py:495
  78.7 7.1 %collective-permute-start.11 = (bf16[144,128]{1,0:T(8,128)(2,1)S(1)}, bf16[144,128]{1,0:T(8,128)(2,1)S(1)}, u32[]{:S(2)}, u32[]{:S(2)}) collective-permute-start(bf16[144,128]{1,0:T(8,128)(2,1)S(1)} %shard_map.113.a_ref), channel_id=1, source_target_pairs={{0,4},{1,5},{2,6},{3,7},{4,0},{5,1},{6,2},{7,3},{8,12},{9,13},{10,... | collective-permute-start | bytes 110600 | tf_op jit(solution)/shard_map/ppermute | solution.py:495
  86.7 27.1 %all-to-all-start.1 = ((bf16[16,144,128]{2,1,0:T(8,128)(2,1)}), bf16[16,144,128]{2,1,0:T(8,128)(2,1)S(1)}, u32[]{:S(2)}, u32[]{:S(2)}) async-start(bf16[16,144,128]{2,1,0:T(8,128)(2,1)} %shard_map.114), calls=%async_computation.1 | async-start | bytes 1179648 | tf_op jit(solution)/shard_map/all_to_all | solution.py:499
  99.9 9.1 %collective-permute-start.6 = (bf16[8,64,256]{2,1,0:T(8,128)(2,1)S(1)}, bf16[8,64,256]{2,1,0:T(8,128)(2,1)S(1)}, u32[]{:S(2)}, u32[]{:S(2)}) collective-permute-start(bf16[8,64,256]{2,1,0:T(8,128)(2,1)S(1)} %get-tuple-element.50), channel_id=1, source_target_pairs={{0,1},{1,2},{2,3},{3,4},{4,5},{5,6},{6,7},{7,8},{8,9},{9,10},{10,1... | collective-permute-start | bytes 786440 | tf_op jit(solution)/shard_map/ppermute | solution.py:481
  103.6 9.3 %collective-permute-start.7 = (bf16[8,64,256]{2,1,0:T(8,128)(2,1)S(1)}, bf16[8,64,256]{2,1,0:T(8,128)(2,1)S(1)}, u32[]{:S(2)}, u32[]{:S(2)}) collective-permute-start(bf16[8,64,256]{2,1,0:T(8,128)(2,1)S(1)} %get-tuple-element.51), channel_id=1, source_target_pairs={{1,0},{2,1},{3,2},{4,3},{5,4},{6,5},{7,6},{8,7},{9,8},{10,9},{11,1... | collective-permute-start | bytes 786440 | tf_op jit(solution)/shard_map/ppermute | solution.py:480

commit v3 on v2

--- a/solution.py
+++ b/solution.py
@@ -314,16 +314,15 @@
 
 def _split_kernel(scale_two, scale_one, rows_two, in_ref, out_ref):
     whole = jnp.sum(in_ref[...].astype(F32), axis=0)
-    out_ref[0:rows_two, :] = (whole[0:rows_two] * scale_two).astype(BF16)
-    out_ref[rows_two:, :] = (whole[rows_two:] * scale_one).astype(BF16)
-
-
-def _add_kernel(a_ref, b_ref, out_ref):
-    out_ref[...] = (a_ref[...].astype(F32) + b_ref[...].astype(F32)).astype(BF16)
-
-
-def _join_kernel(a_ref, b_ref, out_ref):
-    whole = (a_ref[...].astype(F32) + b_ref[...].astype(F32)).astype(BF16)
+    a = (whole[0:rows_two] * scale_two).astype(BF16)
+    b = (whole[rows_two:] * scale_one).astype(BF16)
+    for i in range(out_ref.shape[0]):
+        out_ref[i, 0:rows_two, :] = a
+        out_ref[i, rows_two:, :] = b
+
+
+def _join_kernel(in_ref, out_ref):
+    whole = jnp.sum(in_ref[...].astype(F32), axis=0).astype(BF16)
     for i in range(out_ref.shape[0]):
         out_ref[i] = whole
 
@@ -336,7 +335,7 @@
         if take:
             w_two_ref[at : at + take, :] = in_ref[i, 0:take, :].astype(F32)
         if at <= two < at + rows_two:
-            b_two_ref[...] = in_ref[i, two - at : two - at + 16, :].astype(F32)[0:1]
+            b_two_ref[...] = in_ref[i, two - at : two - at + 8, :].astype(F32)[0:1]
         at = i * rows_one
         take = min(rows_one, max(one - at, 0))
         if take:
@@ -345,7 +344,7 @@
             w_one_ref[one + at : one + at + take, :] = block[:, 64:128]
         if at <= one < at + rows_one:
             spot = rows_two + one - at
-            b_one_ref[...] = in_ref[i, spot : spot + 16, :].astype(F32)[0:1, 0:64]
+            b_one_ref[...] = in_ref[i, spot : spot + 8, :].astype(F32)[0:1, 0:64]
 
 
 def _shape(shape, dtype):
@@ -437,8 +436,12 @@
     )
     gp_from_right = lax.ppermute(gp_left, "space", down)
     gp_from_left = lax.ppermute(gp_right, "space", up)
-    rows_two = _round_up(1744, 16 * dp)
-    rows_one = _round_up(448, 16 * dp)
+    runs = space // 2
+    peers = 2 * dp
+    planes = [[d * space + r * runs + z for d in range(dp) for r in range(2)] for z in range(runs)]
+    lines = [[r * runs + z for z in range(runs)] for r in range(2)]
+    rows_two = _round_up(1744, 8 * peers)
+    rows_one = _round_up(448, 8 * peers)
     gp_own, part_two = _call(
         _own_two_kernel,
         (_shape((groups, half, LANES), F32), _shape((rows_two, LANES), BF16)),
@@ -448,10 +451,10 @@
         16,
         (delta_two, ps_own, ps_halo, ds_two, back_two),
     )
-    rows_all = (rows_two + rows_one) // dp
+    rows_all = (rows_two + rows_one) // peers
     delta_one, parts = _call(
         _grad_one_kernel,
-        (_shape((2, groups, side, 256), BF16), _shape((dp, rows_all, LANES), BF16)),
+        (_shape((2, groups, side, 256), BF16), _shape((peers, rows_all, LANES), BF16)),
         [pltpu.VMEM((8, 256), F32)]
         + [pltpu.VMEM((2, side, LANES), F32)] * 2
         + [pltpu.VMEM((256, 2 * groups * side), BF16), pltpu.VMEM((rows_one, LANES), BF16)],
@@ -460,9 +463,9 @@
         16,
         (gp_own, gp_from_left, gp_from_right, slope, xs_own, xs_halo, part_two),
     )
-    rows_two //= dp
-    rows_one //= dp
-    met = lax.all_to_all(parts, "dp", 0, 0)
+    rows_two //= peers
+    rows_one //= peers
+    met = lax.all_to_all(parts, ("dp", "space"), 0, 0, axis_index_groups=planes)
     block = _shape((groups // 2, side, 256), BF16)
     gx_left, gx_own, gx_right = _call(
         _input_kernel,
@@ -488,15 +491,18 @@
         12,
         (gx_own, gx_from_left, gx_from_right),
     )
-    flat = _shape((rows_all, LANES), BF16)
-    mine = _call(functools.partial(_split_kernel, scale_two, scale_one, rows_two), flat, [], 0, MIB, 8, (met,))
-    far = [space // 2] + [2**k for k in range(space.bit_length() - 2)]
-    for k, gap in enumerate(far):
-        other = lax.ppermute(mine, "space", [(i, i ^ gap) for i in range(space)])
-        if k < len(far) - 1:
-            mine = _call(_add_kernel, flat, [], 0, MIB, 8, (mine, other))
-    joined = _call(_join_kernel, _shape((dp, rows_all, LANES), BF16), [], 0, MIB, 8, (mine, other))
-    done = lax.all_to_all(joined, "dp", 0, 0)
+    mine = _call(
+        functools.partial(_split_kernel, scale_two, scale_one, rows_two),
+        _shape((runs, rows_all, LANES), BF16),
+        [],
+        0,
+        MIB,
+        8,
+        (met,),
+    )
+    met = lax.all_to_all(mine, "space", 0, 0, axis_index_groups=lines)
+    joined = _call(_join_kernel, _shape((peers, rows_all, LANES), BF16), [], 0, MIB, 8, (met,))
+    done = lax.all_to_all(joined, ("dp", "space"), 0, 0, axis_index_groups=planes)
     gw_two, gb_two, gw_one, gb_one = _call(
         functools.partial(_unpack_kernel, rows_two, rows_one),
         (

time: 116 us -> 109 us (0.940)
  blocking collectives: 23.8 us -> 35.6 us
  starting transfers between devices: 37.3 us -> 26.7 us
  waiting for transfers between devices: 28.7 us -> 19.7 us
    all_to_all x1 -> x2, blocking collectives: 23.8 us -> 35.6 us  [the longest x1 22.3 us: local(): met = lax.all_to_all(parts, ('dp', 'space'), 0, 0, axis_index_groups=planes)]
    ppermute x4 -> x0, waiting for transfers between devices: 8.84 us -> none  [local(): other = lax.ppermute(mine, 'space', [(i, i ^ gap) for i in range(space)])]
    ppermute x4 -> x0, starting transfers between devices: 8.14 us -> none  [local(): other = lax.ppermute(mine, 'space', [(i, i ^ gap) for i in range(space)])]
    ppermute x1, starting transfers between devices: 3.65 us -> 2.2 us  [local(): gx_from_left = lax.ppermute(gx_right, 'space', up)]
    pallas_call x15 -> x12, Pallas kernels: 22.2 us -> 22.2 us  [_call(): pl.pallas_call(kernel, out_shape=out, scratch_shapes=scratch, compiler_pa...]
  transfers between devices with their start and end apart: 13 -> 9, of which waited for: 10 -> 6; matrix products, arithmetic and copies ran while one was open for 0% -> 0% of each run, Pallas kernels for 10% -> 11%
where the time goes in v3:
time: 109 us; the launch traced here: 107 us
  blocking collectives  35.6 us (33%)
  starting transfers between devices  26.7 us (24%)
  Pallas kernels  22.2 us (20%)
  waiting for transfers between devices  19.7 us (18%)
  local copies, waits for them, and re-layouts  2.02 us (2%)
    all_to_all x1, blocking collectives, local(): met = lax.all_to_all(parts, ('dp', 'space'), 0, 0, axis_index_groups=planes)  22.3 us
    pallas_call x12, Pallas kernels, _call(): pl.pallas_call(kernel, out_shape=out, scratch_shapes=scratch, compiler_pa...  22.2 us
    all_to_all x1, blocking collectives, local(): met = lax.all_to_all(mine, 'space', 0, 0, axis_index_groups=lines)  13.4 us
    all_to_all x1, starting transfers between devices, local(): lax.all_to_all(joined, ('dp', 'space'), 0, 0, axis_index_groups=planes)  6.92 us
    ppermute x1, waiting for transfers between devices, local(): pool_right = lax.ppermute(pooled, 'space', down)  4.55 us
    ppermute x1, starting transfers between devices, local(): from_left = lax.ppermute(x1, 'space', up)  4.38 us
    ppermute x1, starting transfers between devices, local(): gp_from_left = lax.ppermute(gp_right, 'space', up)  4.3 us
    ppermute x1, waiting for transfers between devices, local(): from_right = lax.ppermute(x0, 'space', down)  4.19 us
  transfers between devices with their start and end apart: 9, of which 6 were waited for; matrix products, arithmetic and copies ran while one was open for 0% of the time, Pallas kernels for 11%

profile of v3, /device:TPU:1, one launch (start us, length us, event | category | flops | bytes accessed | tf_op | source)
XLA Modules:
  0.0 106.9 jit_solution(152604383399573199)
XLA Ops:
  0.6 1.1 slice_bitcast_fusion
  1.7 4.4 %collective-permute-start = (bf16[64,2048]{1,0:T(8,128)(2,1)S(1)}, bf16[64,2048]{1,0:T(8,128)(2,1)S(1)}, u32[]{:S(2)}, u32[]{:S(2)}) collective-permute-start(bf16[64,2048]{1,0:T(8,128)(2,1)S(1)} %get-tuple-element.58.x1_ref), channel_id=1, source_target_pairs={{0,1},{1,2},{2,3},{3,4},{4,5},{5,6},{6,7},{7,8},{8,9},{9,10},{10,1... | collective-permute-start | bytes 786440 | tf_op jit(solution)/shard_map/ppermute | solution.py:378
  6.1 1.3 %collective-permute-start.1 = (bf16[64,2048]{1,0:T(8,128)(2,1)S(1)}, bf16[64,2048]{1,0:T(8,128)(2,1)S(1)}, u32[]{:S(2)}, u32[]{:S(2)}) collective-permute-start(bf16[64,2048]{1,0:T(8,128)(2,1)S(1)} %get-tuple-element.57.x0_ref), channel_id=1, source_target_pairs={{1,0},{2,1},{3,2},{4,3},{5,4},{6,5},{7,6},{8,7},{9,8},{10,9},{11,1... | collective-permute-start | bytes 786440 | tf_op jit(solution)/shard_map/ppermute | solution.py:379
  7.4 0.0 copy-start.4
  7.4 0.9 copy-done.4
  8.3 0.0 copy-start.1
  8.3 2.6 %shard_map.101 = (f32[2,16,64,256]{3,2,1,0:T(8,128)S(1)}, bf16[2,3,17,64,128]{4,3,2,1,0:T(8,128)(2,1)S(1)}, bf16[2304,256]{1,0:T(8,128)(2,1)S(1)}) custom-call(bf16[64,2048]{1,0:T(8,128)(2,1)S(1)} %get-tuple-element.57.x0_ref, bf16[64,2048]{1,0:T(8,128)(2,1)S(1)} %get-tuple-element.58.x1_ref, bf16[9,96,64]{2,1,0:T(8,128)(2,1)S(1)} %bitcast.18), custom_call_target="tpu_custom_call" | custom-call | flops 1610612736 | bytes 8388608 | tf_op jit(solution)/shard_map/pallas_call | solution.py:355
  10.9 0.2 collective-permute-done.left_ref
  11.0 4.2 %collective-permute-done.1.right_ref = bf16[64,2048]{1,0:T(8,128)(2,1)S(1)} collective-permute-done((bf16[64,2048]{1,0:T(8,128)(2,1)S(1)}, bf16[64,2048]{1,0:T(8,128)(2,1)S(1)}, u32[]{:S(2)}, u32[]{:S(2)}) %collective-permute-start.1) | collective-permute-done | bytes 262176 | tf_op jit(solution)/shard_map/ppermute | solution.py:379
  15.2 0.0 copy-done.1
  15.2 0.0 copy-start.3
  15.2 0.0 copy-start.2
  15.2 2.9 %shard_map.102 = (f32[2,16,64,256]{3,2,1,0:T(8,128)S(1)}, bf16[16,32,128]{2,1,0:T(8,128)(2,1)S(1)}, bf16[2,3,17,64,128]{4,3,2,1,0:T(8,128)(2,1)S(1)}) custom-call(bf16[64,2048]{1,0:T(8,128)(2,1)S(1)} %collective-permute-done.left_ref, bf16[64,2048]{1,0:T(8,128)(2,1)S(1)} %collective-permute-done.1.right_ref, ...), custom_call_target="tpu_custom_call" | custom-call | flops 805306368 | bytes 8388608 | tf_op jit(solution)/shard_map/pallas_call | solution.py:355
  18.1 0.0 copy-start
  18.1 3.7 %collective-permute-start.2 = (bf16[16,32,128]{2,1,0:T(8,128)(2,1)S(1)}, bf16[16,32,128]{2,1,0:T(8,128)(2,1)S(1)}, u32[]{:S(2)}, u32[]{:S(2)}) collective-permute-start(bf16[16,32,128]{2,1,0:T(8,128)(2,1)S(1)} %get-tuple-element.33.own_ref), channel_id=1, source_target_pairs={{0,1},{1,2},{2,3},{3,4},{4,5},{5,6},{6,7},{7,8},{8,9},{9,10},{10,1... | collective-permute-start | bytes 393224 | tf_op jit(solution)/shard_map/ppermute | solution.py:411
  21.8 1.3 %collective-permute-start.3 = (bf16[16,32,128]{2,1,0:T(8,128)(2,1)S(1)}, bf16[16,32,128]{2,1,0:T(8,128)(2,1)S(1)}, u32[]{:S(2)}, u32[]{:S(2)}) collective-permute-start(bf16[16,32,128]{2,1,0:T(8,128)(2,1)S(1)} %get-tuple-element.33.own_ref), channel_id=1, source_target_pairs={{1,0},{2,1},{3,2},{4,3},{5,4},{6,5},{7,6},{8,7},{9,8},{10,9},{11,1... | collective-permute-start | bytes 393224 | tf_op jit(solution)/shard_map/ppermute | solution.py:412
  23.1 0.0 copy-done.3
  23.1 0.9 shard_map.103
  24.0 0.0 copy-done.2
  24.0 0.4 shard_map.104
  24.5 0.0 collective-permute-done.2.left_ref
  24.5 4.5 %collective-permute-done.3.right_ref = bf16[16,32,128]{2,1,0:T(8,128)(2,1)S(1)} collective-permute-done((bf16[16,32,128]{2,1,0:T(8,128)(2,1)S(1)}, bf16[16,32,128]{2,1,0:T(8,128)(2,1)S(1)}, u32[]{:S(2)}, u32[]{:S(2)}) %collective-permute-start.3) | collective-permute-done | bytes 131104 | tf_op jit(solution)/shard_map/ppermute | solution.py:412
  29.0 0.0 copy-done
  29.0 2.3 %shard_map.105 = (bf16[512,256]{1,0:T(8,128)(2,1)S(1)}, bf16[2,3,17,32,128]{4,3,2,1,0:T(8,128)(2,1)S(1)}, bf16[3,34,32,128]{3,2,1,0:T(8,128)(2,1)S(1)}, bf16[16,...) custom-call(bf16[16,32,128]{2,1,0:T(8,128)(2,1)S(1)} %collective-permute-done.2.left_ref, ...), custom_call_target="tpu_custom_call" | custom-call | flops 805306368 | bytes 4194304 | tf_op jit(solution)/shard_map/pallas_call | solution.py:355
  31.3 4.3 %collective-permute-start.4 = (bf16[16,32,128]{2,1,0:T(8,128)(2,1)S(1)}, bf16[16,32,128]{2,1,0:T(8,128)(2,1)S(1)}, u32[]{:S(2)}, u32[]{:S(2)}) collective-permute-start(bf16[16,32,128]{2,1,0:T(8,128)(2,1)S(1)} %get-tuple-element.42), channel_id=1, source_target_pairs={{0,1},{1,2},{2,3},{3,4},{4,5},{5,6},{6,7},{7,8},{8,9},{9,10},{10,1... | collective-permute-start | bytes 393224 | tf_op jit(solution)/shard_map/ppermute | solution.py:438
  35.6 1.3 %collective-permute-start.5 = (bf16[16,32,128]{2,1,0:T(8,128)(2,1)S(1)}, bf16[16,32,128]{2,1,0:T(8,128)(2,1)S(1)}, u32[]{:S(2)}, u32[]{:S(2)}) collective-permute-start(bf16[16,32,128]{2,1,0:T(8,128)(2,1)S(1)} %get-tuple-element.43), channel_id=1, source_target_pairs={{1,0},{2,1},{3,2},{4,3},{5,4},{6,5},{7,6},{8,7},{9,8},{10,9},{11,1... | collective-permute-start | bytes 393224 | tf_op jit(solution)/shard_map/ppermute | solution.py:437
  36.9 1.4 %shard_map.106 = (f32[16,32,128]{2,1,0:T(8,128)S(1)}, bf16[1792,128]{1,0:T(8,128)(2,1)S(1)}) custom-call(bf16[512,256]{1,0:T(8,128)(2,1)S(1)} %get-tuple-element.37.delta_ref, bf16[3,17,32,128]{3,2,1,0:T(8,128)(2,1)S(1)} %get-tuple-element.38.own_ref, bf16[2,3,17,32,128]{4,3,2,1,0:T(8,128)(2,1)S(1)} %get-tuple-element.39.halo_ref, ...), custom_call_target="tpu_custom_call" | custom-call | flops 805306368 | bytes 2097152 | tf_op jit(solution)/shard_map/pallas_call | solution.py:355
  38.4 0.0 collective-permute-done.4.fl_ref
  38.4 3.0 %collective-permute-done.5.fr_ref = bf16[16,32,128]{2,1,0:T(8,128)(2,1)S(1)} collective-permute-done((bf16[16,32,128]{2,1,0:T(8,128)(2,1)S(1)}, bf16[16,32,128]{2,1,0:T(8,128)(2,1)S(1)}, u32[]{:S(2)}, u32[]{:S(2)}) %collective-permute-start.5) | collective-permute-done | bytes 131104 | tf_op jit(solution)/shard_map/ppermute | solution.py:437
  41.4 3.5 %shard_map.107 = (bf16[2,16,64,256]{3,2,1,0:T(8,128)(2,1)S(1)}, bf16[32,72,128]{2,1,0:T(8,128)(2,1)S(1)}) custom-call(f32[16,32,128]{2,1,0:T(8,128)S(1)} %get-tuple-element.41.gm_ref, bf16[16,32,128]{2,1,0:T(8,128)(2,1)S(1)} %collective-permute-done.4.fl_ref, bf16[16,32,128]{2,1,0:T(8,128)(2,1)S(1)} %collective-permute-done.5.fr_ref, ...), custom_call_target="tpu_custom_call" | custom-call | flops 2415919104 | bytes 4194304 | tf_op jit(solution)/shard_map/pallas_call | solution.py:355
  44.9 22.3 %all_to_all.15.in_ref = bf16[32,72,128]{2,1,0:T(8,128)(2,1)S(1)} all-to-all(bf16[32,72,128]{2,1,0:T(8,128)(2,1)S(1)} %get-tuple-element.52), channel_id=1, replica_groups={{0,8,16,24,32,40,48,56,64,72,80,88,96,104,112,120,128,136,144,152,160,1..., dimensions={0} | all-to-all | bytes 1179648 | tf_op jit(solution)/shard_map/all_to_all | solution.py:468
  67.1 0.0 copy-start.5
  67.1 0.1 shard_map.110
  67.2 13.4 %all_to_all.16.in_ref = bf16[8,72,128]{2,1,0:T(8,128)(2,1)S(1)} all-to-all(bf16[8,72,128]{2,1,0:T(8,128)(2,1)S(1)} %shard_map.110), channel_id=1, replica_groups={{0,1,2,3,4,5,6,7},{8,9,10,11,12,13,14,15},{16,17,18,19,20,21,22,23},{24..., dimensions={0} | all-to-all | bytes 294912 | tf_op jit(solution)/shard_map/all_to_all | solution.py:503
  80.6 0.9 shard_map.111
  81.5 6.9 %all-to-all-start.2 = ((bf16[32,72,128]{2,1,0:T(8,128)(2,1)}), bf16[32,72,128]{2,1,0:T(8,128)(2,1)S(1)}, u32[]{:S(2)}, u32[]{:S(2)}) async-start(bf16[32,72,128]{2,1,0:T(8,128)(2,1)} %shard_map.111), calls=%async_computation.2 | async-start | bytes 1179648 | tf_op jit(solution)/shard_map/all_to_all | solution.py:505
  88.4 0.0 copy-done.5
  88.4 5.2 %shard_map.108 = (bf16[8,64,256]{2,1,0:T(8,128)(2,1)S(1)}, bf16[2,8,64,256]{3,2,1,0:T(8,128)(2,1)S(1)}, bf16[8,64,256]{2,1,0:T(8,128)(2,1)S(1)}) custom-call(bf16[2,16,64,256]{3,2,1,0:T(8,128)(2,1)S(1)} %get-tuple-element.48.delta_ref, bf16[9,96,64]{2,1,0:T(8,128)(2,1)S(1)} %bitcast.19), custom_call_target="tpu_custom_call" | custom-call | flops 1207959552 | bytes 8388608 | tf_op jit(solution)/shard_map/pallas_call | solution.py:355
  93.6 2.2 %collective-permute-start.6 = (bf16[8,64,256]{2,1,0:T(8,128)(2,1)S(1)}, bf16[8,64,256]{2,1,0:T(8,128)(2,1)S(1)}, u32[]{:S(2)}, u32[]{:S(2)}) collective-permute-start(bf16[8,64,256]{2,1,0:T(8,128)(2,1)S(1)} %get-tuple-element.50), channel_id=1, source_target_pairs={{0,1},{1,2},{2,3},{3,4},{4,5},{5,6},{6,7},{7,8},{8,9},{9,10},{10,1... | collective-permute-start | bytes 786440 | tf_op jit(solution)/shard_map/ppermute | solution.py:484
  95.8 1.3 %collective-permute-start.7 = (bf16[8,64,256]{2,1,0:T(8,128)(2,1)S(1)}, bf16[8,64,256]{2,1,0:T(8,128)(2,1)S(1)}, u32[]{:S(2)}, u32[]{:S(2)}) collective-permute-start(bf16[8,64,256]{2,1,0:T(8,128)(2,1)S(1)} %get-tuple-element.51), channel_id=1, source_target_pairs={{1,0},{2,1},{3,2},{4,3},{5,4},{6,5},{7,6},{8,7},{9,8},{10,9},{11,1... | collective-permute-start | bytes 786440 | tf_op jit(solution)/shard_map/ppermute | solution.py:483
  97.1 3.9 %collective-permute-done.6.fl_ref = bf16[8,64,256]{2,1,0:T(8,128)(2,1)S(1)} collective-permute-done((bf16[8,64,256]{2,1,0:T(8,128)(2,1)S(1)}, bf16[8,64,256]{2,1,0:T(8,128)(2,1)S(1)}, u32[]{:S(2)}, u32[]{:S(2)}) %collective-permute-start.6) | collective-permute-done | bytes 262176 | tf_op jit(solution)/shard_map/ppermute | solution.py:484
  101.0 3.8 %collective-permute-done.7.fr_ref = bf16[8,64,256]{2,1,0:T(8,128)(2,1)S(1)} collective-permute-done((bf16[8,64,256]{2,1,0:T(8,128)(2,1)S(1)}, bf16[8,64,256]{2,1,0:T(8,128)(2,1)S(1)}, u32[]{:S(2)}, u32[]{:S(2)}) %collective-permute-start.7) | collective-permute-done | bytes 262176 | tf_op jit(solution)/shard_map/ppermute | solution.py:483
  104.9 0.9 shard_map.109
  105.8 0.0 all-to-all-done.2.in_ref
  105.8 1.1 %shard_map.112 = (f32[1728,128]{1,0:T(8,128)}, f32[1,128]{1,0:T(1,128)}, f32[864,64]{1,0:T(8,128)}, f32[1,64]{1,0:T(1,128)}) custom-call(bf16[32,72,128]{2,1,0:T(8,128)(2,1)S(1)} %all-to-all-done.2.in_ref), custom_call_target="tpu_custom_call" | custom-call | bytes 1048576 | tf_op jit(solution)/shard_map/pallas_call | solution.py:355
Async XLA Ops:
  1.7 9.3 %collective-permute-start = (bf16[64,2048]{1,0:T(8,128)(2,1)S(1)}, bf16[64,2048]{1,0:T(8,128)(2,1)S(1)}, u32[]{:S(2)}, u32[]{:S(2)}) collective-permute-start(bf16[64,2048]{1,0:T(8,128)(2,1)S(1)} %get-tuple-element.58.x1_ref), channel_id=1, source_target_pairs={{0,1},{1,2},{2,3},{3,4},{4,5},{5,6},{6,7},{7,8},{8,9},{9,10},{10,1... | collective-permute-start | bytes 786440 | tf_op jit(solution)/shard_map/ppermute | solution.py:378
  6.1 9.1 %collective-permute-start.1 = (bf16[64,2048]{1,0:T(8,128)(2,1)S(1)}, bf16[64,2048]{1,0:T(8,128)(2,1)S(1)}, u32[]{:S(2)}, u32[]{:S(2)}) collective-permute-start(bf16[64,2048]{1,0:T(8,128)(2,1)S(1)} %get-tuple-element.57.x0_ref), channel_id=1, source_target_pairs={{1,0},{2,1},{3,2},{4,3},{5,4},{6,5},{7,6},{8,7},{9,8},{10,9},{11,1... | collective-permute-start | bytes 786440 | tf_op jit(solution)/shard_map/ppermute | solution.py:379
  7.4 0.9 copy-start.4
  8.3 6.9 %copy-start.1 = (f32[64]{0:T(128)S(1)}, f32[64]{0:T(128)}, u32[]{:S(2)}) copy-start(f32[64]{0:T(128)} %param.8) | copy-start | bytes 772
  15.2 7.9 %copy-start.3 = (bf16[3,3,3,64,128]{4,3,2,1,0:T(8,128)(2,1)S(1)}, bf16[3,3,3,64,128]{4,3,2,1,0:T(8,128)(2,1)}, u32[]{:S(2)}) copy-start(bf16[3,3,3,64,128]{4,3,2,1,0:T(8,128)(2,1)} %param.9) | copy-start | bytes 1327108
  15.2 8.8 %copy-start.2 = (f32[128]{0:T(128)S(1)}, f32[128]{0:T(128)}, u32[]{:S(2)}) copy-start(f32[128]{0:T(128)} %param.10) | copy-start | bytes 1540
  18.1 10.9 %copy-start = (bf16[1,1,32,4096]{3,2,1,0:T(8,128)(2,1)S(1)}, bf16[1,1,32,4096]{3,2,1,0:T(8,128)(2,1)}, u32[]{:S(2)}) copy-start(bf16[1,1,32,4096]{3,2,1,0:T(8,128)(2,1)} %param.11) | copy-start | bytes 786436
  18.1 6.3 %collective-permute-start.2 = (bf16[16,32,128]{2,1,0:T(8,128)(2,1)S(1)}, bf16[16,32,128]{2,1,0:T(8,128)(2,1)S(1)}, u32[]{:S(2)}, u32[]{:S(2)}) collective-permute-start(bf16[16,32,128]{2,1,0:T(8,128)(2,1)S(1)} %get-tuple-element.33.own_ref), channel_id=1, source_target_pairs={{0,1},{1,2},{2,3},{3,4},{4,5},{5,6},{6,7},{7,8},{8,9},{9,10},{10,1... | collective-permute-start | bytes 393224 | tf_op jit(solution)/shard_map/ppermute | solution.py:411
  21.8 7.2 %collective-permute-start.3 = (bf16[16,32,128]{2,1,0:T(8,128)(2,1)S(1)}, bf16[16,32,128]{2,1,0:T(8,128)(2,1)S(1)}, u32[]{:S(2)}, u32[]{:S(2)}) collective-permute-start(bf16[16,32,128]{2,1,0:T(8,128)(2,1)S(1)} %get-tuple-element.33.own_ref), channel_id=1, source_target_pairs={{1,0},{2,1},{3,2},{4,3},{5,4},{6,5},{7,6},{8,7},{9,8},{10,9},{11,1... | collective-permute-start | bytes 393224 | tf_op jit(solution)/shard_map/ppermute | solution.py:412
  31.3 7.0 %collective-permute-start.4 = (bf16[16,32,128]{2,1,0:T(8,128)(2,1)S(1)}, bf16[16,32,128]{2,1,0:T(8,128)(2,1)S(1)}, u32[]{:S(2)}, u32[]{:S(2)}) collective-permute-start(bf16[16,32,128]{2,1,0:T(8,128)(2,1)S(1)} %get-tuple-element.42), channel_id=1, source_target_pairs={{0,1},{1,2},{2,3},{3,4},{4,5},{5,6},{6,7},{7,8},{8,9},{9,10},{10,1... | collective-permute-start | bytes 393224 | tf_op jit(solution)/shard_map/ppermute | solution.py:438
  35.6 5.7 %collective-permute-start.5 = (bf16[16,32,128]{2,1,0:T(8,128)(2,1)S(1)}, bf16[16,32,128]{2,1,0:T(8,128)(2,1)S(1)}, u32[]{:S(2)}, u32[]{:S(2)}) collective-permute-start(bf16[16,32,128]{2,1,0:T(8,128)(2,1)S(1)} %get-tuple-element.43), channel_id=1, source_target_pairs={{1,0},{2,1},{3,2},{4,3},{5,4},{6,5},{7,6},{8,7},{9,8},{10,9},{11,1... | collective-permute-start | bytes 393224 | tf_op jit(solution)/shard_map/ppermute | solution.py:437
  67.1 21.2 %copy-start.5 = (bf16[3,3,3,32,64]{4,3,2,1,0:T(8,128)(2,1)S(1)}, bf16[3,3,3,32,64]{4,3,2,1,0:T(8,128)(2,1)}, u32[]{:S(2)}) copy-start(bf16[3,3,3,32,64]{4,3,2,1,0:T(8,128)(2,1)} %param.7) | copy-start | bytes 331780
  81.5 24.4 %all-to-all-start.2 = ((bf16[32,72,128]{2,1,0:T(8,128)(2,1)}), bf16[32,72,128]{2,1,0:T(8,128)(2,1)S(1)}, u32[]{:S(2)}, u32[]{:S(2)}) async-start(bf16[32,72,128]{2,1,0:T(8,128)(2,1)} %shard_map.111), calls=%async_computation.2 | async-start | bytes 1179648 | tf_op jit(solution)/shard_map/all_to_all | solution.py:505
  93.6 7.4 %collective-permute-start.6 = (bf16[8,64,256]{2,1,0:T(8,128)(2,1)S(1)}, bf16[8,64,256]{2,1,0:T(8,128)(2,1)S(1)}, u32[]{:S(2)}, u32[]{:S(2)}) collective-permute-start(bf16[8,64,256]{2,1,0:T(8,128)(2,1)S(1)} %get-tuple-element.50), channel_id=1, source_target_pairs={{0,1},{1,2},{2,3},{3,4},{4,5},{5,6},{6,7},{7,8},{8,9},{9,10},{10,1... | collective-permute-start | bytes 786440 | tf_op jit(solution)/shard_map/ppermute | solution.py:484
  95.8 9.1 %collective-permute-start.7 = (bf16[8,64,256]{2,1,0:T(8,128)(2,1)S(1)}, bf16[8,64,256]{2,1,0:T(8,128)(2,1)S(1)}, u32[]{:S(2)}, u32[]{:S(2)}) collective-permute-start(bf16[8,64,256]{2,1,0:T(8,128)(2,1)S(1)} %get-tuple-element.51), channel_id=1, source_target_pairs={{1,0},{2,1},{3,2},{4,3},{5,4},{6,5},{7,6},{8,7},{9,8},{10,9},{11,1... | collective-permute-start | bytes 786440 | tf_op jit(solution)/shard_map/ppermute | solution.py:483

commit v4 on v3

--- a/solution.py
+++ b/solution.py
@@ -28,7 +28,7 @@
 
 
 def _sigmoid(v):
-    return 1.0 / (1.0 + jnp.exp(-v))
+    return 0.5 * jnp.tanh(0.5 * v) + 0.5
 
 
 def _zero_edges(buf, rows):
@@ -102,13 +102,21 @@
     lax.fori_loop(0, groups // step, chunk, 0)
 
 
-def _second_kernel(left_ref, right_ref, pre_ref, band_ref, bias_ref, slope_ref, pool_ref, xs_ref, buf, low, high):
+def _second_kernel(keep_ref, left_ref, right_ref, pre_ref, band_ref, bias_ref, slope_ref, pool_ref, xs_ref, buf, low, high):
     rows, groups = left_ref.shape[0], pre_ref.shape[1]
     half = rows // 2
     bias = jnp.concatenate([bias_ref[...]] * 4, axis=1)
     _zero_edges(buf, rows)
     for s, ref in enumerate((left_ref, right_ref)):
-        _spread(lambda t, ref=ref: ref[:, LANES * t : LANES * (t + 1)], groups, rows, 32, buf, xs_ref.at[s])
+        keep = keep_ref[0, s]
+        _spread(
+            lambda t, ref=ref, keep=keep: ref[:, LANES * t : LANES * (t + 1)].astype(F32) * keep,
+            groups,
+            rows,
+            32,
+            buf,
+            xs_ref.at[s],
+        )
     step = 4
     lane = lax.broadcasted_iota(jnp.int32, (step * half, LANES), 1)
 
@@ -145,12 +153,13 @@
 
 
 def _third_kernel(
-    left_ref, right_ref, pre_ref, band_ref, back_ref, cot_ref, delta_ref, ps_ref, ds_ref, gl_ref, gr_ref, buf
+    keep_ref, left_ref, right_ref, pre_ref, band_ref, back_ref, cot_ref, delta_ref, ps_ref, ds_ref, gl_ref, gr_ref, buf
 ):
     groups, rows = left_ref.shape[0], left_ref.shape[1]
     _zero_edges(buf, rows)
     for s, ref in enumerate((left_ref, right_ref)):
-        _spread(lambda t, ref=ref: ref[t], groups, rows, 64, buf, ps_ref.at[s])
+        keep = keep_ref[0, s]
+        _spread(lambda t, ref=ref, keep=keep: ref[t].astype(F32) * keep, groups, rows, 64, buf, ps_ref.at[s])
     near = jnp.concatenate([_cols(ps_ref.at[0, kh], 0, groups) for kh in range(3)], axis=1)
     far = jnp.concatenate([_cols(ps_ref.at[1, kh], 0, groups) for kh in range(3)], axis=1)
     pre = pre_ref[...] + _dot(near, band_ref[0:768, :]) + _dot(far, band_ref[1536:2304, :])
@@ -201,14 +210,15 @@
 
 
 def _grad_one_kernel(
-    gm_ref, fl_ref, fr_ref, slope_ref, own_ref, halo_ref, two_ref, delta_ref, out_ref, sums, up0, up1, flip, one
+    keep_ref, gm_ref, fl_ref, fr_ref, slope_ref, own_ref, halo_ref, two_ref, delta_ref, out_ref, sums, up0, up1, flip, one
 ):
     groups, rows = slope_ref.shape[1], slope_ref.shape[2]
     half = rows // 2
     lane = lax.broadcasted_iota(jnp.int32, (half, LANES), 1)
     sums[...] = jnp.zeros(sums.shape, F32)
+    keep_left, keep_right = keep_ref[0, 0], keep_ref[0, 1]
     for g in range(groups):
-        v = (gm_ref[g] + fl_ref[g].astype(F32) + fr_ref[g].astype(F32)) * 0.125
+        v = (gm_ref[g] + fl_ref[g].astype(F32) * keep_left + fr_ref[g].astype(F32) * keep_right) * 0.125
         turned = pltpu.roll(v, 64, 1)
         a = jnp.where(lane < 64, v, turned)
         b = jnp.where(lane < 64, turned, v)
@@ -305,10 +315,10 @@
     return jnp.concatenate(parts, axis=1)
 
 
-def _edges_kernel(own_ref, fl_ref, fr_ref, out_ref):
+def _edges_kernel(keep_ref, own_ref, fl_ref, fr_ref, out_ref):
     for g in range(fl_ref.shape[0]):
         for p, ref in ((0, fl_ref), (1, fr_ref)):
-            whole = own_ref[p, g].astype(F32) + ref[g].astype(F32)
+            whole = own_ref[p, g].astype(F32) + ref[g].astype(F32) * keep_ref[0, p]
             out_ref[p, :, 256 * g : 256 * (g + 1)] = whole.astype(BF16)
 
 
@@ -351,9 +361,14 @@
     return jax.ShapeDtypeStruct(shape, dtype)
 
 
-def _call(kernel, out, scratch, flops, moved, mib, args):
+def _call(kernel, out, scratch, flops, moved, mib, args, masks=0):
     return pl.pallas_call(
-        kernel, out_shape=out, scratch_shapes=scratch, compiler_params=_params(mib), cost_estimate=_cost(flops, moved)
+        kernel,
+        out_shape=out,
+        in_specs=[pl.BlockSpec(memory_space=pltpu.SMEM)] * masks + [pl.BlockSpec()] * (len(args) - masks),
+        scratch_shapes=scratch,
+        compiler_params=_params(mib),
+        cost_estimate=_cost(flops, moved),
     )(*args)
 
 
@@ -370,8 +385,10 @@
     depth_all = slab * space
     scale_one = 16.0 / math.sqrt(dp * depth_all * side * side)
     scale_two = 1.0 / math.sqrt(dp * (depth_all // 2) * half * half)
-    up = [(i, i + 1) for i in range(space - 1)]
-    down = [(i + 1, i) for i in range(space - 1)]
+    up = [(i, (i + 1) % space) for i in range(space)]
+    down = [((i + 1) % space, i) for i in range(space)]
+    place = lax.axis_index("space")
+    keep = jnp.stack([place > 0, place < space - 1]).astype(F32).reshape(1, 2)
 
     x = act_in.reshape(slab, side, merged)
     x0, x1 = x[0], x[slab - 1]
@@ -406,7 +423,8 @@
         2 * work * 768,
         8 * MIB,
         16,
-        (from_left, from_right, pre, band_one, bias_one.reshape(1, c1)),
+        (keep, from_left, from_right, pre, band_one, bias_one.reshape(1, c1)),
+        1,
     )
     pool_left = lax.ppermute(pooled, "space", up)
     pool_right = lax.ppermute(pooled, "space", down)
@@ -432,7 +450,8 @@
         8 * work_two,
         4 * MIB,
         16,
-        (pool_left, pool_right, pre_two, band_two, back_two, cotangent.reshape(half, -1)),
+        (keep, pool_left, pool_right, pre_two, band_two, back_two, cotangent.reshape(half, -1)),
+        1,
     )
     gp_from_right = lax.ppermute(gp_left, "space", down)
     gp_from_left = lax.ppermute(gp_right, "space", up)
@@ -461,7 +480,8 @@
         2 * work * 2304,
         4 * MIB,
         16,
-        (gp_own, gp_from_left, gp_from_right, slope, xs_own, xs_halo, part_two),
+        (keep, gp_own, gp_from_left, gp_from_right, slope, xs_own, xs_halo, part_two),
+        1,
     )
     rows_two //= peers
     rows_one //= peers
@@ -489,7 +509,8 @@
         2 * work * 128,
         4 * MIB,
         12,
-        (gx_own, gx_from_left, gx_from_right),
+        (keep, gx_own, gx_from_left, gx_from_right),
+        1,
     )
     mine = _call(
         functools.partial(_split_kernel, scale_two, scale_one, rows_two),

time: 109 us -> 97.3 us (0.89); the launches traced: 107 us -> 97 us
  waiting for transfers between devices: 19.7 us -> 10.2 us
  Pallas kernels: 22.2 us -> 24.5 us
  blocking collectives: 35.6 us -> 33.8 us
  starting transfers between devices: 26.7 us -> 25.6 us
    ppermute x1, waiting for transfers between devices: 4.55 us -> 0.01 us  [local(): pool_right = lax.ppermute(pooled, 'space', down)]
    ppermute x1, starting transfers between devices: 4.3 us -> 0.08 us  [local(): gp_from_left = lax.ppermute(gp_right, 'space', up)]
    ppermute x1, waiting for transfers between devices: 4.19 us -> 0.01 us  [local(): from_right = lax.ppermute(x0, 'space', down)]
    ppermute x1, waiting for transfers between devices: 3.85 us -> 0.01 us  [local(): gx_from_right = lax.ppermute(gx_left, 'space', down)]
    ppermute x1, starting transfers between devices: 1.29 us -> 4.96 us  [local(): from_right = lax.ppermute(x0, 'space', down)]
    ppermute x1, starting transfers between devices: 3.7 us -> 0.08 us  [local(): pool_left = lax.ppermute(pooled, 'space', up)]
    ppermute x1, waiting for transfers between devices: 2.99 us -> 0.01 us  [local(): gp_from_right = lax.ppermute(gp_left, 'space', down)]
    ppermute x1, starting transfers between devices: 1.29 us -> 3.83 us  [local(): gp_from_right = lax.ppermute(gp_left, 'space', down)]
  transfers between devices with their start and end apart: 9 -> 9, of which waited for: 6 -> 4; matrix products, arithmetic and copies ran while one was open for 0% -> 0% of each run, Pallas kernels for 11% -> 12%
where the time goes in v4:
time: 97.3 us; the launch traced here: 97 us
  blocking collectives  33.8 us (35%)
  starting transfers between devices  25.6 us (26%)
  Pallas kernels  24.5 us (25%)
  waiting for transfers between devices  10.2 us (10%)
  local copies, waits for them, and re-layouts  2.02 us (2%)
    pallas_call x12, Pallas kernels, _call(): pl.pallas_call(kernel, out_shape=out, in_specs=[pl.BlockSpec(memory_space...  24.5 us
    all_to_all x1, blocking collectives, local(): met = lax.all_to_all(parts, ('dp', 'space'), 0, 0, axis_index_groups=planes)  21.1 us
    all_to_all x1, blocking collectives, local(): met = lax.all_to_all(mine, 'space', 0, 0, axis_index_groups=lines)  12.7 us
    all_to_all x1, starting transfers between devices, local(): lax.all_to_all(joined, ('dp', 'space'), 0, 0, axis_index_groups=planes)  6.91 us
    ppermute x1, waiting for transfers between devices, local(): gx_from_left = lax.ppermute(gx_right, 'space', up)  6.16 us
    ppermute x1, starting transfers between devices, local(): from_right = lax.ppermute(x0, 'space', down)  4.96 us
    ppermute x1, starting transfers between devices, local(): gp_from_right = lax.ppermute(gp_left, 'space', down)  3.83 us
    ppermute x1, starting transfers between devices, local(): pool_right = lax.ppermute(pooled, 'space', down)  3.56 us
  transfers between devices with their start and end apart: 9, of which 4 were waited for; matrix products, arithmetic and copies ran while one was open for 0% of the time, Pallas kernels for 12%

profile of v4, /device:TPU:1, one launch (start us, length us, event | category | flops | bytes accessed | tf_op | source)
XLA Modules:
  0.0 97.0 jit_solution(16238252325506142423)
XLA Ops:
  0.6 1.1 %slice_bitcast_fusion = (bf16[64,2048]{1,0:T(8,128)(2,1)S(1)}, bf16[64,2048]{1,0:T(8,128)(2,1)S(1)}) fusion(bf16[1,2,64,2048]{3,2,1,0:T(8,128)(2,1)} %param.6), kind=kLoop, calls=%fused_computation | loop fusion | bytes 1048576 | tf_op jit(solution)/shard_map/squeeze | solution.py:394
  1.7 2.5 %collective-permute-start = (bf16[64,2048]{1,0:T(8,128)(2,1)S(1)}, bf16[64,2048]{1,0:T(8,128)(2,1)S(1)}, u32[]{:S(2)}, u32[]{:S(2)}) collective-permute-start(bf16[64,2048]{1,0:T(8,128)(2,1)S(1)} %get-tuple-element.58.x1_ref), channel_id=1, source_target_pairs={{0,1},{1,2},{2,3},{3,4},{4,5},{5,6},{6,7},{7,8},{8,9},{9,10},{10,1... | collective-permute-start | bytes 786440 | tf_op jit(solution)/shard_map/ppermute | solution.py:395
  4.2 5.0 %collective-permute-start.1 = (bf16[64,2048]{1,0:T(8,128)(2,1)S(1)}, bf16[64,2048]{1,0:T(8,128)(2,1)S(1)}, u32[]{:S(2)}, u32[]{:S(2)}) collective-permute-start(bf16[64,2048]{1,0:T(8,128)(2,1)S(1)} %get-tuple-element.57.x0_ref), channel_id=1, source_target_pairs={{1,0},{2,1},{3,2},{4,3},{5,4},{6,5},{7,6},{8,7},{9,8},{10,9},{11,1... | collective-permute-start | bytes 786440 | tf_op jit(solution)/shard_map/ppermute | solution.py:396
  9.2 0.1 add_convert_fusion.keep_ref
  9.3 0.0 copy-start.4
  9.3 0.9 copy-done.4
  10.2 0.0 copy-start.1
  10.2 2.6 %shard_map.101 = (f32[2,16,64,256]{3,2,1,0:T(8,128)S(1)}, bf16[2,3,17,64,128]{4,3,2,1,0:T(8,128)(2,1)S(1)}, bf16[2304,256]{1,0:T(8,128)(2,1)S(1)}) custom-call(bf16[64,2048]{1,0:T(8,128)(2,1)S(1)} %get-tuple-element.57.x0_ref, bf16[64,2048]{1,0:T(8,128)(2,1)S(1)} %get-tuple-element.58.x1_ref, bf16[9,96,64]{2,1,0:T(8,128)(2,1)S(1)} %bitcast.20), custom_call_target="tpu_custom_call" | custom-call | flops 1610612736 | bytes 8388608 | tf_op jit(solution)/shard_map/pallas_call | solution.py:365
  12.8 2.3 %collective-permute-done.left_ref = bf16[64,2048]{1,0:T(8,128)(2,1)S(1)} collective-permute-done((bf16[64,2048]{1,0:T(8,128)(2,1)S(1)}, bf16[64,2048]{1,0:T(8,128)(2,1)S(1)}, u32[]{:S(2)}, u32[]{:S(2)}) %collective-permute-start) | collective-permute-done | bytes 262176 | tf_op jit(solution)/shard_map/ppermute | solution.py:395
  15.1 0.0 collective-permute-done.1.right_ref
  15.1 0.0 copy-done.1
  15.1 0.0 copy-start.3
  15.1 0.0 copy-start.2
  15.1 3.4 %shard_map.102 = (f32[2,16,64,256]{3,2,1,0:T(8,128)S(1)}, bf16[16,32,128]{2,1,0:T(8,128)(2,1)S(1)}, bf16[2,3,17,64,128]{4,3,2,1,0:T(8,128)(2,1)S(1)}) custom-call(f32[1,2]{1,0:T(1,128)S(1)} %add_convert_fusion.keep_ref, bf16[64,2048]{1,0:T(8,128)(2,1)S(1)} %collective-permute-done.left_ref, bf16[64,2048]{1,0:T(8,128)(2,1)S(1)} %collective-permute-done.1.right_ref, ...), custom_call_target="tpu_custom_call" | custom-call | flops 805306368 | bytes 8388608 | tf_op jit(solution)/shard_map/pallas_call | solution.py:365
  18.6 0.0 copy-start
  18.6 0.1 collective-permute-start.2
  18.7 3.6 %collective-permute-start.3 = (bf16[16,32,128]{2,1,0:T(8,128)(2,1)S(1)}, bf16[16,32,128]{2,1,0:T(8,128)(2,1)S(1)}, u32[]{:S(2)}, u32[]{:S(2)}) collective-permute-start(bf16[16,32,128]{2,1,0:T(8,128)(2,1)S(1)} %get-tuple-element.33.own_ref), channel_id=1, source_target_pairs={{1,0},{2,1},{3,2},{4,3},{5,4},{6,5},{7,6},{8,7},{9,8},{10,9},{11,1... | collective-permute-start | bytes 393224 | tf_op jit(solution)/shard_map/ppermute | solution.py:430
  22.2 0.0 copy-done.3
  22.2 0.9 shard_map.103
  23.1 0.0 copy-done.2
  23.1 0.4 shard_map.104
  23.6 1.0 %collective-permute-done.2.left_ref = bf16[16,32,128]{2,1,0:T(8,128)(2,1)S(1)} collective-permute-done((bf16[16,32,128]{2,1,0:T(8,128)(2,1)S(1)}, bf16[16,32,128]{2,1,0:T(8,128)(2,1)S(1)}, u32[]{:S(2)}, u32[]{:S(2)}) %collective-permute-start.2) | collective-permute-done | bytes 131104 | tf_op jit(solution)/shard_map/ppermute | solution.py:429
  24.6 0.0 collective-permute-done.3.right_ref
  24.6 0.0 copy-done
  24.6 2.9 %shard_map.105 = (bf16[512,256]{1,0:T(8,128)(2,1)S(1)}, bf16[2,3,17,32,128]{4,3,2,1,0:T(8,128)(2,1)S(1)}, bf16[3,34,32,128]{3,2,1,0:T(8,128)(2,1)S(1)}, bf16[16,...) custom-call(f32[1,2]{1,0:T(1,128)S(1)} %add_convert_fusion.keep_ref, ...), custom_call_target="tpu_custom_call" | custom-call | flops 805306368 | bytes 4194304 | tf_op jit(solution)/shard_map/pallas_call | solution.py:365
  27.5 0.1 collective-permute-start.4
  27.6 3.8 %collective-permute-start.5 = (bf16[16,32,128]{2,1,0:T(8,128)(2,1)S(1)}, bf16[16,32,128]{2,1,0:T(8,128)(2,1)S(1)}, u32[]{:S(2)}, u32[]{:S(2)}) collective-permute-start(bf16[16,32,128]{2,1,0:T(8,128)(2,1)S(1)} %get-tuple-element.43), channel_id=1, source_target_pairs={{1,0},{2,1},{3,2},{4,3},{5,4},{6,5},{7,6},{8,7},{9,8},{10,9},{11,1... | collective-permute-start | bytes 393224 | tf_op jit(solution)/shard_map/ppermute | solution.py:456
  31.4 1.4 %shard_map.106 = (f32[16,32,128]{2,1,0:T(8,128)S(1)}, bf16[1792,128]{1,0:T(8,128)(2,1)S(1)}) custom-call(bf16[512,256]{1,0:T(8,128)(2,1)S(1)} %get-tuple-element.37.delta_ref, bf16[3,17,32,128]{3,2,1,0:T(8,128)(2,1)S(1)} %get-tuple-element.38.own_ref, bf16[2,3,17,32,128]{4,3,2,1,0:T(8,128)(2,1)S(1)} %get-tuple-element.39.halo_ref, ...), custom_call_target="tpu_custom_call" | custom-call | flops 805306368 | bytes 2097152 | tf_op jit(solution)/shard_map/pallas_call | solution.py:365
  32.8 0.7 collective-permute-done.4.fl_ref
  33.5 0.0 collective-permute-done.5.fr_ref
  33.5 4.1 %shard_map.107 = (bf16[2,16,64,256]{3,2,1,0:T(8,128)(2,1)S(1)}, bf16[32,72,128]{2,1,0:T(8,128)(2,1)S(1)}) custom-call(f32[1,2]{1,0:T(1,128)S(1)} %add_convert_fusion.keep_ref, f32[16,32,128]{2,1,0:T(8,128)S(1)} %get-tuple-element.41.gm_ref, bf16[16,32,128]{2,1,0:T(8,128)(2,1)S(1)} %collective-permute-done.4.fl_ref, ...), custom_call_target="tpu_custom_call" | custom-call | flops 2415919104 | bytes 4194304 | tf_op jit(solution)/shard_map/pallas_call | solution.py:365
  37.6 21.1 %all_to_all.15.in_ref = bf16[32,72,128]{2,1,0:T(8,128)(2,1)S(1)} all-to-all(bf16[32,72,128]{2,1,0:T(8,128)(2,1)S(1)} %get-tuple-element.52), channel_id=1, replica_groups={{0,8,16,24,32,40,48,56,64,72,80,88,96,104,112,120,128,136,144,152,160,1..., dimensions={0} | all-to-all | bytes 1179648 | tf_op jit(solution)/shard_map/all_to_all | solution.py:488
  58.7 0.0 copy-start.5
  58.7 0.1 shard_map.110
  58.8 12.7 %all_to_all.16.in_ref = bf16[8,72,128]{2,1,0:T(8,128)(2,1)S(1)} all-to-all(bf16[8,72,128]{2,1,0:T(8,128)(2,1)S(1)} %shard_map.110), channel_id=1, replica_groups={{0,1,2,3,4,5,6,7},{8,9,10,11,12,13,14,15},{16,17,18,19,20,21,22,23},{24..., dimensions={0} | all-to-all | bytes 294912 | tf_op jit(solution)/shard_map/all_to_all | solution.py:524
  71.5 0.9 shard_map.111
  72.4 6.9 %all-to-all-start.2 = ((bf16[32,72,128]{2,1,0:T(8,128)(2,1)}), bf16[32,72,128]{2,1,0:T(8,128)(2,1)S(1)}, u32[]{:S(2)}, u32[]{:S(2)}) async-start(bf16[32,72,128]{2,1,0:T(8,128)(2,1)} %shard_map.111), calls=%async_computation.2 | async-start | bytes 1179648 | tf_op jit(solution)/shard_map/all_to_all | solution.py:526
  79.3 0.0 copy-done.5
  79.3 5.2 %shard_map.108 = (bf16[8,64,256]{2,1,0:T(8,128)(2,1)S(1)}, bf16[2,8,64,256]{3,2,1,0:T(8,128)(2,1)S(1)}, bf16[8,64,256]{2,1,0:T(8,128)(2,1)S(1)}) custom-call(bf16[2,16,64,256]{3,2,1,0:T(8,128)(2,1)S(1)} %get-tuple-element.48.delta_ref, bf16[9,96,64]{2,1,0:T(8,128)(2,1)S(1)} %bitcast.21), custom_call_target="tpu_custom_call" | custom-call | flops 1207959552 | bytes 8388608 | tf_op jit(solution)/shard_map/pallas_call | solution.py:365
  84.5 0.4 collective-permute-start.6
  84.9 3.3 %collective-permute-start.7 = (bf16[8,64,256]{2,1,0:T(8,128)(2,1)S(1)}, bf16[8,64,256]{2,1,0:T(8,128)(2,1)S(1)}, u32[]{:S(2)}, u32[]{:S(2)}) collective-permute-start(bf16[8,64,256]{2,1,0:T(8,128)(2,1)S(1)} %get-tuple-element.51), channel_id=1, source_target_pairs={{1,0},{2,1},{3,2},{4,3},{5,4},{6,5},{7,6},{8,7},{9,8},{10,9},{11,1... | collective-permute-start | bytes 786440 | tf_op jit(solution)/shard_map/ppermute | solution.py:503
  88.2 6.2 %collective-permute-done.6.fl_ref = bf16[8,64,256]{2,1,0:T(8,128)(2,1)S(1)} collective-permute-done((bf16[8,64,256]{2,1,0:T(8,128)(2,1)S(1)}, bf16[8,64,256]{2,1,0:T(8,128)(2,1)S(1)}, u32[]{:S(2)}, u32[]{:S(2)}) %collective-permute-start.6) | collective-permute-done | bytes 262176 | tf_op jit(solution)/shard_map/ppermute | solution.py:504
  94.3 0.0 collective-permute-done.7.fr_ref
  94.3 1.5 %shard_map.109 = bf16[2,64,2048]{2,1,0:T(8,128)(2,1)} custom-call(f32[1,2]{1,0:T(1,128)S(1)} %add_convert_fusion.keep_ref, bf16[2,8,64,256]{3,2,1,0:T(8,128)(2,1)S(1)} %get-tuple-element.49.own_ref, bf16[8,64,256]{2,1,0:T(8,128)(2,1)S(1)} %collective-permute-done.6.fl_ref, bf16[8,64,256]{2,1,0:T(8,128)(2,1)S(1)} %collective-permute-done.7.fr_ref), custom_call_target="tpu_custom_call" | custom-call | flops 134217728 | bytes 4194304 | tf_op jit(solution)/shard_map/pallas_call | solution.py:365
  95.8 0.0 all-to-all-done.2.in_ref
  95.8 1.1 %shard_map.112 = (f32[1728,128]{1,0:T(8,128)}, f32[1,128]{1,0:T(1,128)}, f32[864,64]{1,0:T(8,128)}, f32[1,64]{1,0:T(1,128)}) custom-call(bf16[32,72,128]{2,1,0:T(8,128)(2,1)S(1)} %all-to-all-done.2.in_ref), custom_call_target="tpu_custom_call" | custom-call | bytes 1048576 | tf_op jit(solution)/shard_map/pallas_call | solution.py:365
Async XLA Ops:
  1.7 13.4 %collective-permute-start = (bf16[64,2048]{1,0:T(8,128)(2,1)S(1)}, bf16[64,2048]{1,0:T(8,128)(2,1)S(1)}, u32[]{:S(2)}, u32[]{:S(2)}) collective-permute-start(bf16[64,2048]{1,0:T(8,128)(2,1)S(1)} %get-tuple-element.58.x1_ref), channel_id=1, source_target_pairs={{0,1},{1,2},{2,3},{3,4},{4,5},{5,6},{6,7},{7,8},{8,9},{9,10},{10,1... | collective-permute-start | bytes 786440 | tf_op jit(solution)/shard_map/ppermute | solution.py:395
  4.2 10.9 %collective-permute-start.1 = (bf16[64,2048]{1,0:T(8,128)(2,1)S(1)}, bf16[64,2048]{1,0:T(8,128)(2,1)S(1)}, u32[]{:S(2)}, u32[]{:S(2)}) collective-permute-start(bf16[64,2048]{1,0:T(8,128)(2,1)S(1)} %get-tuple-element.57.x0_ref), channel_id=1, source_target_pairs={{1,0},{2,1},{3,2},{4,3},{5,4},{6,5},{7,6},{8,7},{9,8},{10,9},{11,1... | collective-permute-start | bytes 786440 | tf_op jit(solution)/shard_map/ppermute | solution.py:396
  9.3 0.9 copy-start.4
  10.2 4.9 %copy-start.1 = (f32[64]{0:T(128)S(1)}, f32[64]{0:T(128)}, u32[]{:S(2)}) copy-start(f32[64]{0:T(128)} %param.8) | copy-start | bytes 772
  15.1 7.1 %copy-start.3 = (bf16[3,3,3,64,128]{4,3,2,1,0:T(8,128)(2,1)S(1)}, bf16[3,3,3,64,128]{4,3,2,1,0:T(8,128)(2,1)}, u32[]{:S(2)}) copy-start(bf16[3,3,3,64,128]{4,3,2,1,0:T(8,128)(2,1)} %param.9) | copy-start | bytes 1327108
  15.1 8.0 %copy-start.2 = (f32[128]{0:T(128)S(1)}, f32[128]{0:T(128)}, u32[]{:S(2)}) copy-start(f32[128]{0:T(128)} %param.10) | copy-start | bytes 1540
  18.6 6.0 %copy-start = (bf16[1,1,32,4096]{3,2,1,0:T(8,128)(2,1)S(1)}, bf16[1,1,32,4096]{3,2,1,0:T(8,128)(2,1)}, u32[]{:S(2)}) copy-start(bf16[1,1,32,4096]{3,2,1,0:T(8,128)(2,1)} %param.11) | copy-start | bytes 786436
  18.6 6.0 %collective-permute-start.2 = (bf16[16,32,128]{2,1,0:T(8,128)(2,1)S(1)}, bf16[16,32,128]{2,1,0:T(8,128)(2,1)S(1)}, u32[]{:S(2)}, u32[]{:S(2)}) collective-permute-start(bf16[16,32,128]{2,1,0:T(8,128)(2,1)S(1)} %get-tuple-element.33.own_ref), channel_id=1, source_target_pairs={{0,1},{1,2},{2,3},{3,4},{4,5},{5,6},{6,7},{7,8},{8,9},{9,10},{10,1... | collective-permute-start | bytes 393224 | tf_op jit(solution)/shard_map/ppermute | solution.py:429
  18.7 5.9 %collective-permute-start.3 = (bf16[16,32,128]{2,1,0:T(8,128)(2,1)S(1)}, bf16[16,32,128]{2,1,0:T(8,128)(2,1)S(1)}, u32[]{:S(2)}, u32[]{:S(2)}) collective-permute-start(bf16[16,32,128]{2,1,0:T(8,128)(2,1)S(1)} %get-tuple-element.33.own_ref), channel_id=1, source_target_pairs={{1,0},{2,1},{3,2},{4,3},{5,4},{6,5},{7,6},{8,7},{9,8},{10,9},{11,1... | collective-permute-start | bytes 393224 | tf_op jit(solution)/shard_map/ppermute | solution.py:430
  27.5 6.0 %collective-permute-start.4 = (bf16[16,32,128]{2,1,0:T(8,128)(2,1)S(1)}, bf16[16,32,128]{2,1,0:T(8,128)(2,1)S(1)}, u32[]{:S(2)}, u32[]{:S(2)}) collective-permute-start(bf16[16,32,128]{2,1,0:T(8,128)(2,1)S(1)} %get-tuple-element.42), channel_id=1, source_target_pairs={{0,1},{1,2},{2,3},{3,4},{4,5},{5,6},{6,7},{7,8},{8,9},{9,10},{10,1... | collective-permute-start | bytes 393224 | tf_op jit(solution)/shard_map/ppermute | solution.py:457
  27.6 5.9 %collective-permute-start.5 = (bf16[16,32,128]{2,1,0:T(8,128)(2,1)S(1)}, bf16[16,32,128]{2,1,0:T(8,128)(2,1)S(1)}, u32[]{:S(2)}, u32[]{:S(2)}) collective-permute-start(bf16[16,32,128]{2,1,0:T(8,128)(2,1)S(1)} %get-tuple-element.43), channel_id=1, source_target_pairs={{1,0},{2,1},{3,2},{4,3},{5,4},{6,5},{7,6},{8,7},{9,8},{10,9},{11,1... | collective-permute-start | bytes 393224 | tf_op jit(solution)/shard_map/ppermute | solution.py:456
  58.7 20.6 %copy-start.5 = (bf16[3,3,3,32,64]{4,3,2,1,0:T(8,128)(2,1)S(1)}, bf16[3,3,3,32,64]{4,3,2,1,0:T(8,128)(2,1)}, u32[]{:S(2)}) copy-start(bf16[3,3,3,32,64]{4,3,2,1,0:T(8,128)(2,1)} %param.7) | copy-start | bytes 331780
  72.4 23.4 %all-to-all-start.2 = ((bf16[32,72,128]{2,1,0:T(8,128)(2,1)}), bf16[32,72,128]{2,1,0:T(8,128)(2,1)S(1)}, u32[]{:S(2)}, u32[]{:S(2)}) async-start(bf16[32,72,128]{2,1,0:T(8,128)(2,1)} %shard_map.111), calls=%async_computation.2 | async-start | bytes 1179648 | tf_op jit(solution)/shard_map/all_to_all | solution.py:526
  84.5 9.8 %collective-permute-start.6 = (bf16[8,64,256]{2,1,0:T(8,128)(2,1)S(1)}, bf16[8,64,256]{2,1,0:T(8,128)(2,1)S(1)}, u32[]{:S(2)}, u32[]{:S(2)}) collective-permute-start(bf16[8,64,256]{2,1,0:T(8,128)(2,1)S(1)} %get-tuple-element.50), channel_id=1, source_target_pairs={{0,1},{1,2},{2,3},{3,4},{4,5},{5,6},{6,7},{7,8},{8,9},{9,10},{10,1... | collective-permute-start | bytes 786440 | tf_op jit(solution)/shard_map/ppermute | solution.py:504
  84.9 9.5 %collective-permute-start.7 = (bf16[8,64,256]{2,1,0:T(8,128)(2,1)S(1)}, bf16[8,64,256]{2,1,0:T(8,128)(2,1)S(1)}, u32[]{:S(2)}, u32[]{:S(2)}) collective-permute-start(bf16[8,64,256]{2,1,0:T(8,128)(2,1)S(1)} %get-tuple-element.51), channel_id=1, source_target_pairs={{1,0},{2,1},{3,2},{4,3},{5,4},{6,5},{7,6},{8,7},{9,8},{10,9},{11,1... | collective-permute-start | bytes 786440 | tf_op jit(solution)/shard_map/ppermute | solution.py:503

commit v5 on v4

--- a/solution.py
+++ b/solution.py
@@ -29,6 +29,10 @@
 
 def _sigmoid(v):
     return 0.5 * jnp.tanh(0.5 * v) + 0.5
+
+
+def _mask(keep_ref, side, rows):
+    return jnp.concatenate([keep_ref[side]] * (rows // 8), axis=0)
 
 
 def _zero_edges(buf, rows):
@@ -90,16 +94,11 @@
     for p, ref in enumerate((x0_ref, x1_ref)):
         _spread(lambda t, ref=ref: ref[:, LANES * t : LANES * (t + 1)], groups, rows, 32, buf, xs_ref.at[p])
     step = 8
-
-    def chunk(c, carry):
-        g = c * step
+    for g in range(0, groups, step):
         sides = [[_cols(xs_ref.at[p, kh], g, step) for kh in range(3)] for p in range(2)]
         lhs = jnp.concatenate(sides[0] + sides[1], axis=1)
         pre_ref[0, pl.ds(g, step)] = _dot(lhs, band_ref[768:2304, :]).reshape(step, rows, 256)
         pre_ref[1, pl.ds(g, step)] = _dot(lhs, band_ref[0:1536, :]).reshape(step, rows, 256)
-        return carry
-
-    lax.fori_loop(0, groups // step, chunk, 0)
 
 
 def _second_kernel(keep_ref, left_ref, right_ref, pre_ref, band_ref, bias_ref, slope_ref, pool_ref, xs_ref, buf, low, high):
@@ -108,7 +107,7 @@
     bias = jnp.concatenate([bias_ref[...]] * 4, axis=1)
     _zero_edges(buf, rows)
     for s, ref in enumerate((left_ref, right_ref)):
-        keep = keep_ref[0, s]
+        keep = _mask(keep_ref, s, rows)
         _spread(
             lambda t, ref=ref, keep=keep: ref[:, LANES * t : LANES * (t + 1)].astype(F32) * keep,
             groups,
@@ -120,8 +119,7 @@
     step = 4
     lane = lax.broadcasted_iota(jnp.int32, (step * half, LANES), 1)
 
-    def chunk(c, carry):
-        g = c * step
+    for g in range(0, groups, step):
         total = None
         for p in range(2):
             lhs = jnp.concatenate([_cols(xs_ref.at[p, kh], g, step) for kh in range(3)], axis=1)
@@ -131,16 +129,14 @@
             slope_ref[p, pl.ds(g, step)] = (sig * (1.0 + pre * (1.0 - sig))).reshape(step, rows, 256)
             act = pre * sig
             total = act if total is None else total + act
-        for part, lanes in ((low, 0), (high, LANES)):
+        sums = []
+        for ref, lanes in ((low, 0), (high, LANES)):
+            part = ref.at[g // step]
             v = total[:, lanes : lanes + LANES]
             part[...] = v + pltpu.roll(v, 64, 1)
-        a = low[pl.ds(0, step * half, stride=2), :] + low[pl.ds(1, step * half, stride=2), :]
-        b = high[pl.ds(0, step * half, stride=2), :] + high[pl.ds(1, step * half, stride=2), :]
-        mean = jnp.where(lane < 64, a, b) * 0.125
+            sums.append(part[pl.ds(0, step * half, stride=2), :] + part[pl.ds(1, step * half, stride=2), :])
+        mean = jnp.where(lane < 64, sums[0], sums[1]) * 0.125
         pool_ref[pl.ds(g, step)] = mean.astype(BF16).reshape(step, half, LANES)
-        return carry
-
-    lax.fori_loop(0, groups // step, chunk, 0)
 
 
 def _mid_kernel(own_ref, band_ref, bias_ref, ps_ref, pre_ref, buf):
@@ -158,7 +154,7 @@
     groups, rows = left_ref.shape[0], left_ref.shape[1]
     _zero_edges(buf, rows)
     for s, ref in enumerate((left_ref, right_ref)):
-        keep = keep_ref[0, s]
+        keep = _mask(keep_ref, s, rows)
         _spread(lambda t, ref=ref, keep=keep: ref[t].astype(F32) * keep, groups, rows, 64, buf, ps_ref.at[s])
     near = jnp.concatenate([_cols(ps_ref.at[0, kh], 0, groups) for kh in range(3)], axis=1)
     far = jnp.concatenate([_cols(ps_ref.at[1, kh], 0, groups) for kh in range(3)], axis=1)
@@ -216,7 +212,7 @@
     half = rows // 2
     lane = lax.broadcasted_iota(jnp.int32, (half, LANES), 1)
     sums[...] = jnp.zeros(sums.shape, F32)
-    keep_left, keep_right = keep_ref[0, 0], keep_ref[0, 1]
+    keep_left, keep_right = _mask(keep_ref, 0, half), _mask(keep_ref, 1, half)
     for g in range(groups):
         v = (gm_ref[g] + fl_ref[g].astype(F32) * keep_left + fr_ref[g].astype(F32) * keep_right) * 0.125
         turned = pltpu.roll(v, 64, 1)
@@ -277,23 +273,18 @@
             ds[p, kh, 0] = zero
             ds[p, kh, cells + 1] = zero
 
-    def group(g, carry):
+    for g in range(groups):
         for p in range(2):
             for j in range(2):
                 low = delta_ref[p, g, :, LANES * j : LANES * (j + 1)]
-                spot = buf.at[2 * p + j]
+                spot = buf.at[(2 * p + j + 4 * g) % buf.shape[0]]
                 spot[8 : 8 + rows, :] = low.astype(F32)
                 t = 2 * g + j + 1
                 ds[p, 0, t] = spot[9 : 9 + rows, :].astype(BF16)
                 ds[p, 1, t] = low
                 ds[p, 2, t] = spot[7 : 7 + rows, :].astype(BF16)
-        return carry
-
-    lax.fori_loop(0, groups, group, 0)
     step = 4
-
-    def chunk(c, carry):
-        g = c * step
+    for g in range(0, groups // 2, step):
         spot = pl.ds(g, step)
         near = _window(ds.at[0], g, step)
         far = _window(ds.at[1], g, step)
@@ -302,9 +293,6 @@
         for p in range(2):
             own = _dot(near, back[1 + p]) + _dot(far, back[p])
             own_ref[p, spot] = own.astype(BF16).reshape(step, rows, 256)
-        return carry
-
-    lax.fori_loop(0, groups // 2 // step, chunk, 0)
 
 
 def _window(ref, first, count):
@@ -316,9 +304,11 @@
 
 
 def _edges_kernel(keep_ref, own_ref, fl_ref, fr_ref, out_ref):
+    rows = fl_ref.shape[1]
+    masks = [jnp.concatenate([_mask(keep_ref, p, rows)] * 2, axis=1) for p in range(2)]
     for g in range(fl_ref.shape[0]):
         for p, ref in ((0, fl_ref), (1, fr_ref)):
-            whole = own_ref[p, g].astype(F32) + ref[g].astype(F32) * keep_ref[0, p]
+            whole = own_ref[p, g].astype(F32) + ref[g].astype(F32) * masks[p]
             out_ref[p, :, 256 * g : 256 * (g + 1)] = whole.astype(BF16)
 
 
@@ -361,14 +351,9 @@
     return jax.ShapeDtypeStruct(shape, dtype)
 
 
-def _call(kernel, out, scratch, flops, moved, mib, args, masks=0):
+def _call(kernel, out, scratch, flops, moved, mib, args):
     return pl.pallas_call(
-        kernel,
-        out_shape=out,
-        in_specs=[pl.BlockSpec(memory_space=pltpu.SMEM)] * masks + [pl.BlockSpec()] * (len(args) - masks),
-        scratch_shapes=scratch,
-        compiler_params=_params(mib),
-        cost_estimate=_cost(flops, moved),
+        kernel, out_shape=out, scratch_shapes=scratch, compiler_params=_params(mib), cost_estimate=_cost(flops, moved)
     )(*args)
 
 
@@ -388,7 +373,8 @@
     up = [(i, (i + 1) % space) for i in range(space)]
     down = [((i + 1) % space, i) for i in range(space)]
     place = lax.axis_index("space")
-    keep = jnp.stack([place > 0, place < space - 1]).astype(F32).reshape(1, 2)
+    keep = jnp.stack([place > 0, place < space - 1]).astype(F32)
+    keep = jnp.broadcast_to(keep[:, None, None], (2, 8, LANES))
 
     x = act_in.reshape(slab, side, merged)
     x0, x1 = x[0], x[slab - 1]
@@ -419,12 +405,11 @@
     slope, pooled, xs_halo = _call(
         _second_kernel,
         (_shape((2, groups, side, 256), F32), tile, _shape(xs_shape, BF16)),
-        [tall] + [pltpu.VMEM((4 * side, LANES), F32)] * 2,
+        [tall] + [pltpu.VMEM((groups // 4, 4 * side, LANES), F32)] * 2,
         2 * work * 768,
         8 * MIB,
         16,
         (keep, from_left, from_right, pre, band_one, bias_one.reshape(1, c1)),
-        1,
     )
     pool_left = lax.ppermute(pooled, "space", up)
     pool_right = lax.ppermute(pooled, "space", down)
@@ -451,7 +436,6 @@
         4 * MIB,
         16,
         (keep, pool_left, pool_right, pre_two, band_two, back_two, cotangent.reshape(half, -1)),
-        1,
     )
     gp_from_right = lax.ppermute(gp_left, "space", down)
     gp_from_left = lax.ppermute(gp_right, "space", up)
@@ -481,7 +465,6 @@
         4 * MIB,
         16,
         (keep, gp_own, gp_from_left, gp_from_right, slope, xs_own, xs_halo, part_two),
-        1,
     )
     rows_two //= peers
     rows_one //= peers
@@ -493,7 +476,7 @@
         [
             pltpu.VMEM((2, 3, 2 * groups + 2, side, LANES), BF16),
             pltpu.VMEM((3, 2304, 256), BF16),
-            pltpu.VMEM((4, side + 16, LANES), F32),
+            pltpu.VMEM((16, side + 16, LANES), F32),
         ],
         2 * work * 2304 // 2,
         8 * MIB,
@@ -510,7 +493,6 @@
         4 * MIB,
         12,
         (keep, gx_own, gx_from_left, gx_from_right),
-        1,
     )
     mine = _call(
         functools.partial(_split_kernel, scale_two, scale_one, rows_two),

time: 97.3 us -> 93.3 us (0.959)
  Pallas kernels: 24.5 us -> 19.9 us
    pallas_call x12, Pallas kernels: 24.5 us -> 19.9 us  [_call(): pl.pallas_call(kernel, out_shape=out, scratch_shapes=scratch, compiler_pa...]
  transfers between devices with their start and end apart: 9 -> 9, of which waited for: 4 -> 4; matrix products, arithmetic and copies ran while one was open for 0% -> 0% of each run, Pallas kernels for 12% -> 11%
where the time goes in v5:
time: 93.3 us; the launch traced here: 93 us
  blocking collectives  33.8 us (36%)
  starting transfers between devices  25.6 us (27%)
  Pallas kernels  19.9 us (21%)
  waiting for transfers between devices  10.7 us (11%)
  local copies, waits for them, and re-layouts  2.09 us (2%)
    all_to_all x1, blocking collectives, local(): met = lax.all_to_all(parts, ('dp', 'space'), 0, 0, axis_index_groups=planes)  21.1 us
    pallas_call x12, Pallas kernels, _call(): pl.pallas_call(kernel, out_shape=out, scratch_shapes=scratch, compiler_pa...  19.9 us
    all_to_all x1, blocking collectives, local(): met = lax.all_to_all(mine, 'space', 0, 0, axis_index_groups=lines)  12.7 us
    all_to_all x1, starting transfers between devices, local(): lax.all_to_all(joined, ('dp', 'space'), 0, 0, axis_index_groups=planes)  6.91 us
    ppermute x1, waiting for transfers between devices, local(): gx_from_left = lax.ppermute(gx_right, 'space', up)  6.16 us
    ppermute x1, starting transfers between devices, local(): from_right = lax.ppermute(x0, 'space', down)  4.96 us
    ppermute x1, starting transfers between devices, local(): gp_from_right = lax.ppermute(gp_left, 'space', down)  3.83 us
    ppermute x1, starting transfers between devices, local(): pool_right = lax.ppermute(pooled, 'space', down)  3.56 us
  transfers between devices with their start and end apart: 9, of which 4 were waited for; matrix products, arithmetic and copies ran while one was open for 0% of the time, Pallas kernels for 11%

profile of v5, /device:TPU:1, one launch (start us, length us, event | category | flops | bytes accessed | tf_op | source)
XLA Modules:
  0.0 93.0 jit_solution(17301289367357239865)
XLA Ops:
  0.6 1.1 %slice_bitcast_fusion = (bf16[64,2048]{1,0:T(8,128)(2,1)S(1)}, bf16[64,2048]{1,0:T(8,128)(2,1)S(1)}) fusion(bf16[1,2,64,2048]{3,2,1,0:T(8,128)(2,1)} %param.6), kind=kLoop, calls=%fused_computation | loop fusion | bytes 1048576 | tf_op jit(solution)/shard_map/squeeze | solution.py:380
  1.7 2.5 %collective-permute-start = (bf16[64,2048]{1,0:T(8,128)(2,1)S(1)}, bf16[64,2048]{1,0:T(8,128)(2,1)S(1)}, u32[]{:S(2)}, u32[]{:S(2)}) collective-permute-start(bf16[64,2048]{1,0:T(8,128)(2,1)S(1)} %get-tuple-element.58.x1_ref), channel_id=1, source_target_pairs={{0,1},{1,2},{2,3},{3,4},{4,5},{5,6},{6,7},{7,8},{8,9},{9,10},{10,1... | collective-permute-start | bytes 786440 | tf_op jit(solution)/shard_map/ppermute | solution.py:381
  4.2 5.0 %collective-permute-start.1 = (bf16[64,2048]{1,0:T(8,128)(2,1)S(1)}, bf16[64,2048]{1,0:T(8,128)(2,1)S(1)}, u32[]{:S(2)}, u32[]{:S(2)}) collective-permute-start(bf16[64,2048]{1,0:T(8,128)(2,1)S(1)} %get-tuple-element.57.x0_ref), channel_id=1, source_target_pairs={{1,0},{2,1},{3,2},{4,3},{5,4},{6,5},{7,6},{8,7},{9,8},{10,9},{11,1... | collective-permute-start | bytes 786440 | tf_op jit(solution)/shard_map/ppermute | solution.py:382
  9.2 0.1 add_convert_fusion
  9.3 0.0 copy-start.4
  9.3 0.9 %copy-done.4 = bf16[3,3,3,32,64]{4,3,2,1,0:T(8,128)(2,1)S(1)} copy-done((bf16[3,3,3,32,64]{4,3,2,1,0:T(8,128)(2,1)S(1)}, bf16[3,3,3,32,64]{4,3,2,1,0:T(8,128)(2,1)}, u32[]{:S(2)}) %copy-start.4) | copy-done | bytes 110616
  10.2 0.0 copy-start.1
  10.2 2.0 %shard_map.101 = (f32[2,16,64,256]{3,2,1,0:T(8,128)S(1)}, bf16[2,3,17,64,128]{4,3,2,1,0:T(8,128)(2,1)S(1)}, bf16[2304,256]{1,0:T(8,128)(2,1)S(1)}) custom-call(bf16[64,2048]{1,0:T(8,128)(2,1)S(1)} %get-tuple-element.57.x0_ref, bf16[64,2048]{1,0:T(8,128)(2,1)S(1)} %get-tuple-element.58.x1_ref, bf16[9,96,64]{2,1,0:T(8,128)(2,1)S(1)} %bitcast.20), custom_call_target="tpu_custom_call" | custom-call | flops 1610612736 | bytes 8388608 | tf_op jit(solution)/shard_map/pallas_call | solution.py:355
  12.2 2.9 %collective-permute-done.left_ref = bf16[64,2048]{1,0:T(8,128)(2,1)S(1)} collective-permute-done((bf16[64,2048]{1,0:T(8,128)(2,1)S(1)}, bf16[64,2048]{1,0:T(8,128)(2,1)S(1)}, u32[]{:S(2)}, u32[]{:S(2)}) %collective-permute-start) | collective-permute-done | bytes 262176 | tf_op jit(solution)/shard_map/ppermute | solution.py:381
  15.1 0.0 collective-permute-done.1.right_ref
  15.1 0.1 broadcast_in_dim.2.keep_ref
  15.2 0.0 copy-done.1
  15.2 0.0 copy-start.3
  15.2 0.0 copy-start.2
  15.2 1.8 %shard_map.102 = (f32[2,16,64,256]{3,2,1,0:T(8,128)S(1)}, bf16[16,32,128]{2,1,0:T(8,128)(2,1)S(1)}, bf16[2,3,17,64,128]{4,3,2,1,0:T(8,128)(2,1)S(1)}) custom-call(f32[2,8,128]{2,1,0:T(8,128)S(1)} %broadcast_in_dim.2.keep_ref, bf16[64,2048]{1,0:T(8,128)(2,1)S(1)} %collective-permute-done.left_ref, bf16[64,2048]{1,0:T(8,128)(2,1)S(1)} %collective-permute-done.1.right_ref, ...), custom_call_target="tpu_custom_call" | custom-call | flops 805306368 | bytes 8388608 | tf_op jit(solution)/shard_map/pallas_call | solution.py:355
  17.0 0.0 copy-start
  17.0 0.1 collective-permute-start.2
  17.1 3.6 %collective-permute-start.3 = (bf16[16,32,128]{2,1,0:T(8,128)(2,1)S(1)}, bf16[16,32,128]{2,1,0:T(8,128)(2,1)S(1)}, u32[]{:S(2)}, u32[]{:S(2)}) collective-permute-start(bf16[16,32,128]{2,1,0:T(8,128)(2,1)S(1)} %get-tuple-element.33.own_ref), channel_id=1, source_target_pairs={{1,0},{2,1},{3,2},{4,3},{5,4},{6,5},{7,6},{8,7},{9,8},{10,9},{11,1... | collective-permute-start | bytes 393224 | tf_op jit(solution)/shard_map/ppermute | solution.py:415
  20.7 0.0 copy-done.3
  20.7 0.9 shard_map.103
  21.5 0.0 copy-done.2
  21.5 0.4 shard_map.104
  22.0 1.0 %collective-permute-done.2.left_ref = bf16[16,32,128]{2,1,0:T(8,128)(2,1)S(1)} collective-permute-done((bf16[16,32,128]{2,1,0:T(8,128)(2,1)S(1)}, bf16[16,32,128]{2,1,0:T(8,128)(2,1)S(1)}, u32[]{:S(2)}, u32[]{:S(2)}) %collective-permute-start.2) | collective-permute-done | bytes 131104 | tf_op jit(solution)/shard_map/ppermute | solution.py:414
  23.0 0.0 collective-permute-done.3.right_ref
  23.0 0.0 copy-done
  23.0 2.3 %shard_map.105 = (bf16[512,256]{1,0:T(8,128)(2,1)S(1)}, bf16[2,3,17,32,128]{4,3,2,1,0:T(8,128)(2,1)S(1)}, bf16[3,34,32,128]{3,2,1,0:T(8,128)(2,1)S(1)}, bf16[16,...) custom-call(f32[2,8,128]{2,1,0:T(8,128)S(1)} %broadcast_in_dim.2.keep_ref, ...), custom_call_target="tpu_custom_call" | custom-call | flops 805306368 | bytes 4194304 | tf_op jit(solution)/shard_map/pallas_call | solution.py:355
  25.4 0.1 collective-permute-start.4
  25.5 3.8 %collective-permute-start.5 = (bf16[16,32,128]{2,1,0:T(8,128)(2,1)S(1)}, bf16[16,32,128]{2,1,0:T(8,128)(2,1)S(1)}, u32[]{:S(2)}, u32[]{:S(2)}) collective-permute-start(bf16[16,32,128]{2,1,0:T(8,128)(2,1)S(1)} %get-tuple-element.43), channel_id=1, source_target_pairs={{1,0},{2,1},{3,2},{4,3},{5,4},{6,5},{7,6},{8,7},{9,8},{10,9},{11,1... | collective-permute-start | bytes 393224 | tf_op jit(solution)/shard_map/ppermute | solution.py:440
  29.3 1.4 %shard_map.106 = (f32[16,32,128]{2,1,0:T(8,128)S(1)}, bf16[1792,128]{1,0:T(8,128)(2,1)S(1)}) custom-call(bf16[512,256]{1,0:T(8,128)(2,1)S(1)} %get-tuple-element.37.delta_ref, bf16[3,17,32,128]{3,2,1,0:T(8,128)(2,1)S(1)} %get-tuple-element.38.own_ref, bf16[2,3,17,32,128]{4,3,2,1,0:T(8,128)(2,1)S(1)} %get-tuple-element.39.halo_ref, ...), custom_call_target="tpu_custom_call" | custom-call | flops 805306368 | bytes 2097152 | tf_op jit(solution)/shard_map/pallas_call | solution.py:355
  30.7 0.7 collective-permute-done.4.fl_ref
  31.4 0.0 collective-permute-done.5.fr_ref
  31.4 3.6 %shard_map.107 = (bf16[2,16,64,256]{3,2,1,0:T(8,128)(2,1)S(1)}, bf16[32,72,128]{2,1,0:T(8,128)(2,1)S(1)}) custom-call(f32[2,8,128]{2,1,0:T(8,128)S(1)} %broadcast_in_dim.2.keep_ref, f32[16,32,128]{2,1,0:T(8,128)S(1)} %get-tuple-element.41.gm_ref, bf16[16,32,128]{2,1,0:T(8,128)(2,1)S(1)} %collective-permute-done.4.fl_ref, ...), custom_call_target="tpu_custom_call" | custom-call | flops 2415919104 | bytes 4194304 | tf_op jit(solution)/shard_map/pallas_call | solution.py:355
  35.0 21.1 %all_to_all.15.in_ref = bf16[32,72,128]{2,1,0:T(8,128)(2,1)S(1)} all-to-all(bf16[32,72,128]{2,1,0:T(8,128)(2,1)S(1)} %get-tuple-element.52), channel_id=1, replica_groups={{0,8,16,24,32,40,48,56,64,72,80,88,96,104,112,120,128,136,144,152,160,1..., dimensions={0} | all-to-all | bytes 1179648 | tf_op jit(solution)/shard_map/all_to_all | solution.py:471
  56.1 0.0 copy-start.5
  56.1 0.1 shard_map.110
  56.2 12.7 %all_to_all.16.in_ref = bf16[8,72,128]{2,1,0:T(8,128)(2,1)S(1)} all-to-all(bf16[8,72,128]{2,1,0:T(8,128)(2,1)S(1)} %shard_map.110), channel_id=1, replica_groups={{0,1,2,3,4,5,6,7},{8,9,10,11,12,13,14,15},{16,17,18,19,20,21,22,23},{24..., dimensions={0} | all-to-all | bytes 294912 | tf_op jit(solution)/shard_map/all_to_all | solution.py:506
  68.9 0.9 shard_map.111
  69.8 6.9 %all-to-all-start.2 = ((bf16[32,72,128]{2,1,0:T(8,128)(2,1)}), bf16[32,72,128]{2,1,0:T(8,128)(2,1)S(1)}, u32[]{:S(2)}, u32[]{:S(2)}) async-start(bf16[32,72,128]{2,1,0:T(8,128)(2,1)} %shard_map.111), calls=%async_computation.2 | async-start | bytes 1179648 | tf_op jit(solution)/shard_map/all_to_all | solution.py:508
  76.7 0.0 copy-done.5
  76.7 4.4 %shard_map.108 = (bf16[8,64,256]{2,1,0:T(8,128)(2,1)S(1)}, bf16[2,8,64,256]{3,2,1,0:T(8,128)(2,1)S(1)}, bf16[8,64,256]{2,1,0:T(8,128)(2,1)S(1)}) custom-call(bf16[2,16,64,256]{3,2,1,0:T(8,128)(2,1)S(1)} %get-tuple-element.48.delta_ref, bf16[9,96,64]{2,1,0:T(8,128)(2,1)S(1)} %bitcast.21), custom_call_target="tpu_custom_call" | custom-call | flops 1207959552 | bytes 8388608 | tf_op jit(solution)/shard_map/pallas_call | solution.py:355
  81.1 0.4 collective-permute-start.6
  81.4 3.3 %collective-permute-start.7 = (bf16[8,64,256]{2,1,0:T(8,128)(2,1)S(1)}, bf16[8,64,256]{2,1,0:T(8,128)(2,1)S(1)}, u32[]{:S(2)}, u32[]{:S(2)}) collective-permute-start(bf16[8,64,256]{2,1,0:T(8,128)(2,1)S(1)} %get-tuple-element.51), channel_id=1, source_target_pairs={{1,0},{2,1},{3,2},{4,3},{5,4},{6,5},{7,6},{8,7},{9,8},{10,9},{11,1... | collective-permute-start | bytes 786440 | tf_op jit(solution)/shard_map/ppermute | solution.py:486
  84.7 6.2 %collective-permute-done.6.fl_ref = bf16[8,64,256]{2,1,0:T(8,128)(2,1)S(1)} collective-permute-done((bf16[8,64,256]{2,1,0:T(8,128)(2,1)S(1)}, bf16[8,64,256]{2,1,0:T(8,128)(2,1)S(1)}, u32[]{:S(2)}, u32[]{:S(2)}) %collective-permute-start.6) | collective-permute-done | bytes 262176 | tf_op jit(solution)/shard_map/ppermute | solution.py:487
  90.9 0.0 collective-permute-done.7.fr_ref
  90.9 1.0 %shard_map.109 = bf16[2,64,2048]{2,1,0:T(8,128)(2,1)} custom-call(f32[2,8,128]{2,1,0:T(8,128)S(1)} %broadcast_in_dim.2.keep_ref, bf16[2,8,64,256]{3,2,1,0:T(8,128)(2,1)S(1)} %get-tuple-element.49.own_ref, bf16[8,64,256]{2,1,0:T(8,128)(2,1)S(1)} %collective-permute-done.6.fl_ref, bf16[8,64,256]{2,1,0:T(8,128)(2,1)S(1)} %collective-permute-done.7.fr_ref), custom_call_target="tpu_custom_call" | custom-call | flops 134217728 | bytes 4194304 | tf_op jit(solution)/shard_map/pallas_call | solution.py:355
  91.8 0.0 all-to-all-done.2.in_ref
  91.8 1.1 %shard_map.112 = (f32[1728,128]{1,0:T(8,128)}, f32[1,128]{1,0:T(1,128)}, f32[864,64]{1,0:T(8,128)}, f32[1,64]{1,0:T(1,128)}) custom-call(bf16[32,72,128]{2,1,0:T(8,128)(2,1)S(1)} %all-to-all-done.2.in_ref), custom_call_target="tpu_custom_call" | custom-call | bytes 1048576 | tf_op jit(solution)/shard_map/pallas_call | solution.py:355
Async XLA Ops:
  1.7 13.4 %collective-permute-start = (bf16[64,2048]{1,0:T(8,128)(2,1)S(1)}, bf16[64,2048]{1,0:T(8,128)(2,1)S(1)}, u32[]{:S(2)}, u32[]{:S(2)}) collective-permute-start(bf16[64,2048]{1,0:T(8,128)(2,1)S(1)} %get-tuple-element.58.x1_ref), channel_id=1, source_target_pairs={{0,1},{1,2},{2,3},{3,4},{4,5},{5,6},{6,7},{7,8},{8,9},{9,10},{10,1... | collective-permute-start | bytes 786440 | tf_op jit(solution)/shard_map/ppermute | solution.py:381
  4.2 10.9 %collective-permute-start.1 = (bf16[64,2048]{1,0:T(8,128)(2,1)S(1)}, bf16[64,2048]{1,0:T(8,128)(2,1)S(1)}, u32[]{:S(2)}, u32[]{:S(2)}) collective-permute-start(bf16[64,2048]{1,0:T(8,128)(2,1)S(1)} %get-tuple-element.57.x0_ref), channel_id=1, source_target_pairs={{1,0},{2,1},{3,2},{4,3},{5,4},{6,5},{7,6},{8,7},{9,8},{10,9},{11,1... | collective-permute-start | bytes 786440 | tf_op jit(solution)/shard_map/ppermute | solution.py:382
  9.3 0.9 %copy-start.4 = (bf16[3,3,3,32,64]{4,3,2,1,0:T(8,128)(2,1)S(1)}, bf16[3,3,3,32,64]{4,3,2,1,0:T(8,128)(2,1)}, u32[]{:S(2)}) copy-start(bf16[3,3,3,32,64]{4,3,2,1,0:T(8,128)(2,1)} %param.7) | copy-start | bytes 331780
  10.2 5.0 %copy-start.1 = (f32[64]{0:T(128)S(1)}, f32[64]{0:T(128)}, u32[]{:S(2)}) copy-start(f32[64]{0:T(128)} %param.8) | copy-start | bytes 772
  15.2 5.5 %copy-start.3 = (bf16[3,3,3,64,128]{4,3,2,1,0:T(8,128)(2,1)S(1)}, bf16[3,3,3,64,128]{4,3,2,1,0:T(8,128)(2,1)}, u32[]{:S(2)}) copy-start(bf16[3,3,3,64,128]{4,3,2,1,0:T(8,128)(2,1)} %param.9) | copy-start | bytes 1327108
  15.2 6.4 %copy-start.2 = (f32[128]{0:T(128)S(1)}, f32[128]{0:T(128)}, u32[]{:S(2)}) copy-start(f32[128]{0:T(128)} %param.10) | copy-start | bytes 1540
  17.0 6.0 %copy-start = (bf16[1,1,32,4096]{3,2,1,0:T(8,128)(2,1)S(1)}, bf16[1,1,32,4096]{3,2,1,0:T(8,128)(2,1)}, u32[]{:S(2)}) copy-start(bf16[1,1,32,4096]{3,2,1,0:T(8,128)(2,1)} %param.11) | copy-start | bytes 786436
  17.0 6.0 %collective-permute-start.2 = (bf16[16,32,128]{2,1,0:T(8,128)(2,1)S(1)}, bf16[16,32,128]{2,1,0:T(8,128)(2,1)S(1)}, u32[]{:S(2)}, u32[]{:S(2)}) collective-permute-start(bf16[16,32,128]{2,1,0:T(8,128)(2,1)S(1)} %get-tuple-element.33.own_ref), channel_id=1, source_target_pairs={{0,1},{1,2},{2,3},{3,4},{4,5},{5,6},{6,7},{7,8},{8,9},{9,10},{10,1... | collective-permute-start | bytes 393224 | tf_op jit(solution)/shard_map/ppermute | solution.py:414
  17.1 5.9 %collective-permute-start.3 = (bf16[16,32,128]{2,1,0:T(8,128)(2,1)S(1)}, bf16[16,32,128]{2,1,0:T(8,128)(2,1)S(1)}, u32[]{:S(2)}, u32[]{:S(2)}) collective-permute-start(bf16[16,32,128]{2,1,0:T(8,128)(2,1)S(1)} %get-tuple-element.33.own_ref), channel_id=1, source_target_pairs={{1,0},{2,1},{3,2},{4,3},{5,4},{6,5},{7,6},{8,7},{9,8},{10,9},{11,1... | collective-permute-start | bytes 393224 | tf_op jit(solution)/shard_map/ppermute | solution.py:415
  25.4 6.0 %collective-permute-start.4 = (bf16[16,32,128]{2,1,0:T(8,128)(2,1)S(1)}, bf16[16,32,128]{2,1,0:T(8,128)(2,1)S(1)}, u32[]{:S(2)}, u32[]{:S(2)}) collective-permute-start(bf16[16,32,128]{2,1,0:T(8,128)(2,1)S(1)} %get-tuple-element.42), channel_id=1, source_target_pairs={{0,1},{1,2},{2,3},{3,4},{4,5},{5,6},{6,7},{7,8},{8,9},{9,10},{10,1... | collective-permute-start | bytes 393224 | tf_op jit(solution)/shard_map/ppermute | solution.py:441
  25.5 5.9 %collective-permute-start.5 = (bf16[16,32,128]{2,1,0:T(8,128)(2,1)S(1)}, bf16[16,32,128]{2,1,0:T(8,128)(2,1)S(1)}, u32[]{:S(2)}, u32[]{:S(2)}) collective-permute-start(bf16[16,32,128]{2,1,0:T(8,128)(2,1)S(1)} %get-tuple-element.43), channel_id=1, source_target_pairs={{1,0},{2,1},{3,2},{4,3},{5,4},{6,5},{7,6},{8,7},{9,8},{10,9},{11,1... | collective-permute-start | bytes 393224 | tf_op jit(solution)/shard_map/ppermute | solution.py:440
  56.1 20.6 %copy-start.5 = (bf16[3,3,3,32,64]{4,3,2,1,0:T(8,128)(2,1)S(1)}, bf16[3,3,3,32,64]{4,3,2,1,0:T(8,128)(2,1)}, u32[]{:S(2)}) copy-start(bf16[3,3,3,32,64]{4,3,2,1,0:T(8,128)(2,1)} %param.7) | copy-start | bytes 331780
  69.8 22.1 %all-to-all-start.2 = ((bf16[32,72,128]{2,1,0:T(8,128)(2,1)}), bf16[32,72,128]{2,1,0:T(8,128)(2,1)S(1)}, u32[]{:S(2)}, u32[]{:S(2)}) async-start(bf16[32,72,128]{2,1,0:T(8,128)(2,1)} %shard_map.111), calls=%async_computation.2 | async-start | bytes 1179648 | tf_op jit(solution)/shard_map/all_to_all | solution.py:508
  81.1 9.8 %collective-permute-start.6 = (bf16[8,64,256]{2,1,0:T(8,128)(2,1)S(1)}, bf16[8,64,256]{2,1,0:T(8,128)(2,1)S(1)}, u32[]{:S(2)}, u32[]{:S(2)}) collective-permute-start(bf16[8,64,256]{2,1,0:T(8,128)(2,1)S(1)} %get-tuple-element.50), channel_id=1, source_target_pairs={{0,1},{1,2},{2,3},{3,4},{4,5},{5,6},{6,7},{7,8},{8,9},{9,10},{10,1... | collective-permute-start | bytes 786440 | tf_op jit(solution)/shard_map/ppermute | solution.py:487
  81.4 9.5 %collective-permute-start.7 = (bf16[8,64,256]{2,1,0:T(8,128)(2,1)S(1)}, bf16[8,64,256]{2,1,0:T(8,128)(2,1)S(1)}, u32[]{:S(2)}, u32[]{:S(2)}) collective-permute-start(bf16[8,64,256]{2,1,0:T(8,128)(2,1)S(1)} %get-tuple-element.51), channel_id=1, source_target_pairs={{1,0},{2,1},{3,2},{4,3},{5,4},{6,5},{7,6},{8,7},{9,8},{10,9},{11,1... | collective-permute-start | bytes 786440 | tf_op jit(solution)/shard_map/ppermute | solution.py:486

commit v6 on v5

--- a/solution.py
+++ b/solution.py
@@ -116,7 +116,7 @@
             buf,
             xs_ref.at[s],
         )
-    step = 4
+    step = 8
     lane = lax.broadcasted_iota(jnp.int32, (step * half, LANES), 1)
 
     for g in range(0, groups, step):
@@ -283,7 +283,7 @@
                 ds[p, 0, t] = spot[9 : 9 + rows, :].astype(BF16)
                 ds[p, 1, t] = low
                 ds[p, 2, t] = spot[7 : 7 + rows, :].astype(BF16)
-    step = 4
+    step = 8
     for g in range(0, groups // 2, step):
         spot = pl.ds(g, step)
         near = _window(ds.at[0], g, step)
@@ -405,7 +405,7 @@
     slope, pooled, xs_halo = _call(
         _second_kernel,
         (_shape((2, groups, side, 256), F32), tile, _shape(xs_shape, BF16)),
-        [tall] + [pltpu.VMEM((groups // 4, 4 * side, LANES), F32)] * 2,
+        [tall] + [pltpu.VMEM((groups // 8, 8 * side, LANES), F32)] * 2,
         2 * work * 768,
         8 * MIB,
         16,

time: 93.3 us -> 93.5 us (level)
  no operation moved by 1% of the time
where the time goes in v6:
time: 93.5 us; the launch traced here: 93.2 us
  blocking collectives  33.8 us (36%)
  starting transfers between devices  25.6 us (27%)
  Pallas kernels  20.2 us (22%)
  waiting for transfers between devices  10.7 us (11%)
  local copies, waits for them, and re-layouts  2.09 us (2%)
    all_to_all x1, blocking collectives, local(): met = lax.all_to_all(parts, ('dp', 'space'), 0, 0, axis_index_groups=planes)  21.1 us
    pallas_call x12, Pallas kernels, _call(): pl.pallas_call(kernel, out_shape=out, scratch_shapes=scratch, compiler_pa...  20.2 us
    all_to_all x1, blocking collectives, local(): met = lax.all_to_all(mine, 'space', 0, 0, axis_index_groups=lines)  12.7 us
    all_to_all x1, starting transfers between devices, local(): lax.all_to_all(joined, ('dp', 'space'), 0, 0, axis_index_groups=planes)  6.91 us
    ppermute x1, waiting for transfers between devices, local(): gx_from_left = lax.ppermute(gx_right, 'space', up)  6.16 us
    ppermute x1, starting transfers between devices, local(): from_right = lax.ppermute(x0, 'space', down)  4.96 us
    ppermute x1, starting transfers between devices, local(): gp_from_right = lax.ppermute(gp_left, 'space', down)  3.83 us
    ppermute x1, starting transfers between devices, local(): pool_right = lax.ppermute(pooled, 'space', down)  3.56 us
  transfers between devices with their start and end apart: 9, of which 4 were waited for; matrix products, arithmetic and copies ran while one was open for 0% of the time, Pallas kernels for 11%

profile of v6, /device:TPU:1, one launch (start us, length us, event | category | flops | bytes accessed | tf_op | source)
XLA Modules:
  0.0 93.2 jit_solution(9950151266740454662)
XLA Ops:
  0.6 1.1 %slice_bitcast_fusion = (bf16[64,2048]{1,0:T(8,128)(2,1)S(1)}, bf16[64,2048]{1,0:T(8,128)(2,1)S(1)}) fusion(bf16[1,2,64,2048]{3,2,1,0:T(8,128)(2,1)} %param.6), kind=kLoop, calls=%fused_computation | loop fusion | bytes 1048576 | tf_op jit(solution)/shard_map/squeeze | solution.py:380
  1.7 2.5 %collective-permute-start = (bf16[64,2048]{1,0:T(8,128)(2,1)S(1)}, bf16[64,2048]{1,0:T(8,128)(2,1)S(1)}, u32[]{:S(2)}, u32[]{:S(2)}) collective-permute-start(bf16[64,2048]{1,0:T(8,128)(2,1)S(1)} %get-tuple-element.58.x1_ref), channel_id=1, source_target_pairs={{0,1},{1,2},{2,3},{3,4},{4,5},{5,6},{6,7},{7,8},{8,9},{9,10},{10,1... | collective-permute-start | bytes 786440 | tf_op jit(solution)/shard_map/ppermute | solution.py:381
  4.2 5.0 %collective-permute-start.1 = (bf16[64,2048]{1,0:T(8,128)(2,1)S(1)}, bf16[64,2048]{1,0:T(8,128)(2,1)S(1)}, u32[]{:S(2)}, u32[]{:S(2)}) collective-permute-start(bf16[64,2048]{1,0:T(8,128)(2,1)S(1)} %get-tuple-element.57.x0_ref), channel_id=1, source_target_pairs={{1,0},{2,1},{3,2},{4,3},{5,4},{6,5},{7,6},{8,7},{9,8},{10,9},{11,1... | collective-permute-start | bytes 786440 | tf_op jit(solution)/shard_map/ppermute | solution.py:382
  9.2 0.1 add_convert_fusion
  9.3 0.0 copy-start.4
  9.3 0.9 %copy-done.4 = bf16[3,3,3,32,64]{4,3,2,1,0:T(8,128)(2,1)S(1)} copy-done((bf16[3,3,3,32,64]{4,3,2,1,0:T(8,128)(2,1)S(1)}, bf16[3,3,3,32,64]{4,3,2,1,0:T(8,128)(2,1)}, u32[]{:S(2)}) %copy-start.4) | copy-done | bytes 110616
  10.2 0.0 copy-start.1
  10.2 2.0 %shard_map.101 = (f32[2,16,64,256]{3,2,1,0:T(8,128)S(1)}, bf16[2,3,17,64,128]{4,3,2,1,0:T(8,128)(2,1)S(1)}, bf16[2304,256]{1,0:T(8,128)(2,1)S(1)}) custom-call(bf16[64,2048]{1,0:T(8,128)(2,1)S(1)} %get-tuple-element.57.x0_ref, bf16[64,2048]{1,0:T(8,128)(2,1)S(1)} %get-tuple-element.58.x1_ref, bf16[9,96,64]{2,1,0:T(8,128)(2,1)S(1)} %bitcast.20), custom_call_target="tpu_custom_call" | custom-call | flops 1610612736 | bytes 8388608 | tf_op jit(solution)/shard_map/pallas_call | solution.py:355
  12.2 2.9 %collective-permute-done.left_ref = bf16[64,2048]{1,0:T(8,128)(2,1)S(1)} collective-permute-done((bf16[64,2048]{1,0:T(8,128)(2,1)S(1)}, bf16[64,2048]{1,0:T(8,128)(2,1)S(1)}, u32[]{:S(2)}, u32[]{:S(2)}) %collective-permute-start) | collective-permute-done | bytes 262176 | tf_op jit(solution)/shard_map/ppermute | solution.py:381
  15.1 0.0 collective-permute-done.1.right_ref
  15.1 0.1 broadcast_in_dim.2.keep_ref
  15.2 0.0 copy-done.1
  15.2 0.0 copy-start.3
  15.2 0.0 copy-start.2
  15.2 1.9 %shard_map.102 = (f32[2,16,64,256]{3,2,1,0:T(8,128)S(1)}, bf16[16,32,128]{2,1,0:T(8,128)(2,1)S(1)}, bf16[2,3,17,64,128]{4,3,2,1,0:T(8,128)(2,1)S(1)}) custom-call(f32[2,8,128]{2,1,0:T(8,128)S(1)} %broadcast_in_dim.2.keep_ref, bf16[64,2048]{1,0:T(8,128)(2,1)S(1)} %collective-permute-done.left_ref, bf16[64,2048]{1,0:T(8,128)(2,1)S(1)} %collective-permute-done.1.right_ref, ...), custom_call_target="tpu_custom_call" | custom-call | flops 805306368 | bytes 8388608 | tf_op jit(solution)/shard_map/pallas_call | solution.py:355
  17.1 0.0 copy-start
  17.1 0.1 collective-permute-start.2
  17.2 3.6 %collective-permute-start.3 = (bf16[16,32,128]{2,1,0:T(8,128)(2,1)S(1)}, bf16[16,32,128]{2,1,0:T(8,128)(2,1)S(1)}, u32[]{:S(2)}, u32[]{:S(2)}) collective-permute-start(bf16[16,32,128]{2,1,0:T(8,128)(2,1)S(1)} %get-tuple-element.33.own_ref), channel_id=1, source_target_pairs={{1,0},{2,1},{3,2},{4,3},{5,4},{6,5},{7,6},{8,7},{9,8},{10,9},{11,1... | collective-permute-start | bytes 393224 | tf_op jit(solution)/shard_map/ppermute | solution.py:415
  20.8 0.0 copy-done.3
  20.8 0.9 shard_map.103
  21.7 0.0 copy-done.2
  21.7 0.4 shard_map.104
  22.1 1.0 %collective-permute-done.2.left_ref = bf16[16,32,128]{2,1,0:T(8,128)(2,1)S(1)} collective-permute-done((bf16[16,32,128]{2,1,0:T(8,128)(2,1)S(1)}, bf16[16,32,128]{2,1,0:T(8,128)(2,1)S(1)}, u32[]{:S(2)}, u32[]{:S(2)}) %collective-permute-start.2) | collective-permute-done | bytes 131104 | tf_op jit(solution)/shard_map/ppermute | solution.py:414
  23.1 0.0 collective-permute-done.3.right_ref
  23.1 0.0 copy-done
  23.1 2.3 %shard_map.105 = (bf16[512,256]{1,0:T(8,128)(2,1)S(1)}, bf16[2,3,17,32,128]{4,3,2,1,0:T(8,128)(2,1)S(1)}, bf16[3,34,32,128]{3,2,1,0:T(8,128)(2,1)S(1)}, bf16[16,...) custom-call(f32[2,8,128]{2,1,0:T(8,128)S(1)} %broadcast_in_dim.2.keep_ref, ...), custom_call_target="tpu_custom_call" | custom-call | flops 805306368 | bytes 4194304 | tf_op jit(solution)/shard_map/pallas_call | solution.py:355
  25.5 0.1 collective-permute-start.4
  25.6 3.8 %collective-permute-start.5 = (bf16[16,32,128]{2,1,0:T(8,128)(2,1)S(1)}, bf16[16,32,128]{2,1,0:T(8,128)(2,1)S(1)}, u32[]{:S(2)}, u32[]{:S(2)}) collective-permute-start(bf16[16,32,128]{2,1,0:T(8,128)(2,1)S(1)} %get-tuple-element.43), channel_id=1, source_target_pairs={{1,0},{2,1},{3,2},{4,3},{5,4},{6,5},{7,6},{8,7},{9,8},{10,9},{11,1... | collective-permute-start | bytes 393224 | tf_op jit(solution)/shard_map/ppermute | solution.py:440
  29.4 1.4 %shard_map.106 = (f32[16,32,128]{2,1,0:T(8,128)S(1)}, bf16[1792,128]{1,0:T(8,128)(2,1)S(1)}) custom-call(bf16[512,256]{1,0:T(8,128)(2,1)S(1)} %get-tuple-element.37.delta_ref, bf16[3,17,32,128]{3,2,1,0:T(8,128)(2,1)S(1)} %get-tuple-element.38.own_ref, bf16[2,3,17,32,128]{4,3,2,1,0:T(8,128)(2,1)S(1)} %get-tuple-element.39.halo_ref, ...), custom_call_target="tpu_custom_call" | custom-call | flops 805306368 | bytes 2097152 | tf_op jit(solution)/shard_map/pallas_call | solution.py:355
  30.8 0.7 collective-permute-done.4.fl_ref
  31.5 0.0 collective-permute-done.5.fr_ref
  31.5 3.6 %shard_map.107 = (bf16[2,16,64,256]{3,2,1,0:T(8,128)(2,1)S(1)}, bf16[32,72,128]{2,1,0:T(8,128)(2,1)S(1)}) custom-call(f32[2,8,128]{2,1,0:T(8,128)S(1)} %broadcast_in_dim.2.keep_ref, f32[16,32,128]{2,1,0:T(8,128)S(1)} %get-tuple-element.41.gm_ref, bf16[16,32,128]{2,1,0:T(8,128)(2,1)S(1)} %collective-permute-done.4.fl_ref, ...), custom_call_target="tpu_custom_call" | custom-call | flops 2415919104 | bytes 4194304 | tf_op jit(solution)/shard_map/pallas_call | solution.py:355
  35.1 21.1 %all_to_all.15.in_ref = bf16[32,72,128]{2,1,0:T(8,128)(2,1)S(1)} all-to-all(bf16[32,72,128]{2,1,0:T(8,128)(2,1)S(1)} %get-tuple-element.52), channel_id=1, replica_groups={{0,8,16,24,32,40,48,56,64,72,80,88,96,104,112,120,128,136,144,152,160,1..., dimensions={0} | all-to-all | bytes 1179648 | tf_op jit(solution)/shard_map/all_to_all | solution.py:471
  56.2 0.0 copy-start.5
  56.2 0.1 shard_map.110
  56.3 12.7 %all_to_all.16.in_ref = bf16[8,72,128]{2,1,0:T(8,128)(2,1)S(1)} all-to-all(bf16[8,72,128]{2,1,0:T(8,128)(2,1)S(1)} %shard_map.110), channel_id=1, replica_groups={{0,1,2,3,4,5,6,7},{8,9,10,11,12,13,14,15},{16,17,18,19,20,21,22,23},{24..., dimensions={0} | all-to-all | bytes 294912 | tf_op jit(solution)/shard_map/all_to_all | solution.py:506
  69.0 0.9 shard_map.111
  69.9 6.9 %all-to-all-start.2 = ((bf16[32,72,128]{2,1,0:T(8,128)(2,1)}), bf16[32,72,128]{2,1,0:T(8,128)(2,1)S(1)}, u32[]{:S(2)}, u32[]{:S(2)}) async-start(bf16[32,72,128]{2,1,0:T(8,128)(2,1)} %shard_map.111), calls=%async_computation.2 | async-start | bytes 1179648 | tf_op jit(solution)/shard_map/all_to_all | solution.py:508
  76.8 0.0 copy-done.5
  76.8 4.5 %shard_map.108 = (bf16[8,64,256]{2,1,0:T(8,128)(2,1)S(1)}, bf16[2,8,64,256]{3,2,1,0:T(8,128)(2,1)S(1)}, bf16[8,64,256]{2,1,0:T(8,128)(2,1)S(1)}) custom-call(bf16[2,16,64,256]{3,2,1,0:T(8,128)(2,1)S(1)} %get-tuple-element.48.delta_ref, bf16[9,96,64]{2,1,0:T(8,128)(2,1)S(1)} %bitcast.21), custom_call_target="tpu_custom_call" | custom-call | flops 1207959552 | bytes 8388608 | tf_op jit(solution)/shard_map/pallas_call | solution.py:355
  81.3 0.4 collective-permute-start.6
  81.7 3.3 %collective-permute-start.7 = (bf16[8,64,256]{2,1,0:T(8,128)(2,1)S(1)}, bf16[8,64,256]{2,1,0:T(8,128)(2,1)S(1)}, u32[]{:S(2)}, u32[]{:S(2)}) collective-permute-start(bf16[8,64,256]{2,1,0:T(8,128)(2,1)S(1)} %get-tuple-element.51), channel_id=1, source_target_pairs={{1,0},{2,1},{3,2},{4,3},{5,4},{6,5},{7,6},{8,7},{9,8},{10,9},{11,1... | collective-permute-start | bytes 786440 | tf_op jit(solution)/shard_map/ppermute | solution.py:486
  85.0 6.2 %collective-permute-done.6.fl_ref = bf16[8,64,256]{2,1,0:T(8,128)(2,1)S(1)} collective-permute-done((bf16[8,64,256]{2,1,0:T(8,128)(2,1)S(1)}, bf16[8,64,256]{2,1,0:T(8,128)(2,1)S(1)}, u32[]{:S(2)}, u32[]{:S(2)}) %collective-permute-start.6) | collective-permute-done | bytes 262176 | tf_op jit(solution)/shard_map/ppermute | solution.py:487
  91.2 0.0 collective-permute-done.7.fr_ref
  91.2 1.0 %shard_map.109 = bf16[2,64,2048]{2,1,0:T(8,128)(2,1)} custom-call(f32[2,8,128]{2,1,0:T(8,128)S(1)} %broadcast_in_dim.2.keep_ref, bf16[2,8,64,256]{3,2,1,0:T(8,128)(2,1)S(1)} %get-tuple-element.49.own_ref, bf16[8,64,256]{2,1,0:T(8,128)(2,1)S(1)} %collective-permute-done.6.fl_ref, bf16[8,64,256]{2,1,0:T(8,128)(2,1)S(1)} %collective-permute-done.7.fr_ref), custom_call_target="tpu_custom_call" | custom-call | flops 134217728 | bytes 4194304 | tf_op jit(solution)/shard_map/pallas_call | solution.py:355
  92.1 0.0 all-to-all-done.2.in_ref
  92.1 1.1 %shard_map.112 = (f32[1728,128]{1,0:T(8,128)}, f32[1,128]{1,0:T(1,128)}, f32[864,64]{1,0:T(8,128)}, f32[1,64]{1,0:T(1,128)}) custom-call(bf16[32,72,128]{2,1,0:T(8,128)(2,1)S(1)} %all-to-all-done.2.in_ref), custom_call_target="tpu_custom_call" | custom-call | bytes 1048576 | tf_op jit(solution)/shard_map/pallas_call | solution.py:355
Async XLA Ops:
  1.7 13.4 %collective-permute-start = (bf16[64,2048]{1,0:T(8,128)(2,1)S(1)}, bf16[64,2048]{1,0:T(8,128)(2,1)S(1)}, u32[]{:S(2)}, u32[]{:S(2)}) collective-permute-start(bf16[64,2048]{1,0:T(8,128)(2,1)S(1)} %get-tuple-element.58.x1_ref), channel_id=1, source_target_pairs={{0,1},{1,2},{2,3},{3,4},{4,5},{5,6},{6,7},{7,8},{8,9},{9,10},{10,1... | collective-permute-start | bytes 786440 | tf_op jit(solution)/shard_map/ppermute | solution.py:381
  4.2 10.9 %collective-permute-start.1 = (bf16[64,2048]{1,0:T(8,128)(2,1)S(1)}, bf16[64,2048]{1,0:T(8,128)(2,1)S(1)}, u32[]{:S(2)}, u32[]{:S(2)}) collective-permute-start(bf16[64,2048]{1,0:T(8,128)(2,1)S(1)} %get-tuple-element.57.x0_ref), channel_id=1, source_target_pairs={{1,0},{2,1},{3,2},{4,3},{5,4},{6,5},{7,6},{8,7},{9,8},{10,9},{11,1... | collective-permute-start | bytes 786440 | tf_op jit(solution)/shard_map/ppermute | solution.py:382
  9.3 0.9 %copy-start.4 = (bf16[3,3,3,32,64]{4,3,2,1,0:T(8,128)(2,1)S(1)}, bf16[3,3,3,32,64]{4,3,2,1,0:T(8,128)(2,1)}, u32[]{:S(2)}) copy-start(bf16[3,3,3,32,64]{4,3,2,1,0:T(8,128)(2,1)} %param.7) | copy-start | bytes 331780
  10.2 5.0 %copy-start.1 = (f32[64]{0:T(128)S(1)}, f32[64]{0:T(128)}, u32[]{:S(2)}) copy-start(f32[64]{0:T(128)} %param.8) | copy-start | bytes 772
  15.2 5.6 %copy-start.3 = (bf16[3,3,3,64,128]{4,3,2,1,0:T(8,128)(2,1)S(1)}, bf16[3,3,3,64,128]{4,3,2,1,0:T(8,128)(2,1)}, u32[]{:S(2)}) copy-start(bf16[3,3,3,64,128]{4,3,2,1,0:T(8,128)(2,1)} %param.9) | copy-start | bytes 1327108
  15.2 6.5 %copy-start.2 = (f32[128]{0:T(128)S(1)}, f32[128]{0:T(128)}, u32[]{:S(2)}) copy-start(f32[128]{0:T(128)} %param.10) | copy-start | bytes 1540
  17.1 6.0 %copy-start = (bf16[1,1,32,4096]{3,2,1,0:T(8,128)(2,1)S(1)}, bf16[1,1,32,4096]{3,2,1,0:T(8,128)(2,1)}, u32[]{:S(2)}) copy-start(bf16[1,1,32,4096]{3,2,1,0:T(8,128)(2,1)} %param.11) | copy-start | bytes 786436
  17.1 6.0 %collective-permute-start.2 = (bf16[16,32,128]{2,1,0:T(8,128)(2,1)S(1)}, bf16[16,32,128]{2,1,0:T(8,128)(2,1)S(1)}, u32[]{:S(2)}, u32[]{:S(2)}) collective-permute-start(bf16[16,32,128]{2,1,0:T(8,128)(2,1)S(1)} %get-tuple-element.33.own_ref), channel_id=1, source_target_pairs={{0,1},{1,2},{2,3},{3,4},{4,5},{5,6},{6,7},{7,8},{8,9},{9,10},{10,1... | collective-permute-start | bytes 393224 | tf_op jit(solution)/shard_map/ppermute | solution.py:414
  17.2 5.9 %collective-permute-start.3 = (bf16[16,32,128]{2,1,0:T(8,128)(2,1)S(1)}, bf16[16,32,128]{2,1,0:T(8,128)(2,1)S(1)}, u32[]{:S(2)}, u32[]{:S(2)}) collective-permute-start(bf16[16,32,128]{2,1,0:T(8,128)(2,1)S(1)} %get-tuple-element.33.own_ref), channel_id=1, source_target_pairs={{1,0},{2,1},{3,2},{4,3},{5,4},{6,5},{7,6},{8,7},{9,8},{10,9},{11,1... | collective-permute-start | bytes 393224 | tf_op jit(solution)/shard_map/ppermute | solution.py:415
  25.5 6.0 %collective-permute-start.4 = (bf16[16,32,128]{2,1,0:T(8,128)(2,1)S(1)}, bf16[16,32,128]{2,1,0:T(8,128)(2,1)S(1)}, u32[]{:S(2)}, u32[]{:S(2)}) collective-permute-start(bf16[16,32,128]{2,1,0:T(8,128)(2,1)S(1)} %get-tuple-element.42), channel_id=1, source_target_pairs={{0,1},{1,2},{2,3},{3,4},{4,5},{5,6},{6,7},{7,8},{8,9},{9,10},{10,1... | collective-permute-start | bytes 393224 | tf_op jit(solution)/shard_map/ppermute | solution.py:441
  25.6 5.9 %collective-permute-start.5 = (bf16[16,32,128]{2,1,0:T(8,128)(2,1)S(1)}, bf16[16,32,128]{2,1,0:T(8,128)(2,1)S(1)}, u32[]{:S(2)}, u32[]{:S(2)}) collective-permute-start(bf16[16,32,128]{2,1,0:T(8,128)(2,1)S(1)} %get-tuple-element.43), channel_id=1, source_target_pairs={{1,0},{2,1},{3,2},{4,3},{5,4},{6,5},{7,6},{8,7},{9,8},{10,9},{11,1... | collective-permute-start | bytes 393224 | tf_op jit(solution)/shard_map/ppermute | solution.py:440
  56.2 20.6 %copy-start.5 = (bf16[3,3,3,32,64]{4,3,2,1,0:T(8,128)(2,1)S(1)}, bf16[3,3,3,32,64]{4,3,2,1,0:T(8,128)(2,1)}, u32[]{:S(2)}) copy-start(bf16[3,3,3,32,64]{4,3,2,1,0:T(8,128)(2,1)} %param.7) | copy-start | bytes 331780
  69.9 22.2 %all-to-all-start.2 = ((bf16[32,72,128]{2,1,0:T(8,128)(2,1)}), bf16[32,72,128]{2,1,0:T(8,128)(2,1)S(1)}, u32[]{:S(2)}, u32[]{:S(2)}) async-start(bf16[32,72,128]{2,1,0:T(8,128)(2,1)} %shard_map.111), calls=%async_computation.2 | async-start | bytes 1179648 | tf_op jit(solution)/shard_map/all_to_all | solution.py:508
  81.3 9.8 %collective-permute-start.6 = (bf16[8,64,256]{2,1,0:T(8,128)(2,1)S(1)}, bf16[8,64,256]{2,1,0:T(8,128)(2,1)S(1)}, u32[]{:S(2)}, u32[]{:S(2)}) collective-permute-start(bf16[8,64,256]{2,1,0:T(8,128)(2,1)S(1)} %get-tuple-element.50), channel_id=1, source_target_pairs={{0,1},{1,2},{2,3},{3,4},{4,5},{5,6},{6,7},{7,8},{8,9},{9,10},{10,1... | collective-permute-start | bytes 786440 | tf_op jit(solution)/shard_map/ppermute | solution.py:487
  81.7 9.5 %collective-permute-start.7 = (bf16[8,64,256]{2,1,0:T(8,128)(2,1)S(1)}, bf16[8,64,256]{2,1,0:T(8,128)(2,1)S(1)}, u32[]{:S(2)}, u32[]{:S(2)}) collective-permute-start(bf16[8,64,256]{2,1,0:T(8,128)(2,1)S(1)} %get-tuple-element.51), channel_id=1, source_target_pairs={{1,0},{2,1},{3,2},{4,3},{5,4},{6,5},{7,6},{8,7},{9,8},{10,9},{11,1... | collective-permute-start | bytes 786440 | tf_op jit(solution)/shard_map/ppermute | solution.py:486
